TPU v7x, 32 devices: a whole 2x2x4 slice. The times are simulated.
32 devices in a mesh: grp: 2 (over core), seq: 4 (over z), fsdp: 4 (over y, x).
Axes of the slice: x: 2, y: 2, z: 4, core: 2. Of those that a mesh axis runs over, the one named last changes fastest.
Arguments:
- inputs: bfloat16 [8, 1024, 1280], P(('grp', 'fsdp'), 'seq'), may hold values from -6 to 6
- segments: int32 [8, 1024], P(('grp', 'fsdp')), may hold values from 0 to 8, as said below
- w_qkv: bfloat16 [1280, 3840], P('fsdp'), may hold values from -0.15625 to 0.15625
- w_out: bfloat16 [1280, 1280], P('fsdp'), may hold values from -0.15625 to 0.15625
- w_upgate: bfloat16 [1280, 10240], P('fsdp'), may hold values from -0.15625 to 0.15625
- w_down: bfloat16 [5120, 1280], P('fsdp'), may hold values from -0.078125 to 0.078125
- s_qk: float32 [1280], replicated, may hold values from 1 to 1.8
- alpha_attn: float32 [1280], replicated, may hold values from 0.15 to 0.6
- alpha_mlp: float32 [1280], replicated, may hold values from 0.15 to 0.6
- s_up: float32 [5120], replicated, may hold values from 0.5 to 2
- s_gate: float32 [5120], replicated, may hold values from 0.5 to 2
- cotangent: bfloat16 [8, 1024, 1280], P(('grp', 'fsdp'), 'seq'), may hold values from -6 to 6
Outputs:
- outputs: bfloat16 [8, 1024, 1280], P(('grp', 'fsdp'), 'seq')
- grad_inputs: float32 [8, 1024, 1280], P(('grp', 'fsdp'), 'seq')
- grad_w_qkv: float32 [1280, 3840], P('fsdp')
- grad_w_out: float32 [1280, 1280], P('fsdp')
- grad_w_upgate: float32 [1280, 10240], P('fsdp')
- grad_w_down: float32 [5120, 1280], P('fsdp')
- grad_s_qk: float32 [1280], P('fsdp')
- grad_alpha_attn: float32 [1280], P('fsdp')
- grad_alpha_mlp: float32 [1280], P('fsdp')
- grad_s_up: float32 [5120], P('fsdp')
- grad_s_gate: float32 [5120], P('fsdp')
Inputs may be any that keep to these rules, and one draw needn't show every extreme that they name: In every group the first 512 tokens have segment 0; the other tokens hold segments 1 to 8 in rising order, each a nonempty run.
All inputs are finite; a program needn't handle non-finite values.
Results may differ from a plain program's by a relative error of at most 0.022.
Values may be sent and summed in bfloat16 or wider, within the bound.
A program may use at most 256 MiB of HBM per device.

v0:
```python
import jax
import jax.numpy as jnp
from jax import lax
from jax.sharding import PartitionSpec as P

D = 1280
HEADS = 20
HEAD = 64


eps_norm = 1e-06
neg_big = -1e30


def unit_rows(value):
    return value * lax.rsqrt(jnp.mean(value * value, axis=-1, keepdims=True) + eps_norm)


def matmul_nt(former, latter):
    return lax.dot_general(
        former, latter, (((1,), (1,)), ((), ())), preferred_element_type=jnp.float32
    )


def matmul_tn(former, latter):
    return lax.dot_general(
        former, latter, (((0,), (0,)), ((), ())), preferred_element_type=jnp.float32
    )


def gathered_product(operand, w_shard):
    return jnp.dot(
        operand,
        lax.all_gather(w_shard, "fsdp", axis=0, tiled=True),
        preferred_element_type=jnp.float32,
    )


def gathered_transpose(gradient, w_shard):
    return matmul_nt(gradient, lax.all_gather(w_shard, "fsdp", axis=0, tiled=True))


def owner_sums(activation, gradient):
    return lax.psum_scatter(
        matmul_tn(activation, gradient).astype(jnp.bfloat16),
        "fsdp",
        scatter_dimension=0,
        tiled=True,
    ).astype(jnp.float32)


def norm_heads(query_raw, key_raw, gain_vector):
    gains = gain_vector.reshape(HEADS, HEAD)
    token_count = query_raw.shape[0]
    return (
        unit_rows(query_raw.reshape(token_count, HEADS, HEAD)) * gains,
        unit_rows(key_raw.reshape(token_count, HEADS, HEAD)) * gains,
    )


def post_update(base_rows, branch_rows, alpha_vector):
    return unit_rows(base_rows + alpha_vector * (unit_rows(branch_rows) - base_rows))


def activate(upgate_rows, up_scale, gate_scale):
    hidden_units = up_scale.shape[0]
    return (
        upgate_rows[:, :hidden_units]
        * up_scale
        * jax.nn.silu(upgate_rows[:, hidden_units:] * gate_scale)
    )


def body(
    inputs,
    segments,
    w_qkv,
    w_out,
    w_upgate,
    w_down,
    s_qk,
    alpha_attn,
    alpha_mlp,
    s_up,
    s_gate,
    cotangent,
):
    shards = (w_qkv, w_out, w_upgate, w_down)

    def forward_mul(operand, slot_index):
        return gathered_product(operand, shards[slot_index])

    def backward_mul(gradient, slot_index):
        return gathered_transpose(gradient, shards[slot_index])

    inputs_f = inputs[0].astype(jnp.float32)
    token_count = inputs_f.shape[0]
    seg_all = segments[0]
    seq_place = lax.axis_index("seq")
    seg_rows = lax.dynamic_slice_in_dim(seg_all, seq_place * token_count, token_count, 0)
    query_pos = seq_place * token_count + jnp.arange(token_count, dtype=jnp.int32)
    scaled = HEAD ** (-0.5)
    unit_in, pull_in = jax.vjp(unit_rows, inputs_f)
    unit_in_b = unit_in.astype(jnp.bfloat16)
    projected = forward_mul(unit_in_b, 0)
    (query_unit, key_unit), pull_heads = jax.vjp(
        norm_heads, projected[:, :D], projected[:, D : 2 * D], s_qk
    )
    query_b = query_unit.astype(jnp.bfloat16)
    kv_local = jnp.concatenate(
        [key_unit.reshape(token_count, D), projected[:, 2 * D :]], axis=1
    ).astype(jnp.bfloat16)
    kv_all = lax.all_gather(kv_local, "seq", axis=0, tiled=True)
    key_total = kv_all.shape[0]
    block_len = min(512, key_total)
    block_count = key_total // block_len
    kv_blocks = kv_all.reshape(block_count, block_len, 2, HEADS, HEAD)
    seg_blocks = seg_all.reshape(block_count, block_len)
    pos_blocks = jnp.arange(key_total, dtype=jnp.int32).reshape(block_count, block_len)
    blocks = (kv_blocks, seg_blocks, pos_blocks)

    def block_scores(kv_blk, seg_blk, pos_blk):
        scores = (
            jnp.einsum("qhe,khe->hqk", query_b, kv_blk[:, 0], preferred_element_type=jnp.float32)
            * scaled
        )
        allowed = (pos_blk[None, :] <= query_pos[:, None]) & (
            (seg_blk[None, :] == 0) | (seg_blk[None, :] == seg_rows[:, None])
        )
        return jnp.where(allowed[None], scores, neg_big)

    def max_step(carry, block):
        top_run, denom = carry
        scores = block_scores(block[0], block[1], block[2])
        new_top = jnp.maximum(top_run, jnp.max(scores, axis=-1))
        denom = denom * jnp.exp(top_run - new_top) + jnp.sum(
            jnp.exp(scores - new_top[..., None]), axis=-1
        )
        return ((new_top, denom), None)

    start_top = jnp.full((HEADS, token_count), neg_big, jnp.float32)
    start_sum = jnp.zeros((HEADS, token_count), jnp.float32)
    (top_all, denom_all), _ = lax.scan(max_step, (start_top, start_sum), blocks)
    log_total = top_all + jnp.log(denom_all)

    def out_step(accum, block):
        scores = block_scores(block[0], block[1], block[2])
        probs_b = jnp.exp(scores - log_total[..., None]).astype(jnp.bfloat16)
        return (
            accum
            + jnp.einsum(
                "hqk,khe->qhe", probs_b, block[0][:, 1], preferred_element_type=jnp.float32
            ),
            None,
        )

    attn_mix, _ = lax.scan(out_step, jnp.zeros((token_count, HEADS, HEAD), jnp.float32), blocks)
    mixture_b = attn_mix.reshape(token_count, D).astype(jnp.bfloat16)
    attention = forward_mul(mixture_b, 1)
    unit_mid, pull_attn = jax.vjp(post_update, unit_in, attention, alpha_attn)
    unit_mid_b = unit_mid.astype(jnp.bfloat16)
    upgate = forward_mul(unit_mid_b, 2)
    hidden, pull_act = jax.vjp(activate, upgate, s_up, s_gate)
    hidden_b = hidden.astype(jnp.bfloat16)
    feed_out = forward_mul(hidden_b, 3)
    result, pull_feed = jax.vjp(post_update, unit_mid, feed_out, alpha_mlp)
    grad_mid_res, grad_feed, grad_alpha_mlp = pull_feed(cotangent[0].astype(jnp.float32))
    grad_feed_b = grad_feed.astype(jnp.bfloat16)
    grad_hidden = backward_mul(grad_feed_b, 3)
    grad_upgate, grad_s_up, grad_s_gate = pull_act(grad_hidden)
    grad_upgate_b = grad_upgate.astype(jnp.bfloat16)
    grad_mid = grad_mid_res + backward_mul(grad_upgate_b, 2)
    grad_in_res, grad_attention, grad_alpha_attn = pull_attn(grad_mid)
    grad_attention_b = grad_attention.astype(jnp.bfloat16)
    grad_mixture = backward_mul(grad_attention_b, 1)
    grad_mix_b = grad_mixture.reshape(token_count, HEADS, HEAD).astype(jnp.bfloat16)
    delta = jnp.sum(grad_mix_b.astype(jnp.float32) * attn_mix, axis=-1).T

    def back_step(grad_query_run, block):
        kv_blk, seg_blk, pos_blk = block
        scores = block_scores(kv_blk, seg_blk, pos_blk)
        probs = jnp.exp(scores - log_total[..., None])
        grad_probs = jnp.einsum(
            "qhe,khe->hqk", grad_mix_b, kv_blk[:, 1], preferred_element_type=jnp.float32
        )
        grad_scores = (probs * (grad_probs - delta[..., None])).astype(jnp.bfloat16)
        grad_query_run = (
            grad_query_run
            + jnp.einsum(
                "hqk,khe->qhe", grad_scores, kv_blk[:, 0], preferred_element_type=jnp.float32
            )
            * scaled
        )
        grad_keys = (
            jnp.einsum("hqk,qhe->khe", grad_scores, query_b, preferred_element_type=jnp.float32)
            * scaled
        )
        grad_values = jnp.einsum(
            "hqk,qhe->khe",
            probs.astype(jnp.bfloat16),
            grad_mix_b,
            preferred_element_type=jnp.float32,
        )
        return (grad_query_run, jnp.stack([grad_keys, grad_values], axis=1))

    grad_query, grad_kv_blocks = lax.scan(
        back_step, jnp.zeros((token_count, HEADS, HEAD), jnp.float32), blocks
    )
    grad_kv_all = grad_kv_blocks.reshape(key_total, 2 * D)
    grad_kv_own = lax.psum_scatter(
        grad_kv_all.astype(jnp.bfloat16), "seq", scatter_dimension=0, tiled=True
    ).astype(jnp.float32)
    grad_query_raw, grad_key_raw, grad_s_qk = pull_heads(
        (grad_query, grad_kv_own[:, :D].reshape(token_count, HEADS, HEAD))
    )
    grad_proj_b = jnp.concatenate(
        [grad_query_raw, grad_key_raw, grad_kv_own[:, D:]], axis=1
    ).astype(jnp.bfloat16)
    grad_unit_in = grad_in_res + backward_mul(grad_proj_b, 0)
    (grad_inputs,) = pull_in(grad_unit_in)
    part_qkv = owner_sums(unit_in_b, grad_proj_b)
    part_out = owner_sums(mixture_b, grad_attention_b)
    part_upgate = owner_sums(unit_mid_b, grad_upgate_b)
    part_down = owner_sums(hidden_b, grad_feed_b)
    vec_qk, vec_attn, vec_mlp, vec_up, vec_gate = (
        lax.psum_scatter(
            grad_s_qk.astype(jnp.bfloat16), "fsdp", scatter_dimension=0, tiled=True
        ).astype(jnp.float32),
        lax.psum_scatter(
            grad_alpha_attn.astype(jnp.bfloat16), "fsdp", scatter_dimension=0, tiled=True
        ).astype(jnp.float32),
        lax.psum_scatter(
            grad_alpha_mlp.astype(jnp.bfloat16), "fsdp", scatter_dimension=0, tiled=True
        ).astype(jnp.float32),
        lax.psum_scatter(
            grad_s_up.astype(jnp.bfloat16), "fsdp", scatter_dimension=0, tiled=True
        ).astype(jnp.float32),
        lax.psum_scatter(
            grad_s_gate.astype(jnp.bfloat16), "fsdp", scatter_dimension=0, tiled=True
        ).astype(jnp.float32),
    )
    owned = (
        lax.psum(part_qkv.astype(jnp.bfloat16), ("grp", "seq")).astype(jnp.float32),
        lax.psum(part_out.astype(jnp.bfloat16), ("grp", "seq")).astype(jnp.float32),
        lax.psum(part_upgate.astype(jnp.bfloat16), ("grp", "seq")).astype(jnp.float32),
        lax.psum(part_down.astype(jnp.bfloat16), ("grp", "seq")).astype(jnp.float32),
        lax.psum(vec_qk.astype(jnp.bfloat16), ("grp", "seq")).astype(jnp.float32),
        lax.psum(vec_attn.astype(jnp.bfloat16), ("grp", "seq")).astype(jnp.float32),
        lax.psum(vec_mlp.astype(jnp.bfloat16), ("grp", "seq")).astype(jnp.float32),
        lax.psum(vec_up.astype(jnp.bfloat16), ("grp", "seq")).astype(jnp.float32),
        lax.psum(vec_gate.astype(jnp.bfloat16), ("grp", "seq")).astype(jnp.float32),
    )
    return (
        result.astype(jnp.bfloat16)[None],
        grad_inputs[None],
        owned[0],
        owned[1],
        owned[2],
        owned[3],
        owned[4],
        owned[5],
        owned[6],
        owned[7],
        owned[8],
    )


def solution(mesh):
    in_specs = (
        P(("grp", "fsdp"), "seq", None),
        P(("grp", "fsdp"), None),
        P("fsdp", None),
        P("fsdp", None),
        P("fsdp", None),
        P("fsdp", None),
        P(),
        P(),
        P(),
        P(),
        P(),
        P(("grp", "fsdp"), "seq", None),
    )
    out_specs = (
        P(("grp", "fsdp"), "seq", None),
        P(("grp", "fsdp"), "seq", None),
        P("fsdp", None),
        P("fsdp", None),
        P("fsdp", None),
        P("fsdp", None),
        P("fsdp"),
        P("fsdp"),
        P("fsdp"),
        P("fsdp"),
        P("fsdp"),
    )
    return jax.shard_map(body, mesh=mesh, in_specs=in_specs, out_specs=out_specs, check_vma=False)
```

profile of v0, /device:TPU:0, one launch (start us, length us, event | category | flops | bytes accessed | tf_op | source)
XLA Modules:
  0.0 1661.8 jit_solution(11509042960246559779)
XLA Ops:
  8.5 103.6 %all-gather.6.cloned.1.call-done = bf16[1280,3840]{1,0:T(8,128)(2,1)} async-done(((bf16[320,3840]{1,0:T(8,128)(2,1)}), bf16[1280,3840]{1,0:T(8,128)(2,1)}) %all-gather.6.cloned.1.call-update) | async-done | bytes 9830416 | tf_op jit(solution)/shard_map/all_gather | solution.py:34
  131.2 93.4 %all-gather.8.cloned.1.call-done = bf16[1024,2560]{1,0:T(8,128)(2,1)} async-done(((bf16[256,2560]{1,0:T(8,128)(2,1)}), bf16[1024,2560]{1,0:T(8,128)(2,1)}) %all-gather.8.cloned.1.call-update) | async-done | bytes 5242896 | tf_op jit(solution)/shard_map/all_gather | solution.py:113
  224.6 8.3 copy.65
  232.8 9.5 reshape.443
  248.4 29.0 %while.37 = (s32[]{:T(128)}, f32[20,256]{1,0:T(8,128)S(1)}, f32[20,256]{1,0:T(8,128)S(1)}, s32[2,512]{1,0:T(2,128)S(1)}, s32[2,512]{1,0:T(2,128)S(1)}, /*index=5...) while((s32[]{:T(128)}, f32[20,256]{1,0:T(8,128)S(1)}, ...), condition=%wide.region_6.7_spmd.clone, body=%wide.region_3.6_spmd.clone.sunk | while | flops 354445056 | bytes 28856452 | solution.py:143
  277.4 16.4 while.38
  299.1 208.6 %all-gather.12.cloned.1.call-done = bf16[1280,10240]{1,0:T(8,128)(2,1)} async-done(((bf16[320,10240]{1,0:T(8,128)(2,1)}), bf16[1280,10240]{1,0:T(8,128)(2,1)}) %all-gather.12.cloned.1.call-update) | async-done | bytes 26214416 | tf_op jit(solution)/shard_map/all_gather | solution.py:34
  507.7 15.9 fusion.73
  529.5 106.6 %all-gather.14.cloned.1.call-done = bf16[5120,1280]{1,0:T(8,128)(2,1)} async-done(((bf16[1280,1280]{1,0:T(8,128)(2,1)}), bf16[5120,1280]{1,0:T(8,128)(2,1)}) %all-gather.14.cloned.1.call-update) | async-done | bytes 13107216 | tf_op jit(solution)/shard_map/all_gather | solution.py:34
  636.1 8.3 multiply_reduce_fusion.13
  647.8 14.0 multiply_reduce_fusion
  667.4 17.2 %multiply_reduce_fusion.10 = (f32[256]{0:T(256)S(1)}, f32[256,1280]{1,0:T(8,128)}) fusion(f32[256,1280]{1,0:T(8,128)S(1)} %get-tuple-element.467, bf16[1280,10240]{1,0:T(8,128)(2,1)} %all-gather.12.cloned.1.call-done, f32[256,5120]{1,0:T(8,128)} %get-tuple-element.470, f32[256,5120]{1,0:T(8,128)} %broadcast_multiply_fusion, f32[1280]{0:T(1024)S(1)} %copy-done.39, ...), kind=kOutput, calls=%fused_computation.120 | convolution fusion | flops 6719733760 | bytes 41295872 | tf_op jit(solution)/shard_map/dot_general | solution.py:20
  694.0 45.6 %while.39 = (s32[]{:T(128)}, f32[256,20,64]{0,2,1:T(8,128)}, bf16[2,512,2,20,64]{1,4,3,2,0:T(8,128)(2,1)}, bf16[2,512,2,20,64]{1,4,3,2,0:T(8,128)(2,1)}, s32[2,5...) while((s32[]{:T(128)}, f32[256,20,64]{0,2,1:T(8,128)}, ...), condition=%wide.region_19.20_spmd.clone, body=%wide.region_18.19_spmd.clone.sunk | while | flops 1711997696 | bytes 90919608 | solution.py:206
  739.6 10.3 copy.71
  756.4 7.9 copy.72
  777.5 80.8 %reduce-scatter.6.cloned.1.call-done = bf16[256,2560]{1,0:T(8,128)(2,1)} async-done(((bf16[1024,2560]{1,0:T(8,128)(2,1)}), bf16[256,2560]{1,0:T(8,128)(2,1)}) %reduce-scatter.6.cloned.1.call-update) | async-done | bytes 1310736 | tf_op jit(solution)/shard_map/reduce_scatter | solution.py:210
  883.3 16.0 convolution_convert_fusion
  906.8 128.6 %reduce-scatter.14.cloned.1.call-done = bf16[1280,1280]{1,0:T(8,128)(2,1)} async-done(((bf16[5120,1280]{1,0:T(8,128)(2,1)}), bf16[1280,1280]{1,0:T(8,128)(2,1)}) %reduce-scatter.14.cloned.1.call-update) | async-done | bytes 3276816 | tf_op jit(solution)/shard_map/reduce_scatter | solution.py:44
  1035.5 101.3 %reduce-scatter.8.cloned.1.call-done = bf16[320,3840]{1,0:T(8,128)(2,1)} async-done(((bf16[1280,3840]{1,0:T(8,128)(2,1)}), bf16[320,3840]{1,0:T(8,128)(2,1)}) %reduce-scatter.8.cloned.1.call-update) | async-done | bytes 2457616 | tf_op jit(solution)/shard_map/reduce_scatter | solution.py:44
  1136.7 233.2 %reduce-scatter.12.cloned.1.call-done = bf16[320,10240]{1,0:T(8,128)(2,1)} async-done(((bf16[1280,10240]{1,0:T(8,128)(2,1)}), bf16[320,10240]{1,0:T(8,128)(2,1)}) %reduce-scatter.12.cloned.1.call-update) | async-done | bytes 6553616 | tf_op jit(solution)/shard_map/reduce_scatter | solution.py:44
  1372.6 15.4 all-reduce.9
  1388.5 29.8 %all-reduce.7 = (bf16[320]{0:T(512)(128)(2,1)S(1)}, bf16[320]{0:T(512)(128)(2,1)S(1)}, bf16[320]{0:T(512)(128)(2,1)S(1)}, bf16[1280]{0:T(1024)(128)(2,1)S(1)}, bf16[1280]{0:T(1024)(128)(2,1)S(1)}) all-reduce(bf16[320]{0:T(512)(128)(2,1)S(1)} %dynamic-slice.2, ...), channel_id=1, replica_groups=mesh['grp'=2,'seq'=4,'fsdp'=4] {'grp','seq'}, use_global_device_ids=true, to_apply=%region_35.36 | all-reduce | flops 3520 | bytes 14080 | tf_op jit(solution)/shard_map/psum | solution.py:247
  1429.6 208.8 %all-reduce.12.cloned.1.call-done = (bf16[320,3840]{1,0:T(8,128)(2,1)}, bf16[320,1280]{1,0:T(8,128)(2,1)}, bf16[320,10240]{1,0:T(8,128)(2,1)}, bf16[1280,1280]{1,0:T(8,128)(2,1)}) async-done(((bf16[320,3840]{1,0:T(8,128)(2,1)}, bf16[320,1280]{1,0:T(8,128)(2,1)}, bf16[320,10240]{1,0:T(8,128)(2,1)}, bf16[1280,1280]{1,0:T(8,128)(2,1)}), (bf16[320,3840]{1,0:T(8,128)(2,1)}, bf16[320,1280]{1,0:T(8,128)(2,1)}, ...) | async-done | bytes 13107216 | tf_op jit(solution)/shard_map/psum | solution.py:243
  1638.4 9.6 convert_element_type.165
  (270 shorter events, 218.3 us)
Async XLA Ops:
  7.2 104.9 %all-gather.6.cloned.1.call-start = ((), (), s32[]{:S(2)}) async-start(), calls=%async_computation.5 | async-start | bytes 12288000 | tf_op jit(solution)/shard_map/all_gather | solution.py:34
  7.9 216.6 %all-gather.8.cloned.1.call-start = ((), (), s32[]{:S(2)}) async-start(), calls=%async_computation.6 | async-start | bytes 6553600 | tf_op jit(solution)/shard_map/all_gather | solution.py:113
  8.5 110.2 %copy-start.49 = (f32[256]{0:T(256)}, f32[256]{0:T(256)S(1)}, u32[]{:S(2)}) copy-start(f32[256]{0:T(256)S(1)} %fusion.56) | copy-start | bytes 3076
  126.4 168.8 %all-gather.10.cloned.1.call-start = ((), (), s32[]{:S(2)}) async-start(), calls=%async_computation.7 | async-start | bytes 4096000 | tf_op jit(solution)/shard_map/all_gather | solution.py:34
  127.1 380.6 %all-gather.12.cloned.1.call-start = ((), (), s32[]{:S(2)}) async-start(), calls=%async_computation.8 | async-start | bytes 32768000 | tf_op jit(solution)/shard_map/all_gather | solution.py:34
  127.7 508.4 %all-gather.14.cloned.1.call-start = ((), (), s32[]{:S(2)}) async-start(), calls=%async_computation.9 | async-start | bytes 16384000 | tf_op jit(solution)/shard_map/all_gather | solution.py:34
  128.3 730.0 %reduce-scatter.6.cloned.1.call-start = ((), (), s32[]{:S(2)}) async-start(), calls=%async_computation.10 | async-start | bytes 6553600 | tf_op jit(solution)/shard_map/reduce_scatter | solution.py:210
  130.2 102.6 %copy-start.34 = (f32[256,20]{0,1:T(8,128)}, f32[256,20]{0,1:T(8,128)S(1)}, u32[]{:S(2)}) copy-start(f32[256,20]{0,1:T(8,128)S(1)} %multiply_reduce_fusion.16) | copy-start | bytes 61444
  130.2 102.6 %copy-start.30 = (f32[256,20]{0,1:T(8,128)}, f32[256,20]{0,1:T(8,128)S(1)}, u32[]{:S(2)}) copy-start(f32[256,20]{0,1:T(8,128)S(1)} %fusion.63) | copy-start | bytes 61444
  299.1 385.5 %copy-start.2 = (f32[256,1280]{1,0:T(8,128)}, f32[256,1280]{1,0:T(8,128)S(1)}, u32[]{:S(2)}) copy-start(f32[256,1280]{1,0:T(8,128)S(1)} %get-tuple-element.467) | copy-start | bytes 3932164
  507.7 15.9 copy-start.38
  507.7 15.9 copy-start.44
  529.5 114.9 %copy-start.39 = (f32[1280]{0:T(1024)S(1)}, f32[1280]{0:T(1024)}, u32[]{:S(2)}) copy-start(f32[1280]{0:T(1024)} %param.26) | copy-start | bytes 15364
  647.8 14.0 copy-start.22
  764.3 142.5 %reduce-scatter.10.cloned.1.call-start = ((), (), s32[]{:S(2)}) async-start(), calls=%async_computation.12 | async-start | bytes 4096000 | tf_op jit(solution)/shard_map/reduce_scatter | solution.py:44
  768.3 267.2 %reduce-scatter.14.cloned.1.call-start = ((), (), s32[]{:S(2)}) async-start(), calls=%async_computation.14 | async-start | bytes 16384000 | tf_op jit(solution)/shard_map/reduce_scatter | solution.py:44
  777.0 86.9 %copy-start.31 = (f32[256,20]{0,1:T(8,128)S(1)}, f32[256,20]{0,1:T(8,128)}, u32[]{:S(2)}) copy-start(f32[256,20]{0,1:T(8,128)} %copy-done.30) | copy-start | bytes 61444
  777.0 86.9 %copy-start.37 = (f32[20,64]{1,0:T(8,128)S(1)}, f32[20,64]{1,0:T(8,128)}, u32[]{:S(2)}) copy-start(f32[20,64]{1,0:T(8,128)} %copy-done.36) | copy-start | bytes 15364
  777.1 359.7 %reduce-scatter.8.cloned.1.call-start = ((), (), s32[]{:S(2)}) async-start(), calls=%async_computation.11 | async-start | bytes 12288000 | tf_op jit(solution)/shard_map/reduce_scatter | solution.py:44
  882.0 487.9 %reduce-scatter.12.cloned.1.call-start = ((), (), s32[]{:S(2)}) async-start(), calls=%async_computation.13 | async-start | bytes 32768000 | tf_op jit(solution)/shard_map/reduce_scatter | solution.py:44
  899.4 739.0 %all-reduce.12.cloned.1.call-start = ((), (), s32[]{:S(2)}) async-start(), calls=%async_computation.15 | async-start | bytes 26214400 | tf_op jit(solution)/shard_map/psum | solution.py:243
  1370.0 51.2 %copy-start.17 = (f32[256,1280]{1,0:T(8,128)S(1)}, f32[256,1280]{1,0:T(8,128)}, u32[]{:S(2)}) copy-start(f32[256,1280]{1,0:T(8,128)} %copy-done.16) | copy-start | bytes 3932164
  1370.0 51.2 %copy-start.41 = (f32[1280]{0:T(1024)S(1)}, f32[1280]{0:T(1024)}, u32[]{:S(2)}) copy-start(f32[1280]{0:T(1024)} %param.25) | copy-start | bytes 15364
  1638.4 9.6 copy-start.21
  (42 other events, 96.5 us)
Sparse Core Ops, SparseCore 0:
  9.8 102.1 all-gather.5
  126.5 98.0 all-gather.7
  226.4 43.2 all-gather.9
  271.4 236.1 all-gather.11
  509.4 126.7 all-gather.13
  764.5 93.7 reduce-scatter.5
  861.3 45.4 reduce-scatter.9
  910.6 124.8 reduce-scatter.13
  1038.6 98.0 reduce-scatter.7
  1139.7 230.1 reduce-scatter.11
  1372.6 265.7 all-reduce.11
where the time goes:
time: 1670 us; the launch traced here: 1660 us
  waiting for transfers between devices  1270 us (76%)
  matrix products  161 us (10%)
  local copies, waits for them, and re-layouts  91.2 us (5%)
  other arithmetic  72.6 us (4%)
  blocking collectives  45.2 us (3%)
    reduce_scatter x4, waiting for transfers between devices, owner_sums(): lax.psum_scatter(matmul_tn(activation, gradient).astype(jnp.bfloat16), 'f...  471 us
    all_gather x4, waiting for transfers between devices, gathered_product(): lax.all_gather(w_shard, 'fsdp', axis=0, tiled=True)  419 us
    psum x1, waiting for transfers between devices, body(): lax.psum(part_qkv.astype(jnp.bfloat16), ('grp', 'seq')).astype(jnp.float32)  209 us
    all_gather x1, waiting for transfers between devices, body(): kv_all = lax.all_gather(kv_local, 'seq', axis=0, tiled=True)  93.4 us
    reduce_scatter x1, waiting for transfers between devices, body(): lax.psum_scatter(grad_kv_all.astype(jnp.bfloat16), 'seq', scatter_dimensi...  80.8 us
    dot_general x4, matrix products, matmul_nt(): lax.dot_general(former, latter, (((1,), (1,)), ((), ())), preferred_eleme...  39.3 us
    dot_general x4, matrix products, gathered_product(): jnp.dot(operand, lax.all_gather(w_shard, 'fsdp', axis=0, tiled=True), pre...  34 us
  transfers between devices with their start and end apart: 11, of which 10 were waited for; matrix products, arithmetic and copies ran while one was open for 10% of the time, Pallas kernels for 0%

commit v1 on v0

v1 whole, which is shorter than its diff:
```python
import jax
import jax.numpy as jnp
from jax import lax
from jax.sharding import PartitionSpec as P

D = 1280
HEADS = 20
HEAD = 64

eps_norm = 1e-06
neg_big = -1e30
BF = jnp.bfloat16
F32 = jnp.float32


def inv_rms(value):
    return lax.rsqrt(jnp.mean(value * value, axis=-1, keepdims=True) + eps_norm)


def back(unit, inv, grad):
    return (grad - unit * jnp.mean(grad * unit, axis=-1, keepdims=True)) * inv


def mm(a, b):
    return jnp.dot(a, b, preferred_element_type=F32)


def mm_nt(a, b):
    return lax.dot_general(a, b, (((1,), (1,)), ((), ())), preferred_element_type=F32)


def mm_tn(a, b):
    return lax.dot_general(a, b, (((0,), (0,)), ((), ())), preferred_element_type=F32)


def gather(x, axes, dim=0):
    return lax.all_gather(x, axes, axis=dim, tiled=True)


def scatter(x, axes, dim=0):
    return lax.psum_scatter(x, axes, scatter_dimension=dim, tiled=True)


def attention(q, k, v, seg):
    n = seg.shape[0]
    pos = jnp.arange(n, dtype=jnp.int32)
    allowed = (pos[None, :] <= pos[:, None]) & ((seg[None, :] == 0) | (seg[None, :] == seg[:, None]))
    scores = jnp.einsum("qhe,khe->hqk", q, k, preferred_element_type=F32) * HEAD**-0.5
    scores = jnp.where(allowed[None], scores, neg_big)
    top = jnp.max(scores, axis=-1, keepdims=True)
    e = jnp.exp(scores - top)
    probs = e / jnp.sum(e, axis=-1, keepdims=True)
    mix = jnp.einsum("hqk,khe->qhe", probs.astype(BF), v, preferred_element_type=F32)
    return mix, probs


def attention_back(q, k, v, probs, gx):
    gp = jnp.einsum("qhe,khe->hqk", gx, v, preferred_element_type=F32)
    delta = jnp.sum(probs * gp, axis=-1, keepdims=True)
    gs = (probs * (gp - delta)).astype(BF)
    dq = jnp.einsum("hqk,khe->qhe", gs, k, preferred_element_type=F32) * HEAD**-0.5
    dk = jnp.einsum("hqk,qhe->khe", gs, q, preferred_element_type=F32) * HEAD**-0.5
    dv = jnp.einsum("hqk,qhe->khe", probs.astype(BF), gx, preferred_element_type=F32)
    return dq, dk, dv


def body(S, FS, inputs, segments, w_qkv, w_out, w_upgate, w_down, s_qk, alpha_attn, alpha_mlp, s_up, s_gate, cotangent):
    z = lax.axis_index("seq")
    f = lax.axis_index("fsdp")
    hp = -(-HEADS // S)
    hw = hp * HEAD
    wide = S * hw
    rows = w_qkv.shape[0]
    ff = s_up.shape[0]
    fl = ff // FS

    def head_pad(a):
        return jnp.pad(a, [(0, 0)] * (a.ndim - 1) + [(0, wide - D)])

    x = inputs[0].astype(F32)
    tok = x.shape[0]
    inv_x = inv_rms(x)
    h = x * inv_x
    hb = h.astype(BF)
    seg = segments[0]
    h_all = gather(hb, "seq")
    total = h_all.shape[0]
    wq = head_pad(w_qkv.reshape(rows, 3, D)).reshape(rows, 3, S, hw)
    wq = lax.dynamic_index_in_dim(wq, z, 2, keepdims=False)
    wq = gather(wq.reshape(rows, 3 * hw), "fsdp")
    wo = gather(w_out, "fsdp")
    wu = lax.all_to_all(w_upgate.reshape(rows, 2, FS, fl), "fsdp", split_axis=2, concat_axis=0, tiled=True)
    wu = wu.reshape(D, 2 * fl)
    gain = lax.dynamic_slice_in_dim(head_pad(s_qk), z * hw, hw).reshape(hp, HEAD)
    qkv = mm(h_all, wq).reshape(total, 3, hp, HEAD)
    inv_qk = inv_rms(qkv[:, :2])
    u_qk = qkv[:, :2] * inv_qk
    n_qk = (u_qk * gain).astype(BF)
    q, k, v = n_qk[:, 0], n_qk[:, 1], qkv[:, 2].astype(BF)
    mix, probs = attention(q, k, v, seg)
    mixb = mix.reshape(total, hw).astype(BF)
    mine = lax.all_to_all(mixb, "seq", split_axis=0, concat_axis=1, tiled=True)[:, :D]
    attn = mm(mine, wo)
    inv_a = inv_rms(attn)
    ua = attn * inv_a
    n = h + alpha_attn * (ua - h)
    inv_n = inv_rms(n)
    mid = n * inv_n
    midb = mid.astype(BF)
    mid_all = gather(midb, "fsdp")
    ug = mm(mid_all, wu)
    up, gate = ug[:, :fl], ug[:, fl:]
    su = lax.dynamic_slice_in_dim(s_up, f * fl, fl)
    sg = lax.dynamic_slice_in_dim(s_gate, f * fl, fl)
    a = gate * sg
    sig = jax.nn.sigmoid(a)
    silu = a * sig
    hidden = (up * su * silu).astype(BF)
    mlp = scatter(mm(hidden, w_down).astype(BF), "fsdp").astype(F32)
    inv_m = inv_rms(mlp)
    um = mlp * inv_m
    m = mid + alpha_mlp * (um - mid)
    inv_o = inv_rms(m)
    out = m * inv_o
    g = cotangent[0].astype(F32)
    g_m = back(out, inv_o, g)
    d_alpha_mlp = jnp.sum(g_m * (um - mid), axis=0)
    g_mlp = back(um, inv_m, alpha_mlp * g_m)
    g_mid1 = (1 - alpha_mlp) * g_m
    gm_all = gather(g_mlp.astype(BF), "fsdp")
    gh = mm_nt(gm_all, w_down)
    d_down = mm_tn(hidden, gm_all)
    g_up = gh * su * silu
    d_su = jnp.sum(up * gh * silu, axis=0)
    g_a = gh * up * su * sig * (1 + a * (1 - sig))
    g_gate = g_a * sg
    d_sg = jnp.sum(gate * g_a, axis=0)
    gu = jnp.concatenate([g_up, g_gate], axis=1).astype(BF)
    g_mid = g_mid1 + scatter(mm_nt(gu, wu).astype(BF), "fsdp").astype(F32)
    d_upgate = mm_tn(mid_all, gu)
    g_n = back(mid, inv_n, g_mid)
    d_alpha_attn = jnp.sum(g_n * (ua - h), axis=0)
    g_attn = back(ua, inv_a, alpha_attn * g_n)
    g_h1 = (1 - alpha_attn) * g_n
    ga = g_attn.astype(BF)
    gmix = head_pad(mm_nt(ga, wo).astype(BF))
    d_out = mm_tn(mine, ga)
    gx = lax.all_to_all(gmix, "seq", split_axis=1, concat_axis=0, tiled=True).reshape(total, hp, HEAD)
    dq, dk, dv = attention_back(q, k, v, probs, gx)
    g_qk = jnp.stack([dq, dk], axis=1)
    d_sqk = jnp.sum(g_qk * u_qk, axis=(0, 1)).reshape(hw)
    g_raw = back(u_qk, inv_qk, g_qk * gain)
    gq = jnp.concatenate([g_raw, dv[:, None]], axis=1).reshape(total, 3 * hw).astype(BF)
    g_h = g_h1 + scatter(mm_nt(gq, wq).astype(BF), "seq").astype(F32)
    d_qkv = mm_tn(h_all, gq)
    g_x = back(h, inv_x, g_h)

    d_down = lax.psum(d_down.astype(BF), ("grp", "seq")).astype(F32)
    d_up = scatter(d_upgate.astype(BF), "grp", 1)
    d_up = scatter(d_up, "seq", 1)
    part = d_up.shape[1]
    d_up = lax.all_to_all(d_up, "fsdp", split_axis=0, concat_axis=1, tiled=True)
    d_up = gather(gather(d_up.reshape(rows, FS, part), "seq", 2), "grp", 2)
    d_up = d_up.reshape(rows, FS, 2, fl).transpose(0, 2, 1, 3).reshape(rows, 2 * ff).astype(F32)
    d_o = scatter(d_out.astype(BF), "fsdp")
    d_o = lax.psum(d_o, ("grp", "seq")).astype(F32)
    d_q = scatter(d_qkv.astype(BF), "fsdp")
    d_q = lax.psum(d_q, "grp")
    d_q = gather(d_q.reshape(rows, 3, hw), "seq", 2)[:, :, :D].reshape(rows, 3 * D).astype(F32)
    slot = jnp.zeros((2, FS, fl), F32)
    slot = lax.dynamic_update_slice(slot, jnp.stack([d_su, d_sg])[:, None], (0, f, 0)).reshape(-1)
    slot_qk = lax.dynamic_update_slice(jnp.zeros((wide,), F32), d_sqk, (z * hw,))[:D]
    flat = lax.psum(jnp.concatenate([slot_qk, d_alpha_attn, d_alpha_mlp, slot]), ("grp", "seq", "fsdp"))

    def own(start, size):
        return lax.dynamic_slice_in_dim(flat, start + f * (size // FS), size // FS)

    return (
        out.astype(BF)[None], g_x[None], d_q, d_o, d_up, d_down,
        own(0, D), own(D, D), own(2 * D, D), own(3 * D, ff), own(3 * D + ff, ff),
    )


def solution(mesh):
    S, FS = mesh.shape["seq"], mesh.shape["fsdp"]
    tok = P(("grp", "fsdp"), "seq", None)
    w = P("fsdp", None)
    in_specs = (tok, P(("grp", "fsdp"), None), w, w, w, w, P(), P(), P(), P(), P(), tok)
    out_specs = (tok, tok, w, w, w, w) + (P("fsdp"),) * 5

    def run(*args):
        return body(S, FS, *args)

    return jax.shard_map(run, mesh=mesh, in_specs=in_specs, out_specs=out_specs, check_vma=False)
```

time: 1670 us -> 1060 us (0.63)
  waiting for transfers between devices: 1270 us -> 635 us
  local copies, waits for them, and re-layouts: 91.2 us -> 143 us
  matrix products: 161 us -> 131 us
  other arithmetic: 72.6 us -> 53.1 us
  blocking collectives: 45.2 us -> 62.9 us
    reduce_scatter x5 -> x6, waiting for transfers between devices: 551 us -> 144 us  [scatter(): return lax.psum_scatter(x, axes, scatter_dimension=dim, tiled=True)]
    all_gather x5 -> x8, waiting for transfers between devices: 512 us -> 271 us  [gather(): return lax.all_gather(x, axes, axis=dim, tiled=True)]
    psum x1 -> x2, waiting for transfers between devices: 209 us -> 116 us  [the longest x1 94.6 us: body(): d_o = lax.psum(d_o, ('grp', 'seq')).astype(F32)]
    all_to_all x0 -> x3, waiting for transfers between devices: none -> 85.3 us  [the longest x1 85.3 us: body(): lax.all_to_all(w_upgate.reshape(rows, 2, FS, fl), 'fsdp', split_axis=2, c...]
    dot_general x26 -> x17, matrix products: 161 us -> 118 us  [the longest x4 28.8 us: mm_nt(): lax.dot_general(a, b, (((1,), (1,)), ((), ())), preferred_element_type=F32)]
    convert_element_type x3 -> x6, local copies, waits for them, and re-layouts: 19.3 us -> 49.3 us  [the longest x3 44.6 us: body(): d_up.reshape(rows, FS, 2, fl).transpose(0, 2, 1, 3).reshape(rows, 2 * ff)]
    all_to_all x0 -> x1, blocking collectives: none -> 21.6 us  [body(): lax.all_to_all(gmix, 'seq', split_axis=1, concat_axis=0, tiled=True)]
    reshape x2 -> x7, local copies, waits for them, and re-layouts: 10.6 us -> 30.6 us  [the longest x2 21.3 us: body(): w_upgate.reshape(rows, 2, FS, fl)]
  transfers between devices with their start and end apart: 11 -> 20, of which waited for: 10 -> 15; matrix products, arithmetic and copies ran while one was open for 10% -> 19% of each run, Pallas kernels for 0% -> 0%
where the time goes in v1:
time: 1060 us
  waiting for transfers between devices  635 us (60%)
  local copies, waits for them, and re-layouts  143 us (13%)
  matrix products  131 us (12%)
  blocking collectives  62.9 us (6%)
  other arithmetic  53.1 us (5%)
  starting transfers between devices  15.4 us (1%)
  between operations  14.7 us (1%)
    all_gather x8, waiting for transfers between devices, gather(): return lax.all_gather(x, axes, axis=dim, tiled=True)  271 us
    reduce_scatter x6, waiting for transfers between devices, scatter(): return lax.psum_scatter(x, axes, scatter_dimension=dim, tiled=True)  144 us
    psum x1, waiting for transfers between devices, body(): d_o = lax.psum(d_o, ('grp', 'seq')).astype(F32)  94.6 us
    all_to_all x1, waiting for transfers between devices, body(): lax.all_to_all(w_upgate.reshape(rows, 2, FS, fl), 'fsdp', split_axis=2, c...  85.3 us
    convert_element_type x3, local copies, waits for them, and re-layouts, body(): d_up.reshape(rows, FS, 2, fl).transpose(0, 2, 1, 3).reshape(rows, 2 * ff)  44.6 us
    psum x1, blocking collectives, body(): lax.psum(jnp.concatenate([slot_qk, d_alpha_attn, d_alpha_mlp, slot]), ('g...  41.4 us
    unnamed x75, local copies, waits for them, and re-layouts  41.1 us
    dot_general x4, matrix products, mm_nt(): lax.dot_general(a, b, (((1,), (1,)), ((), ())), preferred_element_type=F32)  28.8 us
  transfers between devices with their start and end apart: 20, of which 15 were waited for; matrix products, arithmetic and copies ran while one was open for 19% of the time, Pallas kernels for 0%

profile of v1, /device:TPU:0, one launch (start us, length us, event | category | flops | bytes accessed | tf_op | source)
XLA Modules:
  0.0 1055.4 jit_solution(4196872592315419156)
XLA Ops:
  32.6 35.0 %all-gather.11.cloned.1.call-done = bf16[1280,960]{1,0:T(8,128)(2,1)} async-done(((bf16[320,960]{1,0:T(8,128)(2,1)}), bf16[1280,960]{1,0:T(8,128)(2,1)}) %all-gather.11.cloned.1.call-update) | async-done | bytes 2457616 | tf_op jit(solution)/shard_map/all_gather | solution.py:37
  67.6 56.9 %all-gather.9.cloned.1.call-done = bf16[1024,1280]{1,0:T(8,128)(2,1)} async-done(((bf16[256,1280]{1,0:T(8,128)(2,1)}), bf16[1024,1280]{1,0:T(8,128)(2,1)}) %all-gather.9.cloned.1.call-update) | async-done | bytes 2621456 | tf_op jit(solution)/shard_map/all_gather | solution.py:37
  133.9 13.2 %fusion.61 = (f32[5,1024]{1,0:T(8,128)S(1)}, f32[5,1024,1024]{1,2,0:T(8,128)}) fusion(pred[1024,1024]{0,1:T(8,128)(4,1)} %fusion.10, bf16[1024,2,5,64]{0,3,2,1:T(8,128)(2,1)} %multiply_convert_fusion.5), kind=kOutput, calls=%fused_computation.124 | convolution fusion | flops 692061184 | bytes 23351296 | tf_op jit(solution)/shard_map/sub | solution.py:51
  176.8 10.8 %copy.59 = bf16[320,2,4,1280]{3,1,0,2:T(2,128)(2,1)} copy(bf16[320,2,4,1280]{3,2,1,0:T(4,128)(2,1)} %reshape.229) | data formatting | bytes 13107200 | tf_op jit(solution)/shard_map/reshape | solution.py:92
  201.7 85.3 %all-to-all-done.1 = bf16[320,2,4,1280]{3,1,0,2:T(2,128)(2,1)} async-done(((bf16[320,2,4,1280]{3,1,0,2:T(2,128)(2,1)}), bf16[320,2,4,1280]{3,1,0,2:T(2,128)(2,1)}, u32[]{:S(2)}, u32[]{:S(2)}) %all-to-all-start.1) | async-done | bytes 6553632 | tf_op jit(solution)/shard_map/all_to_all | solution.py:92
  314.4 39.8 %reduce-scatter.10.cloned.1.call-done = bf16[256,1280]{1,0:T(8,128)(2,1)} async-done(((bf16[1024,1280]{1,0:T(8,128)(2,1)}), bf16[256,1280]{1,0:T(8,128)(2,1)}) %reduce-scatter.10.cloned.1.call-update) | async-done | bytes 655376 | tf_op jit(solution)/shard_map/reduce_scatter | solution.py:41
  362.0 39.4 %all-gather.17.cloned.1.call-done = bf16[1024,1280]{1,0:T(8,128)(2,1)} async-done(((bf16[256,1280]{1,0:T(8,128)(2,1)}), bf16[1024,1280]{1,0:T(8,128)(2,1)}) %all-gather.17.cloned.1.call-update) | async-done | bytes 2621456 | tf_op jit(solution)/shard_map/all_gather | solution.py:37
  412.7 11.1 %convolution_convert_fusion.5 = bf16[1024,1280]{1,0:T(8,128)(2,1)} fusion(bf16[1280,2560]{1,0:T(8,128)(2,1)} %bitcast.128, bf16[1024,1280]{1,0:T(8,128)(2,1)S(1)} %multiply_convert_fusion.1, bf16[1024,1280]{1,0:T(8,128)(2,1)S(1)} %get-tuple-element.62), kind=kOutput, calls=%fused_computation.32 | convolution fusion | flops 6722682880 | bytes 14417920 | tf_op jit(solution)/shard_map/dot_general | solution.py:29
  423.9 11.1 %convolution_convert_fusion = bf16[1280,2560]{1,0:T(8,128)(2,1)} fusion(bf16[1024,1280]{1,0:T(8,128)(2,1)} %all-gather.15.cloned.1.call-done, bf16[1024,1280]{1,0:T(8,128)(2,1)S(1)} %multiply_convert_fusion.1, bf16[1024,1280]{1,0:T(8,128)(2,1)} %copy-done.34), kind=kOutput, calls=%fused_computation.6 | convolution fusion | flops 6724648960 | bytes 14417920 | tf_op jit(solution)/shard_map/dot_general | solution.py:33
  435.1 28.5 %reduce-scatter.12.cloned.1.call-done = bf16[256,1280]{1,0:T(8,128)(2,1)} async-done(((bf16[1024,1280]{1,0:T(8,128)(2,1)}), bf16[256,1280]{1,0:T(8,128)(2,1)}) %reduce-scatter.12.cloned.1.call-update) | async-done | bytes 655376 | tf_op jit(solution)/shard_map/reduce_scatter | solution.py:41
  470.2 21.6 %all_to_all.63 = bf16[256,4,320]{0,2,1:T(8,128)(2,1)S(1)} all-to-all(bf16[256,4,320]{0,2,1:T(8,128)(2,1)S(1)} %bitcast.133), channel_id=1, replica_groups=mesh['grp'=2,'seq'=4,'fsdp'=4] {'seq'}, dimensions={1} | all-to-all | bytes 1310720 | tf_op jit(solution)/shard_map/all_to_all | solution.py:148
  492.8 14.3 %multiply_reduce_fusion = (f32[5,1024]{1,0:T(8,128)S(1)}, f32[5,1024,1024]{1,2,0:T(8,128)}) fusion(f32[5,1024,1024]{1,2,0:T(8,128)} %get-tuple-element.70, f32[5,1024]{1,0:T(8,128)S(1)} %get-tuple-element.69, bf16[1024,5,64]{0,2,1:T(8,128)(2,1)S(1)} %reshape.231, f32[1024,3,5,64]{0,3,2,1:T(8,128)} %bitcast.123), kind=kOutput, calls=%fused_computation.2 | convolution fusion | flops 686812160 | bytes 43294720 | tf_op jit(solution)/shard_map/qhe,khe->hqk/dot_general | solution.py:58
  513.0 15.1 %multiply_convert_fusion = bf16[5,1024,1024]{1,2,0:T(8,128)(2,1)S(1)} fusion(f32[5,1024,1024]{1,2,0:T(8,128)} %get-tuple-element.74, f32[5,1024]{1,0:T(8,128)S(1)} %get-tuple-element.73, f32[5,1024,1024]{1,2,0:T(8,128)} %get-tuple-element.70, f32[5,1024]{1,0:T(8,128)S(1)} %get-tuple-element.69), kind=kLoop, calls=%fused_computation.1 | loop fusion | flops 20971520 | bytes 52469760 | tf_op jit(solution)/shard_map/convert_element_type | solution.py:60
  556.1 17.4 %reduce-scatter.22.cloned.1.call-done = bf16[320,1280]{1,0:T(8,128)(2,1)} async-done(((bf16[1280,1280]{1,0:T(8,128)(2,1)}), bf16[320,1280]{1,0:T(8,128)(2,1)}) %reduce-scatter.22.cloned.1.call-update) | async-done | bytes 819216
  580.1 43.1 %reduce-scatter.16.cloned.1.call-done = bf16[320,960]{1,0:T(8,128)(2,1)} async-done(((bf16[1280,960]{1,0:T(8,128)(2,1)}), bf16[320,960]{1,0:T(8,128)(2,1)}) %reduce-scatter.16.cloned.1.call-update) | async-done | bytes 614416 | tf_op jit(solution)/shard_map/reduce_scatter | solution.py:41
  642.4 29.4 %reduce-scatter.18.cloned.1.call-done = bf16[320,1280]{1,0:T(8,128)(2,1)} async-done(((bf16[1280,1280]{1,0:T(8,128)(2,1)}), bf16[320,1280]{1,0:T(8,128)(2,1)}) %reduce-scatter.18.cloned.1.call-update) | async-done | bytes 819216 | tf_op jit(solution)/shard_map/reduce_scatter | solution.py:41
  671.9 21.6 %all-reduce.4.cloned.1.call-done = bf16[320,3,320]{0,2,1:T(8,128)(2,1)} async-done(((bf16[320,3,320]{0,2,1:T(8,128)(2,1)}), bf16[320,3,320]{0,2,1:T(8,128)(2,1)}) %all-reduce.4.cloned.1.call-update) | async-done | bytes 614416 | tf_op jit(solution)/shard_map/psum | solution.py:168
  693.6 79.7 %all-gather.21.cloned.1.call-done = bf16[320,4,1280]{0,1,2:T(4,128)(2,1)} async-done(((bf16[320,4,320]{0,1,2:T(4,128)(2,1)}), bf16[320,4,1280]{0,1,2:T(4,128)(2,1)}) %all-gather.21.cloned.1.call-update) | async-done | bytes 3276816 | tf_op jit(solution)/shard_map/all_gather | solution.py:37
  781.7 41.4 %psum.31 = f32[14080]{0:T(1024)S(1)} all-reduce(f32[14080]{0:T(1024)S(1)} %pad_maximum_fusion.5), channel_id=1, replica_groups=mesh['grp'=2,'seq'=4,'fsdp'=4] {'grp','seq','fsdp'}, use_global_device_ids=true, to_apply=%region_30.31 | all-reduce | flops 14080 | bytes 112640 | tf_op jit(solution)/shard_map/psum | solution.py:173
  830.7 94.6 %all-reduce.6.cloned.1.call-done = (bf16[320,1280]{1,0:T(8,128)(2,1)}, bf16[1280,1280]{1,0:T(8,128)(2,1)}) async-done(((bf16[320,1280]{1,0:T(8,128)(2,1)}, bf16[1280,1280]{1,0:T(8,128)(2,1)}), (bf16[320,1280]{1,0:T(8,128)(2,1)}, bf16[1280,1280]{1,0:T(8,128)(2,1)})) %all-reduce.6.cloned.1.call-update) | async-done | bytes 4096016 | tf_op jit(solution)/shard_map/psum | solution.py:166
  933.0 53.9 %all-gather.19.cloned.1.call-done = bf16[320,3,1280]{0,2,1:T(8,128)(2,1)} async-done(((bf16[320,3,320]{0,2,1:T(8,128)(2,1)}), bf16[320,3,1280]{0,2,1:T(8,128)(2,1)}) %all-gather.19.cloned.1.call-update) | async-done | bytes 2457616 | tf_op jit(solution)/shard_map/all_gather | solution.py:37
  1004.1 15.1 %reshape.239 = f32[320,4,2,1280]{3,2,0,1:T(2,128)} reshape(bf16[320,4,2560]{2,0,1:T(8,128)(2,1)} %all-gather.23.cloned.1.call-done) | data formatting | bytes 19660800 | tf_op jit(solution)/shard_map/convert_element_type | solution.py:164
  1019.3 14.0 %copy.69 = f32[320,2,4,1280]{3,2,1,0:T(4,128)} copy(f32[320,2,4,1280]{3,1,0,2:T(2,128)} %bitcast.119) | data formatting | bytes 26214400 | tf_op jit(solution)/shard_map/convert_element_type | solution.py:164
  1033.3 15.5 %reshape.238 = f32[320,10240]{1,0:T(8,128)} reshape(f32[320,2,4,1280]{3,2,1,0:T(4,128)} %copy.69) | data formatting | bytes 26214400 | tf_op jit(solution)/shard_map/convert_element_type | solution.py:164
  (203 shorter events, 232.8 us)
Async XLA Ops:
  7.2 302.3 %copy-start = (bf16[1280,1280]{1,0:T(8,128)(2,1)S(1)}, bf16[1280,1280]{1,0:T(8,128)(2,1)}, u32[]{:S(2)}) copy-start(bf16[1280,1280]{1,0:T(8,128)(2,1)} %param.17) | copy-start | bytes 9830404
  7.2 60.4 %all-gather.11.cloned.1.call-start = ((), (), s32[]{:S(2)}) async-start(), calls=%async_computation.12 | async-start | bytes 3276800 | tf_op jit(solution)/shard_map/all_gather | solution.py:37
  25.2 99.3 %all-gather.9.cloned.1.call-start = ((), (), s32[]{:S(2)}) async-start(), calls=%async_computation.11 | async-start | bytes 3276800 | tf_op jit(solution)/shard_map/all_gather | solution.py:37
  28.7 164.9 %all-gather.13.cloned.1.call-start = ((), (), s32[]{:S(2)}) async-start(), calls=%async_computation.13 | async-start | bytes 4096000 | tf_op jit(solution)/shard_map/all_gather | solution.py:37
  30.3 100.0 %copy-start.29 = (f32[5,64]{1,0:T(8,128)}, f32[5,64]{1,0:T(8,128)S(1)}, u32[]{:S(2)}) copy-start(f32[5,64]{1,0:T(8,128)S(1)} %mul.346) | copy-start | bytes 3844
  162.2 25.5 %all-to-all-start = ((bf16[4,256,320]{1,2,0:T(8,128)(2,1)}), bf16[4,256,320]{1,2,0:T(8,128)(2,1)}, u32[]{:S(2)}, u32[]{:S(2)}) async-start(bf16[4,256,320]{1,2,0:T(8,128)(2,1)} %copy.58), calls=%async_computation | async-start | bytes 1310720 | tf_op jit(solution)/shard_map/all_to_all | solution.py:102
  187.7 99.4 %all-to-all-start.1 = ((bf16[320,2,4,1280]{3,1,0,2:T(2,128)(2,1)}), bf16[320,2,4,1280]{3,1,0,2:T(2,128)(2,1)}, u32[]{:S(2)}, u32[]{:S(2)}) async-start(bf16[320,2,4,1280]{3,1,0,2:T(2,128)(2,1)} %copy.59), calls=%async_computation.1 | async-start | bytes 13107200 | tf_op jit(solution)/shard_map/all_to_all | solution.py:92
  193.0 101.0 %all-gather.15.cloned.1.call-start = ((), (), s32[]{:S(2)}) async-start(), calls=%async_computation.14 | async-start | bytes 3276800 | tf_op jit(solution)/shard_map/all_gather | solution.py:37
  200.1 154.1 %reduce-scatter.10.cloned.1.call-start = ((), (), s32[]{:S(2)}) async-start(), calls=%async_computation.15 | async-start | bytes 3276800 | tf_op jit(solution)/shard_map/reduce_scatter | solution.py:41
  314.3 41.3 %copy-start.27 = (f32[1280]{0:T(1024)S(1)}, f32[1280]{0:T(1024)}, u32[]{:S(2)}) copy-start(f32[1280]{0:T(1024)} %param.20) | copy-start | bytes 15364
  314.3 87.1 %all-gather.17.cloned.1.call-start = ((), (), s32[]{:S(2)}) async-start(), calls=%async_computation.16 | async-start | bytes 3276800 | tf_op jit(solution)/shard_map/all_gather | solution.py:37
  361.7 101.8 %reduce-scatter.12.cloned.1.call-start = ((), (), s32[]{:S(2)}) async-start(), calls=%async_computation.17 | async-start | bytes 3276800 | tf_op jit(solution)/shard_map/reduce_scatter | solution.py:41
  423.8 83.3 %reduce-scatter.20.cloned.1.call-start = ((), (), s32[]{:S(2)}) async-start(), calls=%async_computation.23 | async-start | bytes 9830400 | tf_op jit(solution)/shard_map/reduce_scatter | solution.py:41
  435.0 30.6 %copy-start.7 = (bf16[1,256,1280]{2,1,0:T(8,128)(2,1)S(1)}, bf16[1,256,1280]{2,1,0:T(8,128)(2,1)}, u32[]{:S(2)}) copy-start(bf16[1,256,1280]{2,1,0:T(8,128)(2,1)} %param.12) | copy-start | bytes 1966084
  435.0 138.5 %reduce-scatter.22.cloned.1.call-start = ((), (), s32[]{:S(2)}) async-start(), calls=%async_computation.26 | async-start | bytes 4096000
  512.8 110.4 %reduce-scatter.16.cloned.1.call-start = ((), (), s32[]{:S(2)}) async-start(), calls=%async_computation.19 | async-start | bytes 3276800 | tf_op jit(solution)/shard_map/reduce_scatter | solution.py:41
  551.2 120.6 %reduce-scatter.18.cloned.1.call-start = ((), (), s32[]{:S(2)}) async-start(), calls=%async_computation.22 | async-start | bytes 4096000 | tf_op jit(solution)/shard_map/reduce_scatter | solution.py:41
  576.4 49.4 %all-to-all-start.3 = ((bf16[4,320,320]{1,2,0:T(8,128)(2,1)}), bf16[4,320,320]{1,2,0:T(8,128)(2,1)S(1)}, u32[]{:S(2)}, u32[]{:S(2)}) async-start(bf16[4,320,320]{1,2,0:T(8,128)(2,1)} %copy.66), calls=%async_computation.9 | async-start | bytes 1966080 | tf_op jit(solution)/shard_map/all_to_all | solution.py:162
  580.1 113.4 %all-reduce.4.cloned.1.call-start = ((), (), s32[]{:S(2)}) async-start(), calls=%async_computation.20 | async-start | bytes 1474560 | tf_op jit(solution)/shard_map/psum | solution.py:168
  625.4 147.9 %all-gather.21.cloned.1.call-start = ((), (), s32[]{:S(2)}) async-start(), calls=%async_computation.24 | async-start | bytes 4915200 | tf_op jit(solution)/shard_map/all_gather | solution.py:37
  627.6 200.1 %reduce-scatter.14.cloned.1.call-start = ((), (), s32[]{:S(2)}) async-start(), calls=%async_computation.18 | async-start | bytes 3276800 | tf_op jit(solution)/shard_map/reduce_scatter | solution.py:41
  634.5 290.8 %all-reduce.6.cloned.1.call-start = ((), (), s32[]{:S(2)}) async-start(), calls=%async_computation.27 | async-start | bytes 8192000 | tf_op jit(solution)/shard_map/psum | solution.py:166
  671.8 315.1 %all-gather.19.cloned.1.call-start = ((), (), s32[]{:S(2)}) async-start(), calls=%async_computation.21 | async-start | bytes 3686400 | tf_op jit(solution)/shard_map/all_gather | solution.py:37
  693.5 310.6 %all-gather.23.cloned.1.call-start = ((), (), s32[]{:S(2)}) async-start(), calls=%async_computation.25 | async-start | bytes 9830400 | tf_op jit(solution)/shard_map/all_gather | solution.py:37
  (31 other events, 157.4 us)
Sparse Core Ops, SparseCore 0:
  25.3 42.2 all-gather.10
  69.7 54.7 all-gather.8
  126.3 43.6 all-gather.12
  200.2 80.8 all-gather.14
  314.4 39.7 reduce-scatter.9
  361.9 39.4 all-gather.16
  424.0 39.5 reduce-scatter.11
  466.4 14.0 reduce-scatter.19
  512.9 60.5 reduce-scatter.21
  576.9 46.1 reduce-scatter.15
  626.7 44.9 reduce-scatter.17
  674.6 18.8 all-reduce.3
  695.7 77.6 all-gather.20
  776.0 51.6 reduce-scatter.13
  830.6 94.6 all-reduce.5
  926.8 60.0 all-gather.18
  988.3 15.8 all-gather.22

commit v2 on v1

--- a/solution.py
+++ b/solution.py
@@ -1,6 +1,8 @@
 import jax
 import jax.numpy as jnp
 from jax import lax
+from jax.experimental import pallas as pl
+from jax.experimental.pallas import tpu as pltpu
 from jax.sharding import PartitionSpec as P
 
 D = 1280
@@ -11,6 +13,9 @@
 neg_big = -1e30
 BF = jnp.bfloat16
 F32 = jnp.float32
+MESH = pl.DeviceIdType.MESH
+ANY = pl.BlockSpec(memory_space=pl.ANY)
+VM = pl.BlockSpec(memory_space=pltpu.VMEM)
 
 
 def inv_rms(value):
@@ -33,25 +38,285 @@
     return lax.dot_general(a, b, (((0,), (0,)), ((), ())), preferred_element_type=F32)
 
 
+def rcopy(src, dst, ss, rs, dev):
+    return pltpu.make_async_remote_copy(src, dst, ss, rs, device_id=dev, device_id_type=MESH)
+
+
+def greet(peers):
+    bar = pltpu.get_barrier_semaphore()
+    for p in peers:
+        pl.semaphore_signal(bar, inc=1, device_id=p, device_id_type=MESH)
+    pl.semaphore_wait(bar, len(peers))
+
+
+def ds(start, size, mult):
+    return pl.ds(pl.multiple_of(start, mult), size)
+
+
+def visible(seg_col, seg_row, q0, k0, nq, nk):
+    qi = q0 + lax.broadcasted_iota(jnp.int32, (nq, nk), 0)
+    ki = k0 + lax.broadcasted_iota(jnp.int32, (nq, nk), 1)
+    return (ki <= qi) & ((seg_row == 0) | (seg_row == seg_col))
+
+
+def attn_bias(S, tok, half, bias, segc, segr):
+    for qb in range(S):
+        q0 = qb * tok
+        k0 = q0 if q0 < half else half
+        nk = q0 + tok - k0
+        ok = visible(segc[q0 : q0 + tok], segr[:, k0 : k0 + nk], q0, k0, tok, nk)
+        bias[qb, :, :nk] = jnp.where(ok, 0.0, neg_big)
+
+
+def first_kernel(S, FS, hp, x_ref, segc, segr, wqkv, wout, gain, alpha, wup,
+                 hall_o, wq_o, wo_o, wu_o, raw_o, qkv_o, res_o, mine_o, attn_o, mid_o,
+                 hall, wq, wo, raw, qkv, res, bias, oh, mixs, mine, recv,
+                 s_up, r_up, s_dn, r_dn, s_wq, r_wq, s_wo, r_wo, s_wu, r_wu, f_wq, f_wo, f_wu,
+                 g_wq, g_wo, g_wu, s_mx, r_mx, out_sem):
+    g, z, f = lax.axis_index("grp"), lax.axis_index("seq"), lax.axis_index("fsdp")
+    tok = x_ref.shape[0]
+    rows = wqkv.shape[0]
+    hr = rows // 2
+    hw = hp * HEAD
+    ff = wup.shape[1] // 2
+    fl = ff // FS
+    total = S * tok
+    half = total // 2
+    fpeers = [lax.rem(f + i, FS) for i in range(1, FS)]
+    zpeers = [lax.rem(z + i, S) for i in range(1, S)]
+    greet([(g, z, p) for p in fpeers] + [(g, p, f) for p in zpeers] + [(1 - g, z, f)])
+
+    x = x_ref[...].astype(F32)
+    hall[z] = (x * inv_rms(x)).astype(BF)
+
+    def up(t, b):
+        return rcopy(hall.at[b], hall.at[b], s_up.at[t], r_up.at[t], (g, lax.rem(z + 1, S), f))
+
+    def down(t, b):
+        return rcopy(hall.at[b], hall.at[b], s_dn.at[t], r_dn.at[t], (g, lax.rem(z + S - 1, S), f))
+
+    @pl.when(z + 1 < S)
+    def _():
+        up(0, z).start()
+
+    @pl.when(z > 0)
+    def _():
+        down(0, z).start()
+
+    for k in range(S):
+        lo, hi = k * hw, min((k + 1) * hw, D)
+
+        @pl.when(z == k)
+        def _():
+            parts = []
+            for c in range(3):
+                if hi > lo:
+                    parts.append(wqkv[:, c * D + lo : c * D + hi])
+                if hi - lo < hw:
+                    parts.append(jnp.zeros((rows, hw - max(hi - lo, 0)), BF))
+            wq[ds(f * rows, rows, 16)] = jnp.concatenate(parts, axis=1)
+
+    def wq_half(src, gg):
+        return wq.at[ds(src * rows + gg * hr, hr, 16)]
+
+    def wo_half(src, gg):
+        return wo.at[ds(src * rows + gg * hr, hr, 16)]
+
+    c_wq = [rcopy(wq_half(f, g), wq_half(f, g), s_wq.at[i], r_wq.at[i], (g, z, p)) for i, p in enumerate(fpeers)]
+    for c in c_wq:
+        c.start()
+    attn_bias(S, tok, half, bias, segc, segr)
+    wo[ds(f * rows, rows, 16)] = wout[...]
+    qkv[2, :, :, HEAD:] = jnp.where(lax.broadcasted_iota(jnp.int32, (hp, total, HEAD), 2) == 0, 1.0, 0.0).astype(BF)
+
+    bpeers = [lax.rem(f + FS - i, FS) for i in range(1, FS)]
+    partner = (1 - g, z, f)
+    fw_wq = [rcopy(wq_half(p, g), wq_half(p, g), f_wq.at[i], g_wq.at[i], partner) for i, p in enumerate(bpeers)]
+    for i in range(FS - 1):
+        c_wq[i].wait_recv()
+        fw_wq[i].start()
+    c_wo = [rcopy(wo_half(f, g), wo_half(f, g), s_wo.at[i], r_wo.at[i], (g, z, p)) for i, p in enumerate(fpeers)]
+    for c in c_wo:
+        c.start()
+
+    def wu_cp(i, p):
+        return rcopy(wup.at[:, ds(g * ff + p * fl, fl, 128)], wu_o.at[g, f], s_wu.at[i], r_wu.at[i], (g, z, p))
+
+    c_wu = [wu_cp(i, p) for i, p in enumerate(fpeers)]
+    for c in c_wu:
+        c.start()
+    for i in range(FS - 1):
+        fw_wq[i].wait_recv()
+
+    def step(i, carry):
+        t = lax.div(i - 1, 2)
+        is_up = lax.rem(i, 2) == 1
+        b = jnp.where(i == 0, z, jnp.where(is_up, z - 1 - t, z + 1 + t))
+
+        @pl.when((b >= 0) & (b < S))
+        def _():
+            @pl.when((i > 0) & is_up)
+            def _():
+                up(t, b).wait_recv()
+
+                @pl.when(z + 1 < S)
+                def _():
+                    up(t + 1, b).start()
+
+            @pl.when((i > 0) & jnp.logical_not(is_up))
+            def _():
+                down(t, b).wait_recv()
+
+                @pl.when(z > 0)
+                def _():
+                    down(t + 1, b).start()
+
+            acc = mm(hall[b], wq[...])
+            at = ds(b * tok, tok, 16)
+            for j in range(hp):
+                for c in range(2):
+                    v = acc[:, c * hw + j * HEAD : c * hw + (j + 1) * HEAD]
+                    raw[c, j, at, :] = v
+                    u = v * inv_rms(v) * gain[j : j + 1]
+                    qkv[c, j, at, :HEAD] = u.astype(BF)
+                qkv[2, j, at, :HEAD] = acc[:, 2 * hw + j * HEAD : 2 * hw + (j + 1) * HEAD].astype(BF)
+
+        return carry
+
+    lax.fori_loop(0, 2 * S - 1, step, 0)
+    outs = [
+        pltpu.make_async_copy(hall, hall_o, out_sem.at[0]),
+        pltpu.make_async_copy(wq, wq_o, out_sem.at[1]),
+        pltpu.make_async_copy(raw, raw_o, out_sem.at[2]),
+        pltpu.make_async_copy(qkv, qkv_o, out_sem.at[3]),
+    ]
+    for c in outs:
+        c.start()
+
+    def mx(qb):
+        return rcopy(mixs.at[qb], recv.at[z], s_mx.at[qb], r_mx.at[z], (g, qb, f))
+
+    for qb in reversed(range(S)):
+        q0 = qb * tok
+        n = q0 + tok
+        k0 = q0 if q0 < half else half
+
+        def head(j, carry):
+            q = qkv[0, j, q0:n, :HEAD] * jnp.asarray(HEAD**-0.5, BF)
+            s = mm_nt(q, qkv[1, j, :n, :HEAD])
+            tail = s[:, k0:] + bias[qb, :, : n - k0]
+            e = jnp.exp(jnp.concatenate([s[:, :k0], tail], axis=1) if k0 else tail)
+            o = mm(e.astype(BF), qkv[2, j, :n])
+            rinv = 1.0 / o[:, HEAD : HEAD + 1]
+            o = o[:, :HEAD] * rinv
+            res[j, q0:n, :HEAD] = o
+            res[j, q0:n, HEAD:] = jnp.broadcast_to(rinv, (tok, HEAD))
+            oh[j] = o.astype(BF)
+            return carry
+
+        lax.fori_loop(0, hp, head, 0)
+        block = jnp.concatenate([oh[j] for j in range(hp)], axis=1)
+        mixs[qb] = block
+
+        @pl.when(z != qb)
+        def _():
+            mx(qb).start()
+
+        @pl.when(z == qb)
+        def _():
+            recv[qb] = block
+
+        if qb == S - 1:
+            fw_wo = [rcopy(wo_half(p, g), wo_half(p, g), f_wo.at[i], g_wo.at[i], partner) for i, p in enumerate(bpeers)]
+            for i in range(FS - 1):
+                c_wo[i].wait_recv()
+                fw_wo[i].start()
+
+    fw_wu = [rcopy(wu_o.at[g, p], wu_o.at[g, p], f_wu.at[i], g_wu.at[i], partner) for i, p in enumerate(bpeers)]
+    for i in range(FS - 1):
+        c_wu[i].wait_recv()
+        fw_wu[i].start()
+    for i in range(FS - 1):
+        fw_wo[i].wait_recv()
+    outs2 = [pltpu.make_async_copy(wo, wo_o, out_sem.at[4]), pltpu.make_async_copy(res, res_o, out_sem.at[5])]
+    for c in outs2:
+        c.start()
+    for k in range(S):
+        @pl.when(z != k)
+        def _():
+            rcopy(mixs.at[0], recv.at[k], s_mx.at[0], r_mx.at[k], (g, k, f)).wait_recv()
+
+    mine[...] = jnp.concatenate([recv[k] for k in range(S)], axis=1)[:, :D]
+    attn = mm(mine[...], wo[...])
+    attn_o[...] = attn
+    mine_o[...] = mine[...]
+    x = x_ref[...].astype(F32)
+    h = x * inv_rms(x)
+    n_ = h + alpha[...] * (attn * inv_rms(attn) - h)
+    mid_o[...] = (n_ * inv_rms(n_)).astype(BF)
+
+    for t in range(S - 1):
+        @pl.when((z + 1 < S) & (z - t >= 0))
+        def _():
+            up(t, z).wait_send()
+
+        @pl.when((z > 0) & (z + t < S))
+        def _():
+            down(t, z).wait_send()
+
+    for i in range(FS - 1):
+        c_wq[i].wait_send()
+        c_wo[i].wait_send()
+        c_wu[i].wait_send()
+        fw_wq[i].wait_send()
+        fw_wo[i].wait_send()
+        fw_wu[i].wait()
+    for k in range(S):
+        @pl.when(z != k)
+        def _():
+            mx(k).wait_send()
+    for c in outs + outs2:
+        c.wait()
+
+
+def first(S, FS, hp, x, seg, wqkv, wout, gain, alpha, wup):
+    tok, total = x.shape[0], seg.shape[0]
+    rows = wqkv.shape[0]
+    hw = hp * HEAD
+    fl = wup.shape[1] // 2 // FS
+    sds = jax.ShapeDtypeStruct
+    outs = [
+        sds((S, tok, D), BF), sds((D, 3 * hw), BF), sds((D, D), BF), sds((2, FS, rows, fl), BF),
+        sds((2, hp, total, HEAD), F32), sds((3, hp, total, 2 * HEAD), BF), sds((hp, total, 2 * HEAD), F32),
+        sds((tok, D), BF), sds((tok, D), F32), sds((tok, D), BF),
+    ]
+    dma = lambda n: pltpu.SemaphoreType.DMA((n,))
+    F1 = FS - 1
+    return pl.pallas_call(
+        lambda *refs: first_kernel(S, FS, hp, *refs),
+        out_shape=outs,
+        in_specs=[VM] * 7 + [ANY],
+        out_specs=[ANY] * 7 + [VM] * 3,
+        scratch_shapes=[
+            pltpu.VMEM((S, tok, D), BF), pltpu.VMEM((D, 3 * hw), BF), pltpu.VMEM((D, D), BF),
+            pltpu.VMEM((2, hp, total, HEAD), F32), pltpu.VMEM((3, hp, total, 2 * HEAD), BF),
+            pltpu.VMEM((hp, total, 2 * HEAD), F32), pltpu.VMEM((S, tok, total // 2), F32),
+            pltpu.VMEM((hp, tok, HEAD), BF), pltpu.VMEM((S, tok, hw), BF), pltpu.VMEM((tok, D), BF),
+            pltpu.VMEM((S, tok, hw), BF),
+            dma(S), dma(S), dma(S), dma(S), dma(F1), dma(F1), dma(F1), dma(F1), dma(F1), dma(F1),
+            dma(F1), dma(F1), dma(F1), dma(F1), dma(F1), dma(F1), dma(S), dma(S), dma(6),
+        ],
+        compiler_params=pltpu.CompilerParams(collective_id=1, has_side_effects=True, vmem_limit_bytes=60 * 2**20),
+        name="first",
+    )(x, seg.reshape(total, 1), seg.reshape(1, total), wqkv, wout, gain, alpha.reshape(1, D), wup)
+
+
 def gather(x, axes, dim=0):
     return lax.all_gather(x, axes, axis=dim, tiled=True)
 
 
 def scatter(x, axes, dim=0):
     return lax.psum_scatter(x, axes, scatter_dimension=dim, tiled=True)
-
-
-def attention(q, k, v, seg):
-    n = seg.shape[0]
-    pos = jnp.arange(n, dtype=jnp.int32)
-    allowed = (pos[None, :] <= pos[:, None]) & ((seg[None, :] == 0) | (seg[None, :] == seg[:, None]))
-    scores = jnp.einsum("qhe,khe->hqk", q, k, preferred_element_type=F32) * HEAD**-0.5
-    scores = jnp.where(allowed[None], scores, neg_big)
-    top = jnp.max(scores, axis=-1, keepdims=True)
-    e = jnp.exp(scores - top)
-    probs = e / jnp.sum(e, axis=-1, keepdims=True)
-    mix = jnp.einsum("hqk,khe->qhe", probs.astype(BF), v, preferred_element_type=F32)
-    return mix, probs
 
 
 def attention_back(q, k, v, probs, gx):
@@ -81,26 +346,24 @@
     tok = x.shape[0]
     inv_x = inv_rms(x)
     h = x * inv_x
-    hb = h.astype(BF)
     seg = segments[0]
-    h_all = gather(hb, "seq")
-    total = h_all.shape[0]
-    wq = head_pad(w_qkv.reshape(rows, 3, D)).reshape(rows, 3, S, hw)
-    wq = lax.dynamic_index_in_dim(wq, z, 2, keepdims=False)
-    wq = gather(wq.reshape(rows, 3 * hw), "fsdp")
-    wo = gather(w_out, "fsdp")
-    wu = lax.all_to_all(w_upgate.reshape(rows, 2, FS, fl), "fsdp", split_axis=2, concat_axis=0, tiled=True)
-    wu = wu.reshape(D, 2 * fl)
+    total = seg.shape[0]
     gain = lax.dynamic_slice_in_dim(head_pad(s_qk), z * hw, hw).reshape(hp, HEAD)
-    qkv = mm(h_all, wq).reshape(total, 3, hp, HEAD)
-    inv_qk = inv_rms(qkv[:, :2])
-    u_qk = qkv[:, :2] * inv_qk
-    n_qk = (u_qk * gain).astype(BF)
-    q, k, v = n_qk[:, 0], n_qk[:, 1], qkv[:, 2].astype(BF)
-    mix, probs = attention(q, k, v, seg)
-    mixb = mix.reshape(total, hw).astype(BF)
-    mine = lax.all_to_all(mixb, "seq", split_axis=0, concat_axis=1, tiled=True)[:, :D]
-    attn = mm(mine, wo)
+    h_all, wq, wo, wu4, raw, qkv, res, mine, attn, _ = first(
+        S, FS, hp, inputs[0], seg, w_qkv, w_out, gain, alpha_attn, w_upgate
+    )
+    h_all = h_all.reshape(total, D)
+    own = lax.dynamic_slice_in_dim(w_upgate.reshape(rows, 2, ff), f * fl, fl, 2).transpose(1, 0, 2)
+    wu4 = lax.dynamic_update_slice(wu4, own[:, None], (0, f, 0, 0))
+    wu = wu4.transpose(1, 2, 0, 3).reshape(D, 2 * fl)
+    rawt = raw.transpose(2, 0, 1, 3)
+    inv_qk = inv_rms(rawt)
+    u_qk = rawt * inv_qk
+    q, k, v = [qkv[c, :, :, :HEAD].transpose(1, 0, 2) for c in range(3)]
+    pos = jnp.arange(total, dtype=jnp.int32)
+    allowed = (pos[None, :] <= pos[:, None]) & ((seg[None, :] == 0) | (seg[None, :] == seg[:, None]))
+    probs = jnp.einsum("qhe,khe->hqk", q, k, preferred_element_type=F32) * HEAD**-0.5
+    probs = jnp.exp(jnp.where(allowed[None], probs, neg_big)) * res[:, :, HEAD : HEAD + 1]
     inv_a = inv_rms(attn)
     ua = attn * inv_a
     n = h + alpha_attn * (ua - h)

time: 1060 us -> 931 us (0.88)
  waiting for transfers between devices: 635 us -> 434 us
  Pallas kernels: 0 us -> 90.5 us
  blocking collectives: 62.9 us -> 41.3 us
  matrix products: 131 us -> 117 us
  other arithmetic: 53.1 us -> 64.3 us
    all_gather x8 -> x5, waiting for transfers between devices: 271 us -> 180 us  [gather(): return lax.all_gather(x, axes, axis=dim, tiled=True)]
    pallas_call x0 -> x1, Pallas kernels: none -> 90.5 us  [first(): pl.pallas_call(lambda *refs: first_kernel(S, FS, hp, *refs), out_shape=ou...]
    all_to_all x2 -> x1, waiting for transfers between devices: 85.3 us -> 1.78 us  [body(): lax.all_to_all(gmix, 'seq', split_axis=1, concat_axis=0, tiled=True)]
    transpose x0 -> x1, local copies, waits for them, and re-layouts: none -> 27.5 us  [body(): wu = wu4.transpose(1, 2, 0, 3).reshape(D, 2 * fl)]
    all_to_all x1 -> x0, blocking collectives: 21.6 us -> none  [body(): lax.all_to_all(gmix, 'seq', split_axis=1, concat_axis=0, tiled=True)]
    reshape x4 -> x2, local copies, waits for them, and re-layouts: 30 us -> 11.2 us  [the longest x1 10.5 us: body(): w_upgate.reshape(rows, 2, ff)]
    unnamed x18 -> x15, waiting for transfers between devices: 18 us -> 2.01 us
    sub x1 -> x0, matrix products: 13.2 us -> none  [attention(): e = jnp.exp(scores - top)]
  transfers between devices with their start and end apart: 20 -> 16, of which waited for: 15 -> 13; matrix products, arithmetic and copies ran while one was open for 19% -> 23% of each run, Pallas kernels for 0% -> 0%
where the time goes in v2:
time: 931 us; the launch traced here: 923 us
  waiting for transfers between devices  434 us (47%)
  local copies, waits for them, and re-layouts  150 us (16%)
  matrix products  117 us (13%)
  Pallas kernels  90.5 us (10%)
  other arithmetic  64.3 us (7%)
  blocking collectives  41.3 us (4%)
  between operations  14.9 us (2%)
  starting transfers between devices  10.3 us (1%)
    all_gather x5, waiting for transfers between devices, gather(): return lax.all_gather(x, axes, axis=dim, tiled=True)  180 us
    reduce_scatter x6, waiting for transfers between devices, scatter(): return lax.psum_scatter(x, axes, scatter_dimension=dim, tiled=True)  133 us
    psum x1, waiting for transfers between devices, body(): d_o = lax.psum(d_o, ('grp', 'seq')).astype(F32)  94.7 us
    pallas_call x1, Pallas kernels, first(): pl.pallas_call(lambda *refs: first_kernel(S, FS, hp, *refs), out_shape=ou...  90.5 us
    convert_element_type x3, local copies, waits for them, and re-layouts, body(): d_up.reshape(rows, FS, 2, fl).transpose(0, 2, 1, 3).reshape(rows, 2 * ff)  44.6 us
    psum x1, blocking collectives, body(): lax.psum(jnp.concatenate([slot_qk, d_alpha_attn, d_alpha_mlp, slot]), ('g...  41.3 us
    dot_general x4, matrix products, mm_nt(): lax.dot_general(a, b, (((1,), (1,)), ((), ())), preferred_element_type=F32)  28.7 us
    unnamed x64, local copies, waits for them, and re-layouts  28.7 us
  transfers between devices with their start and end apart: 16, of which 13 were waited for; matrix products, arithmetic and copies ran while one was open for 23% of the time, Pallas kernels for 0%

profile of v2, /device:TPU:0, one launch (start us, length us, event | category | flops | bytes accessed | tf_op | source)
XLA Modules:
  0.0 922.8 jit_solution(5651320587727848156)
XLA Ops:
  13.2 90.5 %first.1 = (bf16[4,256,1280]{2,1,0:T(8,128)(2,1)}, bf16[1280,960]{1,0:T(8,128)(2,1)}, bf16[1280,1280]{1,0:T(8,128)(2,1)}, bf16[2,4,320,1280]{3,2,1,0:T(8,128)(2,...) custom-call(bf16[256,1280]{1,0:T(8,128)(2,1)} %bitcast.115, ...), custom_call_target="tpu_custom_call" | custom-call | tf_op jit(solution)/shard_map/first/pallas_call | solution.py:295
  109.2 10.5 %reshape.217 = bf16[320,2,5120]{2,1,0:T(2,128)(2,1)} reshape(bf16[320,10240]{1,0:T(8,128)(2,1)} %refs_7_.1) | data formatting | bytes 13107200 | tf_op jit(solution)/shard_map/reshape | solution.py:356
  123.6 27.5 %copy.102 = bf16[4,320,2,1280]{3,2,1,0:T(2,128)(2,1)S(1)} copy(bf16[4,320,2,1280]{3,1,0,2:T(8,128)(2,1)} %bitcast.119) | data formatting | bytes 13107200 | tf_op jit(solution)/shard_map/transpose | solution.py:358
  156.8 9.9 %fusion.51 = f32[1024,2560]{1,0:T(8,128)S(1)} fusion(bf16[1024,1280]{1,0:T(8,128)(2,1)} %all-gather.6.cloned.1.call-done, bf16[1280,2560]{1,0:T(8,128)(2,1)} %bitcast.117), kind=kOutput, calls=%fused_computation.118 | convolution fusion | flops 6710886400 | bytes 19660800 | tf_op jit(solution)/shard_map/dot_general | solution.py:30
  177.4 36.3 %reduce-scatter.10.cloned.1.call-done = bf16[256,1280]{1,0:T(8,128)(2,1)} async-done(((bf16[1024,1280]{1,0:T(8,128)(2,1)}), bf16[256,1280]{1,0:T(8,128)(2,1)}) %reduce-scatter.10.cloned.1.call-update) | async-done | bytes 655376 | tf_op jit(solution)/shard_map/reduce_scatter | solution.py:319
  221.2 39.6 %all-gather.8.cloned.1.call-done = bf16[1024,1280]{1,0:T(8,128)(2,1)} async-done(((bf16[256,1280]{1,0:T(8,128)(2,1)}), bf16[1024,1280]{1,0:T(8,128)(2,1)}) %all-gather.8.cloned.1.call-update) | async-done | bytes 2621456 | tf_op jit(solution)/shard_map/all_gather | solution.py:315
  260.8 9.8 %multiply_reduce_fusion.2 = (f32[1280]{0:T(1024)S(1)}, f32[1280]{0:T(1024)S(1)}, f32[1024,1280]{1,0:T(8,128)S(1)}, bf16[1024,1280]{1,0:T(8,128)(2,1)S(1)}) fusion(f32[1024,2560]{1,0:T(8,128)} %copy-done.11, f32[1280]{0:T(1024)S(1)} %dynamic_slice.30, f32[1280]{0:T(1024)S(1)} %dynamic_slice.29, bf16[1024,1280]{1,0:T(8,128)(2,1)} %all-gather.8.cloned.1.call-done, ...), kind=kOutput, calls=%fused_computation.16 | convolution fusion | flops 3380344320 | bytes 24268800 | tf_op jit(solution)/shard_map/dot_general | solution.py:34
  272.1 11.1 %convolution_convert_fusion.5 = bf16[1024,1280]{1,0:T(8,128)(2,1)} fusion(bf16[1280,2560]{1,0:T(8,128)(2,1)} %bitcast.118, bf16[1024,1280]{1,0:T(8,128)(2,1)S(1)} %multiply_convert_fusion.1, bf16[1024,1280]{1,0:T(8,128)(2,1)S(1)} %get-tuple-element.91), kind=kOutput, calls=%fused_computation.32 | convolution fusion | flops 6722682880 | bytes 14417920 | tf_op jit(solution)/shard_map/dot_general | solution.py:34
  283.5 11.1 %convolution_convert_fusion = bf16[1280,2560]{1,0:T(8,128)(2,1)} fusion(bf16[1024,1280]{1,0:T(8,128)(2,1)} %all-gather.6.cloned.1.call-done, bf16[1024,1280]{1,0:T(8,128)(2,1)S(1)} %multiply_convert_fusion.1, bf16[1024,1280]{1,0:T(8,128)(2,1)} %copy-done.27), kind=kOutput, calls=%fused_computation.3 | convolution fusion | flops 6724648960 | bytes 14417920 | tf_op jit(solution)/shard_map/dot_general | solution.py:38
  301.9 21.0 %reduce-scatter.12.cloned.1.call-done = bf16[256,1280]{1,0:T(8,128)(2,1)} async-done(((bf16[1024,1280]{1,0:T(8,128)(2,1)}), bf16[256,1280]{1,0:T(8,128)(2,1)}) %reduce-scatter.12.cloned.1.call-update) | async-done | bytes 655376 | tf_op jit(solution)/shard_map/reduce_scatter | solution.py:319
  340.1 11.6 %fusion.33 = f32[5,1024,1024]{1,2,0:T(8,128)} fusion(bf16[3,5,1024,128]{3,2,1,0:T(8,128)(2,1)} %get-tuple-element.22), kind=kOutput, calls=%fused_computation.70 | convolution fusion | flops 671088640 | bytes 23592960 | tf_op jit(solution)/shard_map/qhe,khe->hqk/dot_general | solution.py:365
  358.3 14.5 %multiply_reduce_fusion = (f32[5,1024]{1,0:T(8,128)S(1)}, f32[5,1024,1024]{1,2,0:T(8,128)}) fusion(f32[5,1024,1024]{1,2,0:T(8,128)} %fusion.33, f32[5,1024]{1,0:T(8,128)S(1)} %slice_reduce_fusion, pred[1024,1024]{0,1:T(8,128)(4,1)S(1)} %copy-done.12, bf16[1024,5,64]{0,2,1:T(8,128)(2,1)} %reshape.219, bf16[3,5,1024,128]{3,2,1,0:T(8,128)(2,1)} %get-tuple-element.22), kind=kOutput, calls=%fused_computation.1 | convolution fusion | flops 697297920 | bytes 44998656 | tf_op jit(solution)/shard_map/qhe,khe->hqk/dot_general | solution.py:323
  378.7 15.4 %multiply_convert_fusion = bf16[5,1024,1024]{1,2,0:T(8,128)(2,1)S(1)} fusion(f32[5,1024,1024]{1,2,0:T(8,128)} %get-tuple-element.99, f32[5,1024,1024]{1,2,0:T(8,128)} %fusion.33, f32[5,1024]{1,0:T(8,128)S(1)} %get-tuple-element.98, f32[5,1024]{1,0:T(8,128)S(1)} %slice_reduce_fusion, pred[1024,1024]{0,1:T(8,128)(4,1)S(1)} %copy-done.12), kind=kLoop, calls=%fused_computation | loop fusion | flops 31457280 | bytes 53518336 | tf_op jit(solution)/shard_map/convert_element_type | solution.py:325
  410.2 9.6 %fusion.7 = bf16[1024,1,5,64]{3,0,2,1:T(8,128)(2,1)S(1)} fusion(bf16[1024,5,64]{0,2,1:T(8,128)(2,1)S(1)} %copy-done.19, f32[5,1024,1024]{1,2,0:T(8,128)} %fusion.33, f32[5,1024]{1,0:T(8,128)S(1)} %slice_reduce_fusion, pred[1024,1024]{0,1:T(8,128)(4,1)S(1)} %copy-done.12), kind=kOutput, calls=%fused_computation.39 | convolution fusion | flops 692060160 | bytes 23351296 | tf_op jit(solution)/shard_map/hqk,qhe->khe/dot_general | solution.py:328
  446.8 43.1 %reduce-scatter.16.cloned.1.call-done = bf16[320,960]{1,0:T(8,128)(2,1)} async-done(((bf16[1280,960]{1,0:T(8,128)(2,1)}), bf16[320,960]{1,0:T(8,128)(2,1)}) %reduce-scatter.16.cloned.1.call-update) | async-done | bytes 614416 | tf_op jit(solution)/shard_map/reduce_scatter | solution.py:319
  509.0 29.5 %reduce-scatter.18.cloned.1.call-done = bf16[320,1280]{1,0:T(8,128)(2,1)} async-done(((bf16[1280,1280]{1,0:T(8,128)(2,1)}), bf16[320,1280]{1,0:T(8,128)(2,1)}) %reduce-scatter.18.cloned.1.call-update) | async-done | bytes 819216 | tf_op jit(solution)/shard_map/reduce_scatter | solution.py:319
  538.6 21.8 %all-reduce.4.cloned.1.call-done = bf16[320,3,320]{0,2,1:T(8,128)(2,1)} async-done(((bf16[320,3,320]{0,2,1:T(8,128)(2,1)}), bf16[320,3,320]{0,2,1:T(8,128)(2,1)}) %all-reduce.4.cloned.1.call-update) | async-done | bytes 614416 | tf_op jit(solution)/shard_map/psum | solution.py:431
  560.5 79.6 %all-gather.12.cloned.1.call-done = bf16[320,4,1280]{0,1,2:T(4,128)(2,1)} async-done(((bf16[320,4,320]{0,1,2:T(4,128)(2,1)}), bf16[320,4,1280]{0,1,2:T(4,128)(2,1)}) %all-gather.12.cloned.1.call-update) | async-done | bytes 3276816 | tf_op jit(solution)/shard_map/all_gather | solution.py:315
  648.4 41.3 %psum.31 = f32[14080]{0:T(1024)S(1)} all-reduce(f32[14080]{0:T(1024)S(1)} %pad_maximum_fusion.4), channel_id=1, replica_groups=mesh['grp'=2,'seq'=4,'fsdp'=4] {'grp','seq','fsdp'}, use_global_device_ids=true, to_apply=%region_28.29 | all-reduce | flops 14080 | bytes 112640 | tf_op jit(solution)/shard_map/psum | solution.py:436
  697.6 94.7 %all-reduce.6.cloned.1.call-done = (bf16[320,1280]{1,0:T(8,128)(2,1)}, bf16[1280,1280]{1,0:T(8,128)(2,1)}) async-done(((bf16[320,1280]{1,0:T(8,128)(2,1)}, bf16[1280,1280]{1,0:T(8,128)(2,1)}), (bf16[320,1280]{1,0:T(8,128)(2,1)}, bf16[1280,1280]{1,0:T(8,128)(2,1)})) %all-reduce.6.cloned.1.call-update) | async-done | bytes 4096016 | tf_op jit(solution)/shard_map/psum | solution.py:429
  798.9 55.1 %all-gather.10.cloned.1.call-done = bf16[320,3,1280]{0,2,1:T(8,128)(2,1)} async-done(((bf16[320,3,320]{0,2,1:T(8,128)(2,1)}), bf16[320,3,1280]{0,2,1:T(8,128)(2,1)}) %all-gather.10.cloned.1.call-update) | async-done | bytes 2457616 | tf_op jit(solution)/shard_map/all_gather | solution.py:315
  871.2 15.1 %reshape.227 = f32[320,4,2,1280]{3,2,0,1:T(2,128)} reshape(bf16[320,4,2560]{2,0,1:T(8,128)(2,1)} %all-gather.14.cloned.1.call-done) | data formatting | bytes 19660800 | tf_op jit(solution)/shard_map/convert_element_type | solution.py:427
  886.4 13.9 %copy.123 = f32[320,2,4,1280]{3,2,1,0:T(4,128)} copy(f32[320,2,4,1280]{3,1,0,2:T(2,128)} %bitcast.111) | data formatting | bytes 26214400 | tf_op jit(solution)/shard_map/convert_element_type | solution.py:427
  900.3 15.5 %reshape.226 = f32[320,10240]{1,0:T(8,128)} reshape(f32[320,2,4,1280]{3,2,1,0:T(4,128)} %copy.123) | data formatting | bytes 26214400 | tf_op jit(solution)/shard_map/convert_element_type | solution.py:427
  (178 shorter events, 179.8 us)
Async XLA Ops:
  7.2 165.1 %copy-start = (bf16[1280,1280]{1,0:T(8,128)(2,1)S(1)}, bf16[1280,1280]{1,0:T(8,128)(2,1)}, u32[]{:S(2)}) copy-start(bf16[1280,1280]{1,0:T(8,128)(2,1)} %param.17) | copy-start | bytes 9830404
  7.2 149.6 %all-gather.6.cloned.1.call-start = ((), (), s32[]{:S(2)}) async-start(), calls=%async_computation.9 | async-start | bytes 3276800 | tf_op jit(solution)/shard_map/all_gather | solution.py:315
  13.1 92.0 %copy-start.4 = (bf16[1,256,1280]{2,1,0:T(8,128)(2,1)S(1)}, bf16[1,256,1280]{2,1,0:T(8,128)(2,1)}, u32[]{:S(2)}) copy-start(bf16[1,256,1280]{2,1,0:T(8,128)(2,1)} %param.12) | copy-start | bytes 1966084
  13.1 92.0 %copy-start.22 = (f32[1280]{0:T(1024)S(1)}, f32[1280]{0:T(1024)}, u32[]{:S(2)}) copy-start(f32[1280]{0:T(1024)} %param.19) | copy-start | bytes 15364
  109.0 104.7 %reduce-scatter.10.cloned.1.call-start = ((), (), s32[]{:S(2)}) async-start(), calls=%async_computation.10 | async-start | bytes 3276800 | tf_op jit(solution)/shard_map/reduce_scatter | solution.py:319
  177.1 38.0 %copy-start.23 = (f32[1280]{0:T(1024)S(1)}, f32[1280]{0:T(1024)}, u32[]{:S(2)}) copy-start(f32[1280]{0:T(1024)} %param.20) | copy-start | bytes 15364
  177.1 83.7 %all-gather.8.cloned.1.call-start = ((), (), s32[]{:S(2)}) async-start(), calls=%async_computation.11 | async-start | bytes 3276800 | tf_op jit(solution)/shard_map/all_gather | solution.py:315
  221.1 101.8 %reduce-scatter.12.cloned.1.call-start = ((), (), s32[]{:S(2)}) async-start(), calls=%async_computation.12 | async-start | bytes 3276800 | tf_op jit(solution)/shard_map/reduce_scatter | solution.py:319
  283.2 89.6 %reduce-scatter.20.cloned.1.call-start = ((), (), s32[]{:S(2)}) async-start(), calls=%async_computation.18 | async-start | bytes 9830400 | tf_op jit(solution)/shard_map/reduce_scatter | solution.py:319
  295.3 27.6 %copy-start.3 = (f32[256,1280]{1,0:T(8,128)S(1)}, f32[256,1280]{1,0:T(8,128)}, u32[]{:S(2)}) copy-start(f32[256,1280]{1,0:T(8,128)} %copy-done.2) | copy-start | bytes 3932164
  295.3 27.6 %copy-start.8 = (f32[256,1280]{1,0:T(8,128)S(1)}, f32[256,1280]{1,0:T(8,128)}, u32[]{:S(2)}) copy-start(f32[256,1280]{1,0:T(8,128)} %copy-done.7) | copy-start | bytes 3932164
  299.6 25.4 %copy-start.5 = (bf16[1,256,1280]{2,1,0:T(8,128)(2,1)S(1)}, bf16[1,256,1280]{2,1,0:T(8,128)(2,1)}, u32[]{:S(2)}) copy-start(bf16[1,256,1280]{2,1,0:T(8,128)(2,1)} %param.12) | copy-start | bytes 1966084
  331.6 21.8 %all-to-all-start = ((bf16[256,4,320]{0,2,1:T(8,128)(2,1)}), bf16[256,4,320]{0,2,1:T(8,128)(2,1)}, u32[]{:S(2)}, u32[]{:S(2)}) async-start(bf16[256,4,320]{0,2,1:T(8,128)(2,1)} %bitcast.14), calls=%async_computation.2 | async-start | bytes 1310720 | tf_op jit(solution)/shard_map/all_to_all | solution.py:411
  336.2 104.0 %reduce-scatter.22.cloned.1.call-start = ((), (), s32[]{:S(2)}) async-start(), calls=%async_computation.21 | async-start | bytes 4096000
  378.5 111.4 %reduce-scatter.16.cloned.1.call-start = ((), (), s32[]{:S(2)}) async-start(), calls=%async_computation.14 | async-start | bytes 3276800 | tf_op jit(solution)/shard_map/reduce_scatter | solution.py:319
  434.4 104.2 %reduce-scatter.18.cloned.1.call-start = ((), (), s32[]{:S(2)}) async-start(), calls=%async_computation.17 | async-start | bytes 4096000 | tf_op jit(solution)/shard_map/reduce_scatter | solution.py:319
  443.1 49.1 %all-to-all-start.1 = ((bf16[4,320,320]{1,2,0:T(8,128)(2,1)}), bf16[4,320,320]{1,2,0:T(8,128)(2,1)S(1)}, u32[]{:S(2)}, u32[]{:S(2)}) async-start(bf16[4,320,320]{1,2,0:T(8,128)(2,1)} %copy.120), calls=%async_computation.7 | async-start | bytes 1966080 | tf_op jit(solution)/shard_map/all_to_all | solution.py:425
  446.8 113.6 %all-reduce.4.cloned.1.call-start = ((), (), s32[]{:S(2)}) async-start(), calls=%async_computation.15 | async-start | bytes 1474560 | tf_op jit(solution)/shard_map/psum | solution.py:431
  492.1 147.9 %all-gather.12.cloned.1.call-start = ((), (), s32[]{:S(2)}) async-start(), calls=%async_computation.19 | async-start | bytes 4915200 | tf_op jit(solution)/shard_map/all_gather | solution.py:315
  493.9 200.7 %reduce-scatter.14.cloned.1.call-start = ((), (), s32[]{:S(2)}) async-start(), calls=%async_computation.13 | async-start | bytes 3276800 | tf_op jit(solution)/shard_map/reduce_scatter | solution.py:319
  500.8 291.5 %all-reduce.6.cloned.1.call-start = ((), (), s32[]{:S(2)}) async-start(), calls=%async_computation.22 | async-start | bytes 8192000 | tf_op jit(solution)/shard_map/psum | solution.py:429
  538.5 315.4 %all-gather.10.cloned.1.call-start = ((), (), s32[]{:S(2)}) async-start(), calls=%async_computation.16 | async-start | bytes 3686400 | tf_op jit(solution)/shard_map/all_gather | solution.py:315
  560.4 310.8 %all-gather.14.cloned.1.call-start = ((), (), s32[]{:S(2)}) async-start(), calls=%async_computation.20 | async-start | bytes 9830400 | tf_op jit(solution)/shard_map/all_gather | solution.py:315
  900.3 15.5 %copy-start.1 = (bf16[1280,1280]{1,0:T(8,128)(2,1)S(1)}, bf16[1280,1280]{1,0:T(8,128)(2,1)}, u32[]{:S(2)}) copy-start(bf16[1280,1280]{1,0:T(8,128)(2,1)} %param.17) | copy-start | bytes 9830404
  (22 other events, 64.7 us)
Sparse Core Ops, SparseCore 0:
  109.1 36.2 all-gather.5
  177.2 36.3 reduce-scatter.9
  221.2 39.5 all-gather.7
  283.3 39.5 reduce-scatter.11
  325.6 14.0 reduce-scatter.19
  378.6 61.5 reduce-scatter.21
  443.8 46.0 reduce-scatter.15
  493.5 44.9 reduce-scatter.17
  541.5 18.8 all-reduce.3
  562.4 77.6 all-gather.11
  642.9 51.6 reduce-scatter.13
  697.6 94.7 all-reduce.5
  793.9 60.0 all-gather.9
  855.4 15.8 all-gather.13

commit v3 on v2

--- a/solution.py
+++ b/solution.py
@@ -59,13 +59,22 @@
     return (ki <= qi) & ((seg_row == 0) | (seg_row == seg_col))
 
 
+def add_into(dst, src, chunk):
+    def one(i, carry):
+        at = ds(i * chunk, chunk, 16)
+        dst[at] = (dst[at].astype(F32) + src[at].astype(F32)).astype(dst.dtype)
+        return carry
+
+    lax.fori_loop(0, src.shape[0] // chunk, one, 0)
+
+
 def attn_bias(S, tok, half, bias, segc, segr):
     for qb in range(S):
         q0 = qb * tok
         k0 = q0 if q0 < half else half
         nk = q0 + tok - k0
         ok = visible(segc[q0 : q0 + tok], segr[:, k0 : k0 + nk], q0, k0, tok, nk)
-        bias[qb, :, :nk] = jnp.where(ok, 0.0, neg_big)
+        bias[qb, :, :nk] = jnp.where(ok, 0.0, neg_big).astype(BF)
 
 
 def first_kernel(S, FS, hp, x_ref, segc, segr, wqkv, wout, gain, alpha, wup,
@@ -204,7 +213,7 @@
         def head(j, carry):
             q = qkv[0, j, q0:n, :HEAD] * jnp.asarray(HEAD**-0.5, BF)
             s = mm_nt(q, qkv[1, j, :n, :HEAD])
-            tail = s[:, k0:] + bias[qb, :, : n - k0]
+            tail = s[:, k0:] + bias[qb, :, : n - k0].astype(F32)
             e = jnp.exp(jnp.concatenate([s[:, :k0], tail], axis=1) if k0 else tail)
             o = mm(e.astype(BF), qkv[2, j, :n])
             rinv = 1.0 / o[:, HEAD : HEAD + 1]
@@ -253,7 +262,7 @@
     x = x_ref[...].astype(F32)
     h = x * inv_rms(x)
     n_ = h + alpha[...] * (attn * inv_rms(attn) - h)
-    mid_o[...] = (n_ * inv_rms(n_)).astype(BF)
+    mid_o[...] = n_ * inv_rms(n_)
 
     for t in range(S - 1):
         @pl.when((z + 1 < S) & (z - t >= 0))
@@ -288,7 +297,7 @@
     outs = [
         sds((S, tok, D), BF), sds((D, 3 * hw), BF), sds((D, D), BF), sds((2, FS, rows, fl), BF),
         sds((2, hp, total, HEAD), F32), sds((3, hp, total, 2 * HEAD), BF), sds((hp, total, 2 * HEAD), F32),
-        sds((tok, D), BF), sds((tok, D), F32), sds((tok, D), BF),
+        sds((tok, D), BF), sds((tok, D), F32), sds((tok, D), F32),
     ]
     dma = lambda n: pltpu.SemaphoreType.DMA((n,))
     F1 = FS - 1
@@ -300,7 +309,7 @@
         scratch_shapes=[
             pltpu.VMEM((S, tok, D), BF), pltpu.VMEM((D, 3 * hw), BF), pltpu.VMEM((D, D), BF),
             pltpu.VMEM((2, hp, total, HEAD), F32), pltpu.VMEM((3, hp, total, 2 * HEAD), BF),
-            pltpu.VMEM((hp, total, 2 * HEAD), F32), pltpu.VMEM((S, tok, total // 2), F32),
+            pltpu.VMEM((hp, total, 2 * HEAD), F32), pltpu.VMEM((S, tok, total // 2), BF),
             pltpu.VMEM((hp, tok, HEAD), BF), pltpu.VMEM((S, tok, hw), BF), pltpu.VMEM((tok, D), BF),
             pltpu.VMEM((S, tok, hw), BF),
             dma(S), dma(S), dma(S), dma(S), dma(F1), dma(F1), dma(F1), dma(F1), dma(F1), dma(F1),
@@ -311,22 +320,664 @@
     )(x, seg.reshape(total, 1), seg.reshape(1, total), wqkv, wout, gain, alpha.reshape(1, D), wup)
 
 
-def gather(x, axes, dim=0):
-    return lax.all_gather(x, axes, axis=dim, tiled=True)
-
-
-def scatter(x, axes, dim=0):
-    return lax.psum_scatter(x, axes, scatter_dimension=dim, tiled=True)
-
-
-def attention_back(q, k, v, probs, gx):
-    gp = jnp.einsum("qhe,khe->hqk", gx, v, preferred_element_type=F32)
-    delta = jnp.sum(probs * gp, axis=-1, keepdims=True)
-    gs = (probs * (gp - delta)).astype(BF)
-    dq = jnp.einsum("hqk,khe->qhe", gs, k, preferred_element_type=F32) * HEAD**-0.5
-    dk = jnp.einsum("hqk,qhe->khe", gs, q, preferred_element_type=F32) * HEAD**-0.5
-    dv = jnp.einsum("hqk,qhe->khe", probs.astype(BF), gx, preferred_element_type=F32)
-    return dq, dk, dv
+def second_kernel(S, FS, NC, mid, cot, wd, su, sg, alpha, wu_i, wup,
+                  out_o, gmid_o, du_o, dd_o, dal_o, dsu_o, dsg_o,
+                  wu, mida, up, gate, hid, ps, pr, gma, gu, dup, ddn, lu, ld,
+                  s_a, r_a, s_b, r_b, s_c, r_c, s_d, r_d, w_sem, s_x, r_x, out_sem):
+    g, z, f = lax.axis_index("grp"), lax.axis_index("seq"), lax.axis_index("fsdp")
+    tok = mid.shape[0]
+    ct = tok // NC
+    fl = wd.shape[0]
+    ff = wup.shape[1] // 2
+    rows = wup.shape[0]
+    hl = fl // 2
+    nt = 256 if fl % 256 == 0 else 128
+    M = FS * ct
+    peers = [lax.rem(f + i, FS) for i in range(1, FS)]
+    bpeers = [lax.rem(f + FS - i, FS) for i in range(1, FS)]
+    partner = (1 - g, z, f)
+    greet([(g, z, p) for p in peers] + [partner])
+
+    def gather_copy(buf, ss, rs, c, i):
+        return rcopy(buf.at[c, f], buf.at[c, f], ss.at[c, i], rs.at[c, i], (g, z, peers[i]))
+
+    def send_partial(ss, rs, c, i):
+        return rcopy(ps.at[c, peers[i]], pr.at[c, i], ss.at[c, i], rs.at[c, i], (g, z, peers[i]))
+
+    R = range(FS - 1)
+    for c in range(NC):
+        mida[c, f] = mid[c * ct : (c + 1) * ct].astype(BF)
+        for i in R:
+            gather_copy(mida, s_a, r_a, c, i).start()
+    loads = []
+    for k in range(2):
+        loads.append(pltpu.make_async_copy(wup.at[:, ds(k * ff + f * fl, fl, 128)], wu.at[k, ds(f * rows, rows, 16)], w_sem.at[k, 0]))
+        for i in R:
+            loads.append(pltpu.make_async_copy(wu_i.at[k, peers[i]], wu.at[k, ds(peers[i] * rows, rows, 16)], w_sem.at[k, i + 1]))
+    for c in loads:
+        c.start()
+    dsu_o[...] = jnp.zeros_like(dsu_o)
+    dsg_o[...] = jnp.zeros_like(dsg_o)
+    dal_o[...] = jnp.zeros_like(dal_o)
+    for c in loads:
+        c.wait()
+
+    for c in range(NC):
+        for i in R:
+            gather_copy(mida, s_a, r_a, c, i).wait_recv()
+
+        def fwd(t, carry):
+            cols = ds(t * nt, nt, 128)
+            a_in = mida[c].reshape(M, D)
+            u = mm(a_in, wu[0, :, cols])
+            gt = mm(a_in, wu[1, :, cols])
+            up[c, :, cols] = u
+            gate[c, :, cols] = gt
+            a = gt * sg[:, cols]
+            hid[c, :, cols] = (u * su[:, cols] * (a * jax.nn.sigmoid(a))).astype(BF)
+            return carry
+
+        lax.fori_loop(0, fl // nt, fwd, 0)
+
+        def proj(t, carry):
+            cols = ds(t * 256, 256, 128)
+            ps[c, :, :, cols] = mm(hid[c], wd[:, cols]).astype(BF).reshape(FS, ct, 256)
+            return carry
+
+        lax.fori_loop(0, D // 256, proj, 0)
+        for i in R:
+            send_partial(s_b, r_b, c, i).start()
+
+    for c in range(NC):
+        at = slice(c * ct, (c + 1) * ct)
+        for i in R:
+            send_partial(s_b, r_b, c, i).wait_recv()
+        mlp = ps[c, f].astype(F32)
+        for i in R:
+            mlp = mlp + pr[c, i].astype(F32)
+        al = alpha[...]
+        md = mid[at]
+        inv_m = inv_rms(mlp)
+        um = mlp * inv_m
+        dif = um - md
+        m = md + al * dif
+        inv_o = inv_rms(m)
+        o = m * inv_o
+        out_o[at] = o.astype(BF)
+        g_m = back(o, inv_o, cot[at].astype(F32))
+        dal_o[...] += jnp.sum(g_m * dif, axis=0, keepdims=True)
+        gmid_o[at] = (1 - al) * g_m
+        gma[c, f] = back(um, inv_m, al * g_m).astype(BF)
+        for i in R:
+            gather_copy(gma, s_c, r_c, c, i).start()
+
+    for c in range(NC):
+        for i in R:
+            gather_copy(gma, s_c, r_c, c, i).wait_recv()
+
+        def bwd(t, carry):
+            cols = ds(t * nt, nt, 128)
+            gh = mm_nt(gma[c].reshape(M, D), wd[cols, :])
+            u = up[c, :, cols]
+            gt = gate[c, :, cols]
+            sgc = sg[:, cols]
+            suc = su[:, cols]
+            a = gt * sgc
+            sig = jax.nn.sigmoid(a)
+            gs = gh * (a * sig)
+            gu[0, c, :, cols] = (gs * suc).astype(BF)
+            dsu_o[:, cols] += jnp.sum(u * gs, axis=0, keepdims=True)
+            g_a = gh * u * suc * (sig * (1 + a * (1 - sig)))
+            gu[1, c, :, cols] = (g_a * sgc).astype(BF)
+            dsg_o[:, cols] += jnp.sum(gt * g_a, axis=0, keepdims=True)
+            return carry
+
+        lax.fori_loop(0, fl // nt, bwd, 0)
+        for i in R:
+            send_partial(s_b, r_b, c, i).wait_send()
+
+        def bproj(t, carry):
+            cols = ds(t * 256, 256, 128)
+            v = mm_nt(gu[0, c], wu[0, cols, :]) + mm_nt(gu[1, c], wu[1, cols, :])
+            ps[c, :, :, cols] = v.astype(BF).reshape(FS, ct, 256)
+            return carry
+
+        lax.fori_loop(0, D // 256, bproj, 0)
+        for i in R:
+            send_partial(s_d, r_d, c, i).start()
+
+    def dwd(t, carry):
+        cols = ds(t * nt, nt, 128)
+        ddn[cols, :] = mm_tn(hid[:, :, cols].reshape(NC * M, nt), gma[...].reshape(NC * M, D)).astype(BF)
+        return carry
+
+    lax.fori_loop(0, fl // nt, dwd, 0)
+    x_d = rcopy(ddn.at[ds((1 - g) * hl, hl, 16)], ld, s_x.at[0], r_x.at[0], partner)
+    x_d.start()
+
+    def dwu(k):
+        def one(t, carry):
+            cols = ds(t * 256, 256, 128)
+            dup[k, cols, :] = mm_tn(mida[:, :, :, cols].reshape(NC * M, 256), gu[k].reshape(NC * M, fl)).astype(BF)
+            return carry
+
+        lax.fori_loop(0, D // 256, one, 0)
+
+    dwu(1 - g)
+    x_u = rcopy(dup.at[1 - g], lu, s_x.at[1], r_x.at[1], partner)
+    x_u.start()
+    dwu(g)
+    mine = ds(g * hl, hl, 16)
+    x_d.wait_recv()
+    add_into(ddn.at[mine], ld, 64)
+    o_d = pltpu.make_async_copy(ddn.at[mine], dd_o, out_sem.at[0])
+    o_d.start()
+    x_u.wait_recv()
+    add_into(dup.at[g], lu, 64)
+    o_u = pltpu.make_async_copy(dup.at[g], du_o, out_sem.at[1])
+    o_u.start()
+
+    for c in range(NC):
+        at = slice(c * ct, (c + 1) * ct)
+        for i in R:
+            send_partial(s_d, r_d, c, i).wait_recv()
+        acc = gmid_o[at] + ps[c, f].astype(F32)
+        for i in R:
+            acc = acc + pr[c, i].astype(F32)
+        gmid_o[at] = acc
+    for c in range(NC):
+        for i in R:
+            gather_copy(mida, s_a, r_a, c, i).wait_send()
+            gather_copy(gma, s_c, r_c, c, i).wait_send()
+            send_partial(s_d, r_d, c, i).wait_send()
+    x_d.wait_send()
+    x_u.wait_send()
+    o_d.wait()
+    o_u.wait()
+
+
+def second(S, FS, mid, cot, wd, su, sg, alpha, wu, wup):
+    NC = 2
+    tok = mid.shape[0]
+    ct = tok // NC
+    fl = wd.shape[0]
+    M = FS * ct
+    sds = jax.ShapeDtypeStruct
+    outs = [sds((tok, D), BF), sds((tok, D), F32), sds((D, fl), BF), sds((fl // 2, D), BF),
+            sds((1, D), F32), sds((1, fl), F32), sds((1, fl), F32)]
+    dma = pltpu.SemaphoreType.DMA
+    F1 = FS - 1
+    return pl.pallas_call(
+        lambda *refs: second_kernel(S, FS, NC, *refs),
+        out_shape=outs,
+        in_specs=[VM] * 6 + [ANY] * 2,
+        out_specs=[VM, VM, ANY, ANY, VM, VM, VM],
+        scratch_shapes=[
+            pltpu.VMEM((2, D, fl), BF), pltpu.VMEM((NC, FS, ct, D), BF), pltpu.VMEM((NC, M, fl), F32),
+            pltpu.VMEM((NC, M, fl), F32), pltpu.VMEM((NC, M, fl), BF), pltpu.VMEM((NC, FS, ct, D), BF),
+            pltpu.VMEM((NC, F1, ct, D), BF), pltpu.VMEM((NC, FS, ct, D), BF), pltpu.VMEM((2, NC, M, fl), BF),
+            pltpu.VMEM((2, D, fl), BF), pltpu.VMEM((fl, D), BF), pltpu.VMEM((D, fl), BF), pltpu.VMEM((fl // 2, D), BF),
+        ] + [dma((NC, F1))] * 8 + [dma((2, FS)), dma((2,)), dma((2,)), dma((2,))],
+        compiler_params=pltpu.CompilerParams(collective_id=2, has_side_effects=True, vmem_limit_bytes=63 * 2**20),
+        name="second",
+    )(mid, cot, wd, su, sg, alpha.reshape(1, D), wu, wup)
+
+
+def third_kernel(S, FS, hp, gmid, x_ref, attn, alpha, mine, segc, segr, gain, wo, wq_i, qkv_i, raw_i, res_i, hall_i,
+                 gx_o, dout_o, dqkv_o, dal_o, dsq_o,
+                 wq, qkv, raw, res, hall, gh1, ga, gsend, gxr, bias, hx, gqh, dkv, gq, ps, pr, dout, dqk, lo, lq,
+                 ld_sem, h_sem, s_gx, r_gx, s_p, r_p, s_x, r_x, out_sem):
+    g, z, f = lax.axis_index("grp"), lax.axis_index("seq"), lax.axis_index("fsdp")
+    tok = x_ref.shape[0]
+    hw = hp * HEAD
+    wide = S * hw
+    total = S * tok
+    half = total // 2
+    w2 = 3 * hw // 2
+    dh = D // 2
+    partner = (1 - g, z, f)
+    greet([(g, lax.rem(z + i, S), f) for i in range(1, S)] + [partner])
+    loads = [pltpu.make_async_copy(a, b, ld_sem.at[i]) for i, (a, b) in enumerate(
+        [(qkv_i, qkv), (raw_i, raw), (res_i, res), (wq_i, wq)])]
+    for c in loads:
+        c.start()
+
+    def h_tile(t):
+        return pltpu.make_async_copy(hall_i.at[:, :, pl.ds(t * 256, 256)], hall.at[t % 2], h_sem.at[t % 2])
+
+    h_tile(0).start()
+    h_tile(1).start()
+    dal_o[...] = jnp.zeros_like(dal_o)
+    dsq_o[...] = jnp.zeros_like(dsq_o)
+    cr = tok // 4
+
+    def pre(i, carry):
+        at = ds(i * cr, cr, 16)
+        x = x_ref[at].astype(F32)
+        h = x * inv_rms(x)
+        av = attn[at]
+        inv_a = inv_rms(av)
+        ua = av * inv_a
+        al = alpha[...]
+        dif = ua - h
+        n_ = h + al * dif
+        inv_n = inv_rms(n_)
+        g_n = back(n_ * inv_n, inv_n, gmid[at])
+        dal_o[...] += jnp.sum(g_n * dif, axis=0, keepdims=True)
+        gh1[at] = (1 - al) * g_n
+        ga[at] = back(ua, inv_a, al * g_n).astype(BF)
+        return carry
+
+    lax.fori_loop(0, 4, pre, 0)
+    gmix = mm_nt(ga[...], wo[...]).astype(BF)
+    if wide > D:
+        gmix = jnp.concatenate([gmix, jnp.zeros((tok, wide - D), BF)], axis=1)
+    for k in range(S):
+        gsend[k] = gmix[:, k * hw : (k + 1) * hw]
+
+    def gx(k):
+        return rcopy(gsend.at[k], gxr.at[z], s_gx.at[k], r_gx.at[z], (g, k, f))
+
+    for k in range(S):
+        @pl.when(z != k)
+        def _():
+            gx(k).start()
+
+        @pl.when(z == k)
+        def _():
+            gxr[k] = gsend[k]
+
+    def dwo(t, carry):
+        cols = ds(t * 256, 256, 128)
+        v = mm_tn(mine[:, cols], ga[...]).astype(BF)
+        dout[0, cols, :] = v[:, :dh]
+        dout[1, cols, :] = v[:, dh:]
+        return carry
+
+    lax.fori_loop(0, D // 256, dwo, 0)
+    x_o = rcopy(dout.at[1 - g], lo, s_x.at[0], r_x.at[0], partner)
+    x_o.start()
+    attn_bias(S, tok, half, bias, segc, segr)
+    for c in loads:
+        c.wait()
+
+    def part(k):
+        return rcopy(ps.at[k], pr.at[z], s_p.at[k], r_p.at[z], (g, k, f))
+
+    for qb in reversed(range(S)):
+        q0 = qb * tok
+        n = q0 + tok
+        k0 = q0 if q0 < half else half
+
+        @pl.when(z != qb)
+        def _():
+            rcopy(gsend.at[0], gxr.at[qb], s_gx.at[0], r_gx.at[qb], (g, qb, f)).wait_recv()
+
+        for j in range(hp):
+            hx[j] = gxr[qb, :, j * HEAD : (j + 1) * HEAD]
+
+        def head(j, carry):
+            q = qkv[0, j, q0:n, :HEAD] * jnp.asarray(HEAD**-0.5, BF)
+            keys = qkv[1, j, :n, :HEAD]
+            gv = hx[j]
+            rinv = res[j, q0:n, HEAD : HEAD + 1]
+            delta = jnp.sum(gv.astype(F32) * res[j, q0:n, :HEAD], axis=-1, keepdims=True)
+            s = mm_nt(q, keys)
+            tail = s[:, k0:] + bias[qb, :, : n - k0].astype(F32)
+            p = jnp.exp(jnp.concatenate([s[:, :k0], tail], axis=1) if k0 else tail) * rinv
+            dp = mm_nt(gv, qkv[2, j, :n, :HEAD])
+            dsb = (p * (dp - delta)).astype(BF)
+            dq = mm(dsb, keys) * HEAD**-0.5
+            dk = mm_tn(dsb, q)
+            dv = mm_tn(p.astype(BF), gv)
+            if qb < S - 1:
+                dk = dk + dkv[j, :n, :HEAD]
+                dv = dv + dkv[j, :n, HEAD:]
+            if qb:
+                dkv[j, :q0, :HEAD] = dk[:q0]
+                dkv[j, :q0, HEAD:] = dv[:q0]
+            gj = gain[pl.ds(j, 1), :]
+            for c, d in ((0, dq), (1, dk[q0:])):
+                v = raw[c, j, q0:n]
+                inv = inv_rms(v)
+                u = v * inv
+                dsq_o[pl.ds(j, 1), :] += jnp.sum(d * u, axis=0, keepdims=True)
+                gqh[c, j] = back(u, inv, d * gj).astype(BF)
+            gqh[2, j] = dv[q0:].astype(BF)
+            return carry
+
+        lax.fori_loop(0, hp, head, 0)
+        gq[qb] = jnp.concatenate([gqh[c, j] for c in range(3) for j in range(hp)], axis=1)
+        ps[qb] = mm_nt(gq[qb], wq[...]).astype(BF)
+
+        @pl.when(z != qb)
+        def _():
+            part(qb).start()
+
+    for t in range(D // 256):
+        h_tile(t).wait()
+        v = mm_tn(hall[t % 2].reshape(total, 256), gq[...].reshape(total, 3 * hw)).astype(BF)
+        dqk[0, t * 256 : (t + 1) * 256, :] = v[:, :w2]
+        dqk[1, t * 256 : (t + 1) * 256, :] = v[:, w2:]
+        if t + 2 < D // 256:
+            h_tile(t + 2).start()
+    x_q = rcopy(dqk.at[1 - g], lq, s_x.at[1], r_x.at[1], partner)
+    x_q.start()
+    x_o.wait_recv()
+    add_into(dout.at[g], lo, 128)
+    o_o = pltpu.make_async_copy(dout.at[g], dout_o, out_sem.at[0])
+    o_o.start()
+    x_q.wait_recv()
+    add_into(dqk.at[g], lq, 128)
+    o_q = pltpu.make_async_copy(dqk.at[g], dqkv_o, out_sem.at[1])
+    o_q.start()
+
+    add_into(gh1, ps.at[z], 64)
+    for k in range(S):
+        @pl.when(z != k)
+        def _():
+            rcopy(ps.at[0], pr.at[k], s_p.at[0], r_p.at[k], (g, k, f)).wait_recv()
+            add_into(gh1, pr.at[k], 64)
+
+    def post(i, carry):
+        at = ds(i * cr, cr, 16)
+        x = x_ref[at].astype(F32)
+        inv = inv_rms(x)
+        gx_o[at] = back(x * inv, inv, gh1[at])
+        return carry
+
+    lax.fori_loop(0, 4, post, 0)
+    for k in range(S):
+        @pl.when(z != k)
+        def _():
+            gx(k).wait_send()
+            part(k).wait_send()
+    x_o.wait_send()
+    x_q.wait_send()
+    o_o.wait()
+    o_q.wait()
+
+
+def third(S, FS, hp, gmid, x, attn, alpha, mine, seg, gain, wo, wq, qkv, raw, res, hall):
+    tok, total = x.shape[0], seg.shape[0]
+    hw = hp * HEAD
+    sds = jax.ShapeDtypeStruct
+    outs = [sds((tok, D), F32), sds((D, D // 2), BF), sds((D, 3 * hw // 2), BF), sds((1, D), F32), sds((hp, HEAD), F32)]
+    dma = lambda n: pltpu.SemaphoreType.DMA((n,))
+    return pl.pallas_call(
+        lambda *refs: third_kernel(S, FS, hp, *refs),
+        out_shape=outs,
+        in_specs=[VM] * 9 + [ANY] * 5,
+        out_specs=[VM, ANY, ANY, VM, VM],
+        scratch_shapes=[
+            pltpu.VMEM((D, 3 * hw), BF), pltpu.VMEM((3, hp, total, 2 * HEAD), BF), pltpu.VMEM((2, hp, total, HEAD), F32),
+            pltpu.VMEM((hp, total, 2 * HEAD), F32), pltpu.VMEM((2, S, tok, 256), BF), pltpu.VMEM((tok, D), F32),
+            pltpu.VMEM((tok, D), BF), pltpu.VMEM((S, tok, hw), BF), pltpu.VMEM((S, tok, hw), BF),
+            pltpu.VMEM((S, tok, total // 2), BF), pltpu.VMEM((hp, tok, HEAD), BF), pltpu.VMEM((3, hp, tok, HEAD), BF),
+            pltpu.VMEM((hp, total, 2 * HEAD), F32), pltpu.VMEM((S, tok, 3 * hw), BF), pltpu.VMEM((S, tok, D), BF),
+            pltpu.VMEM((S, tok, D), BF), pltpu.VMEM((2, D, D // 2), BF), pltpu.VMEM((2, D, 3 * hw // 2), BF),
+            pltpu.VMEM((D, D // 2), BF), pltpu.VMEM((D, 3 * hw // 2), BF),
+            dma(4), dma(2), dma(S), dma(S), dma(S), dma(S), dma(2), dma(2), dma(2),
+        ],
+        compiler_params=pltpu.CompilerParams(collective_id=3, has_side_effects=True, vmem_limit_bytes=63 * 2**20),
+        name="third",
+    )(gmid, x, attn, alpha.reshape(1, D), mine, seg.reshape(total, 1), seg.reshape(1, total), gain, wo, wq, qkv, raw, res, hall)
+
+
+def fourth_kernel(S, FS, hp, vec, du, dd, dout, dqkv,
+                  up_o, dn_o, out_o, qkv_o, vec_o, sqk_o,
+                  own_u, raw_u, oth_u, own_d, raw_d, oth_d, own_o, raw_o, oth_o, so, xo, sq, xq, agq, va, vb, vf, vz,
+                  ld_sem, s_u, r_u, s_xo, r_xo, s_xq, r_xq, s_in, r_raw, r_oth, s_ret,
+                  s_aq, r_aq, s_fq, r_fq, s_v, r_v, o_sem, s_o, r_o):
+    g, z, f = lax.axis_index("grp"), lax.axis_index("seq"), lax.axis_index("fsdp")
+    rows = own_u.shape[1]
+    fl = own_u.shape[2]
+    hl = own_d.shape[0]
+    ff = fl * FS
+    hw = hp * HEAD
+    w2 = 3 * hw // 2
+    dh = D // 2
+    peers = [lax.rem(f + i, FS) for i in range(1, FS)]
+    bpeers = [lax.rem(f + FS - i, FS) for i in range(1, FS)]
+    zpeers = [lax.rem(z + i, S) for i in range(1, S)]
+    zb = [lax.rem(z + S - i, S) for i in range(1, S)]
+    partner = (1 - g, z, f)
+    R = range(FS - 1)
+    greet([(g, z, p) for p in peers] + [(g, p, f) for p in zpeers] + [partner])
+
+    def blk(p):
+        return ds(p * rows, rows, 16)
+
+    l_d = pltpu.make_async_copy(dd, own_d, ld_sem.at[0])
+    l_o = pltpu.make_async_copy(dout.at[blk(f)], so, ld_sem.at[1])
+    l_q = pltpu.make_async_copy(dqkv.at[blk(f)], sq, ld_sem.at[2])
+    l_u = pltpu.make_async_copy(du.at[blk(f)], own_u.at[f], ld_sem.at[3])
+    for c in (l_d, l_o, l_q, l_u):
+        c.start()
+    c_o = [rcopy(dout.at[blk(p)], xo.at[i], s_xo.at[i], r_xo.at[i], (g, z, p)) for i, p in enumerate(peers)]
+    c_q = [rcopy(dqkv.at[blk(p)], xq.at[i], s_xq.at[i], r_xq.at[i], (g, z, p)) for i, p in enumerate(peers)]
+    c_u = [rcopy(du.at[blk(p)], own_u.at[f], s_u.at[i], r_u.at[i], (g, z, p)) for i, p in enumerate(peers)]
+    va[...] = vec[...]
+    v_c = rcopy(va, vb, s_v.at[0], r_v.at[0], partner)
+    v_c.start()
+    for c in c_q + c_o + c_u:
+        c.start()
+
+    lower = z < S // 2
+    inner = jnp.where(lower, z + 1, z - 1)
+    outer = jnp.where(lower, z - 1, z + 1)
+    mid = (z == S // 2 - 1) | (z == S // 2)
+    has_outer = (z > 0) & (z < S - 1)
+    outer = jnp.where(has_outer, outer, inner)
+
+    pieces = []
+    nd = 4
+    for i in range(nd):
+        a = pl.ds(i * (hl // nd), hl // nd)
+        pieces.append((own_d.at[a], raw_d.at[a], oth_d.at[a],
+                       lambda o, i=i: o[1].at[ds(g * hl + i * (hl // nd), hl // nd, 16)]))
+    order = [(f, -1)] + [(p, i) for i, p in enumerate(bpeers)]
+    for p, i in order:
+        if i == 0:
+            pieces.append((own_o, raw_o, oth_o, lambda o: o[2].at[:, ds(g * dh, dh, 128)]))
+        for k in range(2):
+            a = pl.ds(k * (rows // 2), rows // 2)
+            pieces.append((own_u.at[p, a], raw_u.at[p, a], oth_u.at[p, a],
+                           lambda o, p=p, a=a: o[0].at[a, ds(g * ff + p * fl, fl, 128)]))
+
+    def toward(i, to_mid):
+        own, raw, oth, _ = pieces[i]
+        if to_mid:
+            return rcopy(own, oth, s_in.at[i], r_oth.at[i], (g, inner, f))
+        return rcopy(own, raw, s_in.at[i], r_raw.at[i], (g, inner, f))
+
+    def returned(i, from_mid):
+        own, raw, oth, _ = pieces[i]
+        return rcopy(raw if from_mid else oth, oth, s_ret.at[i], r_oth.at[i], (g, outer, f))
+
+    def go_in(i):
+        own, raw, oth, _ = pieces[i]
+
+        @pl.when(has_outer)
+        def _():
+            rcopy(own, raw, s_in.at[i], r_raw.at[i], (g, outer, f)).wait_recv()
+            own[...] = (own[...].astype(F32) + raw[...].astype(F32)).astype(BF)
+
+        @pl.when(mid)
+        def _():
+            toward(i, True).start()
+
+        @pl.when(jnp.logical_not(mid))
+        def _():
+            toward(i, False).start()
+
+    outs = (up_o, dn_o, out_o)
+
+    def local_out(i, src):
+        return pltpu.make_async_copy(src, pieces[i][3](outs), o_sem.at[i])
+
+    def remote_out(i, src):
+        dst = pieces[i][3](outs)
+        return rcopy(src, dst, s_o.at[i], r_o.at[i], partner)
+
+    def mid_out(i):
+        own, raw, oth, _ = pieces[i]
+        rcopy(own, oth, s_in.at[i], r_oth.at[i], (g, inner, f)).wait_recv()
+        raw[...] = (own[...].astype(F32) + oth[...].astype(F32)).astype(BF)
+
+        @pl.when(has_outer)
+        def _():
+            returned(i, True).start()
+
+        local_out(i, raw).start()
+        remote_out(i, raw).start()
+
+    def other_out(i):
+        own, raw, oth, _ = pieces[i]
+        rcopy(own, oth, s_in.at[i], r_oth.at[i], (g, inner, f)).wait_recv()
+
+        @pl.when(has_outer)
+        def _():
+            returned(i, False).start()
+
+        local_out(i, oth).start()
+        remote_out(i, oth).start()
+
+    total = len(pieces)
+    lag = 5
+
+    def step(i):
+        if i < total:
+            go_in(i)
+        if 1 <= i <= total:
+            @pl.when(mid)
+            def _():
+                mid_out(i - 1)
+        if i >= lag:
+            @pl.when(jnp.logical_not(mid))
+            def _():
+                other_out(i - lag)
+
+    def add_all(own, recv):
+        acc = own[...].astype(F32)
+        for i in R:
+            acc = acc + recv[i].astype(F32)
+        return acc.astype(BF)
+
+    def aq(i):
+        return rcopy(agq.at[z, g], agq.at[z, g], s_aq.at[i], r_aq.at[i], (g, zpeers[i], f))
+
+    def fq(i):
+        src = z if i < 0 else zb[i]
+        return rcopy(agq.at[src, g], agq.at[src, g], s_fq.at[i + 1], r_fq.at[i + 1], partner)
+
+    l_d.wait()
+    for i in range(nd):
+        step(i)
+    v_c.wait()
+    vf[f] = va[...] + vb[...]
+    v_f = [rcopy(vf.at[f], vf.at[f], s_v.at[1 + i], r_v.at[1 + i], (g, z, p)) for i, p in enumerate(peers)]
+    for c in v_f:
+        c.start()
+    l_u.wait()
+    step(nd)
+    step(nd + 1)
+    l_o.wait()
+    for c in c_o:
+        c.wait()
+    own_o[...] = add_all(so, xo)
+    step(nd + 2)
+    for c in v_f:
+        c.wait()
+    acc = vf[0]
+    for i in range(1, FS):
+        acc = acc + vf[i]
+    sub = lax.broadcasted_iota(jnp.int32, acc.shape, 0)
+    vz[z] = jnp.where(sub < 3, acc, vf[f])
+    v_z = [rcopy(vz.at[z], vz.at[z], s_v.at[FS + i], r_v.at[FS + i], (g, p, f)) for i, p in enumerate(zpeers)]
+    for c in v_z:
+        c.start()
+    l_q.wait()
+    for c in c_q:
+        c.wait()
+    agq[z, g] = add_all(sq, xq)
+    n = nd + 3
+    for i in R:
+        c_u[i].wait()
+        for k in range(2):
+            step(n)
+            n += 1
+        if i == R[-1]:
+            for j in range(S - 1):
+                aq(j).start()
+            fq(-1).start()
+    for k in range(lag):
+        step(n + k)
+    for j in range(S - 1):
+        aq(j).wait_recv()
+        fq(j).start()
+    for c in v_z:
+        c.wait()
+    acc = vz[0]
+    for i in range(1, S):
+        acc = acc + vz[i]
+    vec_o[...] = acc
+    for i in range(S):
+        sqk_o[i] = vz[i]
+    for j in range(-1, S - 1):
+        fq(j).wait_recv()
+    full = [jnp.concatenate([agq[k, 0], agq[k, 1]], axis=1) for k in range(S)]
+    cols = []
+    for c in range(3):
+        row = jnp.concatenate([full[k][:, c * hw : (c + 1) * hw] for k in range(S)], axis=1)
+        cols.append(row[:, :D])
+    qkv_o[...] = jnp.concatenate(cols, axis=1)
+    for j in range(-1, S - 1):
+        fq(j).wait_send()
+    for j in range(S - 1):
+        aq(j).wait_send()
+    for i in range(n):
+        own, raw, oth, _ = pieces[i]
+        toward(i, True).wait_send()
+
+        @pl.when(has_outer)
+        def _():
+            returned(i, True).wait_send()
+
+        local_out(i, raw).wait()
+        remote_out(i, raw).wait()
+
+
+def fourth(S, FS, hp, vec, du, dd, dout, dqkv):
+    fl = du.shape[1]
+    rows = D // FS
+    hl = dd.shape[0]
+    hw = hp * HEAD
+    w2 = 3 * hw // 2
+    dh = D // 2
+    n = 5 + 2 * FS
+    sds = jax.ShapeDtypeStruct
+    outs = [sds((rows, 2 * FS * fl), BF), sds((2 * hl, D), BF), sds((rows, D), BF), sds((rows, 3 * D), BF),
+            sds(vec.shape, F32), sds((S,) + vec.shape, F32)]
+    dma = lambda k: pltpu.SemaphoreType.DMA((k,))
+    F1 = FS - 1
+    u, d, o = pltpu.VMEM((FS, rows, fl), BF), pltpu.VMEM((hl, D), BF), pltpu.VMEM((rows, dh), BF)
+    v = pltpu.VMEM(vec.shape, F32)
+    return pl.pallas_call(
+        lambda *refs: fourth_kernel(S, FS, hp, *refs),
+        out_shape=outs,
+        in_specs=[VM] + [ANY] * 4,
+        out_specs=[ANY, ANY, ANY, VM, VM, VM],
+        scratch_shapes=[
+            u, u, u, d, d, d, o, o, o, o, pltpu.VMEM((F1, rows, dh), BF),
+            pltpu.VMEM((rows, w2), BF), pltpu.VMEM((F1, rows, w2), BF), pltpu.VMEM((S, 2, rows, w2), BF),
+            v, v, pltpu.VMEM((FS,) + vec.shape, F32), pltpu.VMEM((S,) + vec.shape, F32),
+            dma(4), dma(F1), dma(F1), dma(F1), dma(F1), dma(F1), dma(F1), dma(n), dma(n), dma(n), dma(n),
+            dma(S), dma(S), dma(S), dma(S), dma(FS + S), dma(FS + S), dma(n), dma(n), dma(n),
+        ],
+        compiler_params=pltpu.CompilerParams(collective_id=4, has_side_effects=True, vmem_limit_bytes=60 * 2**20),
+        name="fourth",
+    )(vec, du, dd, dout, dqkv)
 
 
 def body(S, FS, inputs, segments, w_qkv, w_out, w_upgate, w_down, s_qk, alpha_attn, alpha_mlp, s_up, s_gate, cotangent):
@@ -334,113 +985,32 @@
     f = lax.axis_index("fsdp")
     hp = -(-HEADS // S)
     hw = hp * HEAD
-    wide = S * hw
     rows = w_qkv.shape[0]
     ff = s_up.shape[0]
     fl = ff // FS
-
-    def head_pad(a):
-        return jnp.pad(a, [(0, 0)] * (a.ndim - 1) + [(0, wide - D)])
-
-    x = inputs[0].astype(F32)
-    tok = x.shape[0]
-    inv_x = inv_rms(x)
-    h = x * inv_x
+    x = inputs[0]
     seg = segments[0]
-    total = seg.shape[0]
-    gain = lax.dynamic_slice_in_dim(head_pad(s_qk), z * hw, hw).reshape(hp, HEAD)
-    h_all, wq, wo, wu4, raw, qkv, res, mine, attn, _ = first(
-        S, FS, hp, inputs[0], seg, w_qkv, w_out, gain, alpha_attn, w_upgate
-    )
-    h_all = h_all.reshape(total, D)
-    own = lax.dynamic_slice_in_dim(w_upgate.reshape(rows, 2, ff), f * fl, fl, 2).transpose(1, 0, 2)
-    wu4 = lax.dynamic_update_slice(wu4, own[:, None], (0, f, 0, 0))
-    wu = wu4.transpose(1, 2, 0, 3).reshape(D, 2 * fl)
-    rawt = raw.transpose(2, 0, 1, 3)
-    inv_qk = inv_rms(rawt)
-    u_qk = rawt * inv_qk
-    q, k, v = [qkv[c, :, :, :HEAD].transpose(1, 0, 2) for c in range(3)]
-    pos = jnp.arange(total, dtype=jnp.int32)
-    allowed = (pos[None, :] <= pos[:, None]) & ((seg[None, :] == 0) | (seg[None, :] == seg[:, None]))
-    probs = jnp.einsum("qhe,khe->hqk", q, k, preferred_element_type=F32) * HEAD**-0.5
-    probs = jnp.exp(jnp.where(allowed[None], probs, neg_big)) * res[:, :, HEAD : HEAD + 1]
-    inv_a = inv_rms(attn)
-    ua = attn * inv_a
-    n = h + alpha_attn * (ua - h)
-    inv_n = inv_rms(n)
-    mid = n * inv_n
-    midb = mid.astype(BF)
-    mid_all = gather(midb, "fsdp")
-    ug = mm(mid_all, wu)
-    up, gate = ug[:, :fl], ug[:, fl:]
-    su = lax.dynamic_slice_in_dim(s_up, f * fl, fl)
-    sg = lax.dynamic_slice_in_dim(s_gate, f * fl, fl)
-    a = gate * sg
-    sig = jax.nn.sigmoid(a)
-    silu = a * sig
-    hidden = (up * su * silu).astype(BF)
-    mlp = scatter(mm(hidden, w_down).astype(BF), "fsdp").astype(F32)
-    inv_m = inv_rms(mlp)
-    um = mlp * inv_m
-    m = mid + alpha_mlp * (um - mid)
-    inv_o = inv_rms(m)
-    out = m * inv_o
-    g = cotangent[0].astype(F32)
-    g_m = back(out, inv_o, g)
-    d_alpha_mlp = jnp.sum(g_m * (um - mid), axis=0)
-    g_mlp = back(um, inv_m, alpha_mlp * g_m)
-    g_mid1 = (1 - alpha_mlp) * g_m
-    gm_all = gather(g_mlp.astype(BF), "fsdp")
-    gh = mm_nt(gm_all, w_down)
-    d_down = mm_tn(hidden, gm_all)
-    g_up = gh * su * silu
-    d_su = jnp.sum(up * gh * silu, axis=0)
-    g_a = gh * up * su * sig * (1 + a * (1 - sig))
-    g_gate = g_a * sg
-    d_sg = jnp.sum(gate * g_a, axis=0)
-    gu = jnp.concatenate([g_up, g_gate], axis=1).astype(BF)
-    g_mid = g_mid1 + scatter(mm_nt(gu, wu).astype(BF), "fsdp").astype(F32)
-    d_upgate = mm_tn(mid_all, gu)
-    g_n = back(mid, inv_n, g_mid)
-    d_alpha_attn = jnp.sum(g_n * (ua - h), axis=0)
-    g_attn = back(ua, inv_a, alpha_attn * g_n)
-    g_h1 = (1 - alpha_attn) * g_n
-    ga = g_attn.astype(BF)
-    gmix = head_pad(mm_nt(ga, wo).astype(BF))
-    d_out = mm_tn(mine, ga)
-    gx = lax.all_to_all(gmix, "seq", split_axis=1, concat_axis=0, tiled=True).reshape(total, hp, HEAD)
-    dq, dk, dv = attention_back(q, k, v, probs, gx)
-    g_qk = jnp.stack([dq, dk], axis=1)
-    d_sqk = jnp.sum(g_qk * u_qk, axis=(0, 1)).reshape(hw)
-    g_raw = back(u_qk, inv_qk, g_qk * gain)
-    gq = jnp.concatenate([g_raw, dv[:, None]], axis=1).reshape(total, 3 * hw).astype(BF)
-    g_h = g_h1 + scatter(mm_nt(gq, wq).astype(BF), "seq").astype(F32)
-    d_qkv = mm_tn(h_all, gq)
-    g_x = back(h, inv_x, g_h)
-
-    d_down = lax.psum(d_down.astype(BF), ("grp", "seq")).astype(F32)
-    d_up = scatter(d_upgate.astype(BF), "grp", 1)
-    d_up = scatter(d_up, "seq", 1)
-    part = d_up.shape[1]
-    d_up = lax.all_to_all(d_up, "fsdp", split_axis=0, concat_axis=1, tiled=True)
-    d_up = gather(gather(d_up.reshape(rows, FS, part), "seq", 2), "grp", 2)
-    d_up = d_up.reshape(rows, FS, 2, fl).transpose(0, 2, 1, 3).reshape(rows, 2 * ff).astype(F32)
-    d_o = scatter(d_out.astype(BF), "fsdp")
-    d_o = lax.psum(d_o, ("grp", "seq")).astype(F32)
-    d_q = scatter(d_qkv.astype(BF), "fsdp")
-    d_q = lax.psum(d_q, "grp")
-    d_q = gather(d_q.reshape(rows, 3, hw), "seq", 2)[:, :, :D].reshape(rows, 3 * D).astype(F32)
-    slot = jnp.zeros((2, FS, fl), F32)
-    slot = lax.dynamic_update_slice(slot, jnp.stack([d_su, d_sg])[:, None], (0, f, 0)).reshape(-1)
-    slot_qk = lax.dynamic_update_slice(jnp.zeros((wide,), F32), d_sqk, (z * hw,))[:D]
-    flat = lax.psum(jnp.concatenate([slot_qk, d_alpha_attn, d_alpha_mlp, slot]), ("grp", "seq", "fsdp"))
-
-    def own(start, size):
-        return lax.dynamic_slice_in_dim(flat, start + f * (size // FS), size // FS)
+    gains = jnp.pad(s_qk, (0, S * hw - D))
+    gain = lax.dynamic_slice_in_dim(gains, z * hw, hw).reshape(hp, HEAD)
+    hall, wq, wo, wu, raw, qkv, res, mine, attn, mid = first(S, FS, hp, x, seg, w_qkv, w_out, gain, alpha_attn, w_upgate)
+    su = lax.dynamic_slice_in_dim(s_up, f * fl, fl).reshape(1, fl)
+    sg = lax.dynamic_slice_in_dim(s_gate, f * fl, fl).reshape(1, fl)
+    out, g_mid, du, dd, d_mlp, d_su, d_sg = second(S, FS, mid, cotangent[0], w_down, su, sg, alpha_mlp, wu, w_upgate)
+    g_x, dout, dqkv, d_attn, d_sqk = third(S, FS, hp, g_mid, x, attn, alpha_attn, mine, seg, gain, wo, wq, qkv, raw, res, hall)
+
+    def row(v):
+        return jnp.pad(v.reshape(1, -1), ((0, 0), (0, D - v.size)))
+
+    vec = jnp.concatenate([row(d_mlp), row(d_attn), row(d_sqk), row(d_su), row(d_sg), jnp.zeros((3, D), F32)])
+    d_up, d_down, d_o, d_q, tot, parts = fourth(S, FS, hp, vec, du, dd, dout, dqkv)
+    sqk = parts[:, 2, :hw].reshape(-1)
+
+    def own(v):
+        return lax.dynamic_slice_in_dim(v, f * rows, rows)
 
     return (
-        out.astype(BF)[None], g_x[None], d_q, d_o, d_up, d_down,
-        own(0, D), own(D, D), own(2 * D, D), own(3 * D, ff), own(3 * D + ff, ff),
+        out[None], g_x[None], d_q.astype(F32), d_o.astype(F32), d_up.astype(F32), d_down.astype(F32),
+        own(sqk), own(tot[1]), own(tot[0]), tot[3, :fl], tot[4, :fl],
     )
 
 

time: 931 us -> 520 us (0.56)
  waiting for transfers between devices: 434 us -> 0 us
  Pallas kernels: 90.5 us -> 485 us
  local copies, waits for them, and re-layouts: 150 us -> 15.7 us
  matrix products: 117 us -> 0 us
  other arithmetic: 64.3 us -> 16.7 us
  blocking collectives: 41.3 us -> 0 us
  between operations: 14.9 us -> 0.75 us
  starting transfers between devices: 10.3 us -> 0 us
    pallas_call x0 -> x3, Pallas kernels: none -> 395 us  [the longest x1 173 us: fourth(): pl.pallas_call(lambda *refs: fourth_kernel(S, FS, hp, *refs), out_shape=o...]
    all_gather x5 -> x0, waiting for transfers between devices: 180 us -> none  [gather(): return lax.all_gather(x, axes, axis=dim, tiled=True)]
    reduce_scatter x6 -> x0, waiting for transfers between devices: 133 us -> none  [scatter(): return lax.psum_scatter(x, axes, scatter_dimension=dim, tiled=True)]
    dot_general x15 -> x0, matrix products: 117 us -> none  [the longest x4 28.7 us: mm_nt(): lax.dot_general(a, b, (((1,), (1,)), ((), ())), preferred_element_type=F32)]
    psum x2 -> x0, waiting for transfers between devices: 116 us -> none  [the longest x1 94.7 us: body(): d_o = lax.psum(d_o, ('grp', 'seq')).astype(F32)]
    convert_element_type x5 -> x0, local copies, waits for them, and re-layouts: 50.6 us -> none  [the longest x3 44.6 us: body(): d_up.reshape(rows, FS, 2, fl).transpose(0, 2, 1, 3).reshape(rows, 2 * ff)]
    psum x1 -> x0, blocking collectives: 41.3 us -> none  [body(): lax.psum(jnp.concatenate([slot_qk, d_alpha_attn, d_alpha_mlp, slot]), ('g...]
    transpose x1 -> x0, local copies, waits for them, and re-layouts: 27.5 us -> none  [body(): wu = wu4.transpose(1, 2, 0, 3).reshape(D, 2 * fl)]
  transfers between devices with their start and end apart: 16 -> 0, of which waited for: 13 -> 0; matrix products, arithmetic and copies ran while one was open for 23% -> 0% of each run, Pallas kernels for 0% -> 0%
where the time goes in v3:
time: 520 us; the launch traced here: 518 us
  Pallas kernels  485 us (93%)
  other arithmetic  16.7 us (3%)
  local copies, waits for them, and re-layouts  15.7 us (3%)
    pallas_call x1, Pallas kernels, fourth(): pl.pallas_call(lambda *refs: fourth_kernel(S, FS, hp, *refs), out_shape=o...  173 us
    pallas_call x1, Pallas kernels, second(): pl.pallas_call(lambda *refs: second_kernel(S, FS, NC, *refs), out_shape=o...  120 us
    pallas_call x1, Pallas kernels, third(): pl.pallas_call(lambda *refs: third_kernel(S, FS, hp, *refs), out_shape=ou...  102 us
    pallas_call x1, Pallas kernels, first(): pl.pallas_call(lambda *refs: first_kernel(S, FS, hp, *refs), out_shape=ou...  90.6 us

profile of v3, /device:TPU:0, one launch (start us, length us, event | category | flops | bytes accessed | tf_op | source)
XLA Modules:
  0.0 518.3 jit_solution(6022798846074011568)
XLA Ops:
  0.6 0.8 dynamic_slice.22
  1.4 0.7 reshape.43.refs_5_.refs_7_
  2.1 1.7 copy.23.refs_1_.refs_5_
  3.8 1.3 reshape.44.refs_6_.refs_3_
  5.1 90.6 %first.1 = (bf16[4,256,1280]{2,1,0:T(8,128)(2,1)}, bf16[1280,960]{1,0:T(8,128)(2,1)}, bf16[1280,1280]{1,0:T(8,128)(2,1)}, bf16[2,4,320,1280]{3,2,1,0:T(8,128)(2,...) custom-call(bf16[256,1280]{1,0:T(8,128)(2,1)} %bitcast.5, ...), custom_call_target="tpu_custom_call" | custom-call | tf_op jit(solution)/shard_map/first/pallas_call | solution.py:304
  95.7 0.8 dynamic_slice.23
  96.4 0.6 reshape.45.refs_3_
  97.0 0.8 dynamic_slice.24
  97.8 0.6 reshape.46.refs_4_
  99.0 120.4 %second.1 = (bf16[256,1280]{1,0:T(8,128)(2,1)}, f32[256,1280]{1,0:T(8,128)}, bf16[1280,1280]{1,0:T(8,128)(2,1)}, bf16[640,1280]{1,0:T(8,128)(2,1)}, f32[1,1280]{...) custom-call(f32[256,1280]{1,0:T(8,128)} %get-tuple-element.39.refs_0_, bf16[256,1280]{1,0:T(8,128)(2,1)} %bitcast.8, ...), custom_call_target="tpu_custom_call" | custom-call | tf_op jit(solution)/shard_map/second/pallas_call | solution.py:510
  219.5 101.7 %third.1 = (f32[256,1280]{1,0:T(8,128)}, bf16[1280,640]{1,0:T(8,128)(2,1)}, bf16[1280,480]{1,0:T(8,128)(2,1)}, f32[1,1280]{1,0:T(1,128)}, f32[5,64]{1,0:T(8,128)}) custom-call(f32[256,1280]{1,0:T(8,128)} %get-tuple-element.42.refs_0_, bf16[256,1280]{1,0:T(8,128)(2,1)} %bitcast.6, f32[256,1280]{1,0:T(8,128)} %get-tuple-element.43.refs_2_, ...), custom_call_target="tpu_custom_call" | custom-call | tf_op jit(solution)/shard_map/third/pallas_call | solution.py:707
  321.2 0.7 reshape.48
  322.0 1.4 concatenate.3.refs_0_
  323.4 172.5 %fourth.1 = (bf16[320,10240]{1,0:T(8,128)(2,1)}, bf16[1280,1280]{1,0:T(8,128)(2,1)}, bf16[320,1280]{1,0:T(8,128)(2,1)}, bf16[320,3840]{1,0:T(8,128)(2,1)}, f32[8,1280]{1,0:T(8,128)}, /*index=5*/f32[4,8,1280]{2,1,0:T(8,128)}) custom-call(f32[8,1280]{1,0:T(8,128)} %concatenate.3.refs_0_, bf16[1280,1280]{1,0:T(8,128)(2,1)} %get-tuple-element.57.refs_1_, ...), custom_call_target="tpu_custom_call" | custom-call | tf_op jit(solution)/shard_map/fourth/pallas_call | solution.py:966
  495.9 1.6 slice_reduce_fusion.1
  497.5 0.7 dynamic-slice_reduce_fusion
  498.1 9.6 %convert_element_type.16 = f32[320,10240]{1,0:T(8,128)} convert(bf16[320,10240]{1,0:T(8,128)(2,1)} %get-tuple-element.63) | non-fusion elementwise | flops 3276800 | bytes 19660800 | tf_op jit(solution)/shard_map/convert_element_type | solution.py:1012
  507.7 3.3 convert_element_type.17
  511.0 2.6 convert_element_type.14
  513.6 1.3 convert_element_type.15
  514.8 0.8 slice_reduce_fusion
  515.8 0.7 dynamic_slice.25
  516.4 0.8 copy.27
  517.2 1.1 copy.28
  (22 shorter events, 0.7 us)
Async XLA Ops:
  5.1 93.3 %copy-start.5 = (f32[1280]{0:T(1024)S(1)}, f32[1280]{0:T(1024)}, u32[]{:S(2)}) copy-start(f32[1280]{0:T(1024)} %param.20) | copy-start | bytes 15364
  219.5 102.5 %copy-start.6 = (f32[1,1280]{1,0:T(1,128)S(1)}, f32[1,1280]{1,0:T(1,128)}, u32[]{:S(2)}) copy-start(f32[1,1280]{1,0:T(1,128)} %get-tuple-element.52) | copy-start | bytes 15364
  219.5 102.5 %copy-start.7 = (f32[1,1280]{1,0:T(1,128)S(1)}, f32[1,1280]{1,0:T(1,128)}, u32[]{:S(2)}) copy-start(f32[1,1280]{1,0:T(1,128)} %get-tuple-element.55) | copy-start | bytes 15364
  219.5 102.5 %copy-start.8 = (f32[1,1280]{1,0:T(1,128)S(1)}, f32[1,1280]{1,0:T(1,128)}, u32[]{:S(2)}) copy-start(f32[1,1280]{1,0:T(1,128)} %get-tuple-element.56) | copy-start | bytes 15364
  498.1 9.6 %copy-start = (bf16[1280,1280]{1,0:T(8,128)(2,1)S(1)}, bf16[1280,1280]{1,0:T(8,128)(2,1)}, u32[]{:S(2)}) copy-start(bf16[1280,1280]{1,0:T(8,128)(2,1)} %get-tuple-element.64) | copy-start | bytes 9830404
  507.7 3.3 copy-start.1
  511.0 2.6 copy-start.3
  513.6 2.8 copy-start.4
  513.6 3.7 copy-start.2

commit v4 on v3

--- a/solution.py
+++ b/solution.py
@@ -322,49 +322,135 @@
 
 def second_kernel(S, FS, NC, mid, cot, wd, su, sg, alpha, wu_i, wup,
                   out_o, gmid_o, du_o, dd_o, dal_o, dsu_o, dsg_o,
-                  wu, mida, up, gate, hid, ps, pr, gma, gu, dup, ddn, lu, ld,
+                  wu, mida, up, gate, hid, ps, pr, rl, gma, gu, dup, ddn, lu, ld,
                   s_a, r_a, s_b, r_b, s_c, r_c, s_d, r_d, w_sem, s_x, r_x, out_sem):
     g, z, f = lax.axis_index("grp"), lax.axis_index("seq"), lax.axis_index("fsdp")
     tok = mid.shape[0]
     ct = tok // NC
+    hc = ct // 2
     fl = wd.shape[0]
     ff = wup.shape[1] // 2
     rows = wup.shape[0]
     hl = fl // 2
     nt = 256 if fl % 256 == 0 else 128
     M = FS * ct
+    relay = FS == 4
     peers = [lax.rem(f + i, FS) for i in range(1, FS)]
-    bpeers = [lax.rem(f + FS - i, FS) for i in range(1, FS)]
     partner = (1 - g, z, f)
     greet([(g, z, p) for p in peers] + [partner])
-
-    def gather_copy(buf, ss, rs, c, i):
+    R = range(FS - 1)
+    A, B = pl.ds(0, hc), pl.ds(hc, hc)
+    if relay:
+        fx, fy, fd = f + 1 - 2 * lax.rem(f, 2), lax.rem(f + 2, 4), 3 - f
+        dx, dy = (g, z, fx), (g, z, fy)
+
+    def direct(buf, ss, rs, c, i):
         return rcopy(buf.at[c, f], buf.at[c, f], ss.at[c, i], rs.at[c, i], (g, z, peers[i]))
 
-    def send_partial(ss, rs, c, i):
+    def gcopy(buf, ss, rs, c, k):
+        src, half, dev = ((f, A, dx), (f, B, dx), (f, B, dy), (f, A, dy), (fx, A, dy), (fy, B, dx))[k]
+        view = buf.at[c, src, half]
+        return rcopy(view, view, ss.at[c, k], rs.at[c, k], dev)
+
+    def g_issue(buf, ss, rs, c):
+        if relay:
+            for k in (0, 2, 1, 3):
+                gcopy(buf, ss, rs, c, k).start()
+        else:
+            for i in R:
+                direct(buf, ss, rs, c, i).start()
+
+    def g_relay(buf, ss, rs, c):
+        if relay:
+            for k in (0, 2):
+                gcopy(buf, ss, rs, c, k).wait_recv()
+                gcopy(buf, ss, rs, c, 4 if k == 0 else 5).start()
+
+    def g_wait(buf, ss, rs, c):
+        if relay:
+            for k in (1, 3, 4, 5):
+                gcopy(buf, ss, rs, c, k).wait_recv()
+        else:
+            for i in R:
+                direct(buf, ss, rs, c, i).wait_recv()
+
+    def g_sent(buf, ss, rs, c):
+        if relay:
+            for k in range(6):
+                gcopy(buf, ss, rs, c, k).wait_send()
+        else:
+            for i in R:
+                direct(buf, ss, rs, c, i).wait_send()
+
+    def scopy(ss, rs, c, k):
+        src, dst, dev = (
+            (ps.at[c, fd, A], rl.at[c, 0], dx),
+            (ps.at[c, fd, B], rl.at[c, 1], dy),
+            (ps.at[c, fx, A], pr.at[c, 0, A], dx),
+            (ps.at[c, fy, B], pr.at[c, 1, B], dy),
+            (ps.at[c, fy, A], pr.at[c, 1, A], dy),
+            (ps.at[c, fx, B], pr.at[c, 0, B], dx),
+        )[k]
+        return rcopy(src, dst, ss.at[c, k], rs.at[c, k], dev)
+
+    def sdirect(ss, rs, c, i):
         return rcopy(ps.at[c, peers[i]], pr.at[c, i], ss.at[c, i], rs.at[c, i], (g, z, peers[i]))
 
-    R = range(FS - 1)
+    def s_issue(ss, rs, c):
+        if relay:
+            for k in range(4):
+                scopy(ss, rs, c, k).start()
+        else:
+            for i in R:
+                sdirect(ss, rs, c, i).start()
+
+    def s_relay(ss, rs, c):
+        if relay:
+            for k, tgt, half in ((0, fy, A), (1, fx, B)):
+                scopy(ss, rs, c, k).wait_recv()
+                ps[c, tgt, half] = (ps[c, tgt, half].astype(F32) + rl[c, k].astype(F32)).astype(BF)
+                scopy(ss, rs, c, 4 + k).start()
+
+    def s_total(ss, rs, c):
+        if relay:
+            for k in range(2, 6):
+                scopy(ss, rs, c, k).wait_recv()
+        else:
+            for i in R:
+                sdirect(ss, rs, c, i).wait_recv()
+        acc = ps[c, f].astype(F32)
+        for i in range(2 if relay else FS - 1):
+            acc = acc + pr[c, i].astype(F32)
+        return acc
+
+    def s_sent(ss, rs, c):
+        if relay:
+            for k in range(6):
+                scopy(ss, rs, c, k).wait_send()
+        else:
+            for i in R:
+                sdirect(ss, rs, c, i).wait_send()
+
     for c in range(NC):
         mida[c, f] = mid[c * ct : (c + 1) * ct].astype(BF)
-        for i in R:
-            gather_copy(mida, s_a, r_a, c, i).start()
-    loads = []
-    for k in range(2):
-        loads.append(pltpu.make_async_copy(wup.at[:, ds(k * ff + f * fl, fl, 128)], wu.at[k, ds(f * rows, rows, 16)], w_sem.at[k, 0]))
-        for i in R:
-            loads.append(pltpu.make_async_copy(wu_i.at[k, peers[i]], wu.at[k, ds(peers[i] * rows, rows, 16)], w_sem.at[k, i + 1]))
-    for c in loads:
-        c.start()
-    dsu_o[...] = jnp.zeros_like(dsu_o)
-    dsg_o[...] = jnp.zeros_like(dsg_o)
-    dal_o[...] = jnp.zeros_like(dal_o)
-    for c in loads:
-        c.wait()
+        g_issue(mida, s_a, r_a, c)
+        if c == 0:
+            loads = []
+            for k in range(2):
+                loads.append(pltpu.make_async_copy(wup.at[:, ds(k * ff + f * fl, fl, 128)], wu.at[k, ds(f * rows, rows, 16)], w_sem.at[k, 0]))
+                for i in R:
+                    loads.append(pltpu.make_async_copy(wu_i.at[k, peers[i]], wu.at[k, ds(peers[i] * rows, rows, 16)], w_sem.at[k, i + 1]))
+            for ld_c in loads:
+                ld_c.start()
+            dsu_o[...] = jnp.zeros_like(dsu_o)
+            dsg_o[...] = jnp.zeros_like(dsg_o)
+            dal_o[...] = jnp.zeros_like(dal_o)
+        g_relay(mida, s_a, r_a, c)
+    for ld_c in loads:
+        ld_c.wait()
 
     for c in range(NC):
-        for i in R:
-            gather_copy(mida, s_a, r_a, c, i).wait_recv()
+        g_wait(mida, s_a, r_a, c)
 
         def fwd(t, carry):
             cols = ds(t * nt, nt, 128)
@@ -378,6 +464,8 @@
             return carry
 
         lax.fori_loop(0, fl // nt, fwd, 0)
+        if c:
+            s_relay(s_b, r_b, c - 1)
 
         def proj(t, carry):
             cols = ds(t * 256, 256, 128)
@@ -385,16 +473,12 @@
             return carry
 
         lax.fori_loop(0, D // 256, proj, 0)
-        for i in R:
-            send_partial(s_b, r_b, c, i).start()
+        s_issue(s_b, r_b, c)
+    s_relay(s_b, r_b, NC - 1)
 
     for c in range(NC):
         at = slice(c * ct, (c + 1) * ct)
-        for i in R:
-            send_partial(s_b, r_b, c, i).wait_recv()
-        mlp = ps[c, f].astype(F32)
-        for i in R:
-            mlp = mlp + pr[c, i].astype(F32)
+        mlp = s_total(s_b, r_b, c)
         al = alpha[...]
         md = mid[at]
         inv_m = inv_rms(mlp)
@@ -408,12 +492,11 @@
         dal_o[...] += jnp.sum(g_m * dif, axis=0, keepdims=True)
         gmid_o[at] = (1 - al) * g_m
         gma[c, f] = back(um, inv_m, al * g_m).astype(BF)
-        for i in R:
-            gather_copy(gma, s_c, r_c, c, i).start()
+        g_issue(gma, s_c, r_c, c)
+        g_relay(gma, s_c, r_c, c)
 
     for c in range(NC):
-        for i in R:
-            gather_copy(gma, s_c, r_c, c, i).wait_recv()
+        g_wait(gma, s_c, r_c, c)
 
         def bwd(t, carry):
             cols = ds(t * nt, nt, 128)
@@ -433,8 +516,9 @@
             return carry
 
         lax.fori_loop(0, fl // nt, bwd, 0)
-        for i in R:
-            send_partial(s_b, r_b, c, i).wait_send()
+        if c:
+            s_relay(s_d, r_d, c - 1)
+        s_sent(s_b, r_b, c)
 
         def bproj(t, carry):
             cols = ds(t * 256, 256, 128)
@@ -443,8 +527,7 @@
             return carry
 
         lax.fori_loop(0, D // 256, bproj, 0)
-        for i in R:
-            send_partial(s_d, r_d, c, i).start()
+        s_issue(s_d, r_d, c)
 
     def dwd(t, carry):
         cols = ds(t * nt, nt, 128)
@@ -452,6 +535,7 @@
         return carry
 
     lax.fori_loop(0, fl // nt, dwd, 0)
+    s_relay(s_d, r_d, NC - 1)
     x_d = rcopy(ddn.at[ds((1 - g) * hl, hl, 16)], ld, s_x.at[0], r_x.at[0], partner)
     x_d.start()
 
@@ -479,17 +563,11 @@
 
     for c in range(NC):
         at = slice(c * ct, (c + 1) * ct)
-        for i in R:
-            send_partial(s_d, r_d, c, i).wait_recv()
-        acc = gmid_o[at] + ps[c, f].astype(F32)
-        for i in R:
-            acc = acc + pr[c, i].astype(F32)
-        gmid_o[at] = acc
+        gmid_o[at] = gmid_o[at] + s_total(s_d, r_d, c)
     for c in range(NC):
-        for i in R:
-            gather_copy(mida, s_a, r_a, c, i).wait_send()
-            gather_copy(gma, s_c, r_c, c, i).wait_send()
-            send_partial(s_d, r_d, c, i).wait_send()
+        g_sent(mida, s_a, r_a, c)
+        g_sent(gma, s_c, r_c, c)
+        s_sent(s_d, r_d, c)
     x_d.wait_send()
     x_u.wait_send()
     o_d.wait()
@@ -515,9 +593,10 @@
         scratch_shapes=[
             pltpu.VMEM((2, D, fl), BF), pltpu.VMEM((NC, FS, ct, D), BF), pltpu.VMEM((NC, M, fl), F32),
             pltpu.VMEM((NC, M, fl), F32), pltpu.VMEM((NC, M, fl), BF), pltpu.VMEM((NC, FS, ct, D), BF),
-            pltpu.VMEM((NC, F1, ct, D), BF), pltpu.VMEM((NC, FS, ct, D), BF), pltpu.VMEM((2, NC, M, fl), BF),
+            pltpu.VMEM((NC, 2 if FS == 4 else F1, ct, D), BF), pltpu.VMEM((NC, 2, ct // 2, D), BF),
+            pltpu.VMEM((NC, FS, ct, D), BF), pltpu.VMEM((2, NC, M, fl), BF),
             pltpu.VMEM((2, D, fl), BF), pltpu.VMEM((fl, D), BF), pltpu.VMEM((D, fl), BF), pltpu.VMEM((fl // 2, D), BF),
-        ] + [dma((NC, F1))] * 8 + [dma((2, FS)), dma((2,)), dma((2,)), dma((2,))],
+        ] + [dma((NC, max(F1, 6)))] * 8 + [dma((2, FS)), dma((2,)), dma((2,)), dma((2,))],
         compiler_params=pltpu.CompilerParams(collective_id=2, has_side_effects=True, vmem_limit_bytes=63 * 2**20),
         name="second",
     )(mid, cot, wd, su, sg, alpha.reshape(1, D), wu, wup)

time: 520 us -> 507 us (0.975)
  Pallas kernels: 485 us -> 472 us
    pallas_call x1, Pallas kernels: 120 us -> 103 us  [second(): pl.pallas_call(lambda *refs: second_kernel(S, FS, NC, *refs), out_shape=o...]
where the time goes in v4:
time: 507 us; the launch traced here: 506 us
  Pallas kernels  472 us (93%)
  other arithmetic  16.7 us (3%)
  local copies, waits for them, and re-layouts  15.7 us (3%)
    pallas_call x1, Pallas kernels, fourth(): pl.pallas_call(lambda *refs: fourth_kernel(S, FS, hp, *refs), out_shape=o...  175 us
    pallas_call x1, Pallas kernels, third(): pl.pallas_call(lambda *refs: third_kernel(S, FS, hp, *refs), out_shape=ou...  104 us
    pallas_call x1, Pallas kernels, second(): pl.pallas_call(lambda *refs: second_kernel(S, FS, NC, *refs), out_shape=o...  103 us
    pallas_call x1, Pallas kernels, first(): pl.pallas_call(lambda *refs: first_kernel(S, FS, hp, *refs), out_shape=ou...  90.6 us

profile of v4, /device:TPU:0, one launch (start us, length us, event | category | flops | bytes accessed | tf_op | source)
XLA Modules:
  0.0 505.5 jit_solution(5555734413149982467)
XLA Ops:
  0.6 0.8 dynamic_slice.22
  1.4 0.7 reshape.43.refs_5_.refs_7_
  2.1 1.7 copy.23.refs_1_.refs_5_
  3.8 1.3 reshape.44.refs_6_.refs_3_
  5.1 90.6 %first.1 = (bf16[4,256,1280]{2,1,0:T(8,128)(2,1)}, bf16[1280,960]{1,0:T(8,128)(2,1)}, bf16[1280,1280]{1,0:T(8,128)(2,1)}, bf16[2,4,320,1280]{3,2,1,0:T(8,128)(2,...) custom-call(bf16[256,1280]{1,0:T(8,128)(2,1)} %bitcast.5, ...), custom_call_target="tpu_custom_call" | custom-call | tf_op jit(solution)/shard_map/first/pallas_call | solution.py:304
  95.7 0.8 dynamic_slice.23
  96.4 0.6 reshape.45.refs_3_
  97.0 0.8 dynamic_slice.24
  97.8 0.6 reshape.46.refs_4_
  99.0 102.6 %second.1 = (bf16[256,1280]{1,0:T(8,128)(2,1)}, f32[256,1280]{1,0:T(8,128)}, bf16[1280,1280]{1,0:T(8,128)(2,1)}, bf16[640,1280]{1,0:T(8,128)(2,1)}, f32[1,1280]{...) custom-call(f32[256,1280]{1,0:T(8,128)} %get-tuple-element.39.refs_0_, bf16[256,1280]{1,0:T(8,128)(2,1)} %bitcast.8, ...), custom_call_target="tpu_custom_call" | custom-call | tf_op jit(solution)/shard_map/second/pallas_call | solution.py:588
  201.7 104.3 %third.1 = (f32[256,1280]{1,0:T(8,128)}, bf16[1280,640]{1,0:T(8,128)(2,1)}, bf16[1280,480]{1,0:T(8,128)(2,1)}, f32[1,1280]{1,0:T(1,128)}, f32[5,64]{1,0:T(8,128)}) custom-call(f32[256,1280]{1,0:T(8,128)} %get-tuple-element.42.refs_0_, bf16[256,1280]{1,0:T(8,128)(2,1)} %bitcast.6, f32[256,1280]{1,0:T(8,128)} %get-tuple-element.43.refs_2_, ...), custom_call_target="tpu_custom_call" | custom-call | tf_op jit(solution)/shard_map/third/pallas_call | solution.py:786
  306.0 0.7 reshape.48
  306.8 1.4 concatenate.3.refs_0_
  308.1 174.9 %fourth.1 = (bf16[320,10240]{1,0:T(8,128)(2,1)}, bf16[1280,1280]{1,0:T(8,128)(2,1)}, bf16[320,1280]{1,0:T(8,128)(2,1)}, bf16[320,3840]{1,0:T(8,128)(2,1)}, f32[8,1280]{1,0:T(8,128)}, /*index=5*/f32[4,8,1280]{2,1,0:T(8,128)}) custom-call(f32[8,1280]{1,0:T(8,128)} %concatenate.3.refs_0_, bf16[1280,1280]{1,0:T(8,128)(2,1)} %get-tuple-element.57.refs_1_, ...), custom_call_target="tpu_custom_call" | custom-call | tf_op jit(solution)/shard_map/fourth/pallas_call | solution.py:1045
  483.1 1.6 slice_reduce_fusion.1
  484.7 0.7 dynamic-slice_reduce_fusion
  485.4 9.6 %convert_element_type.16 = f32[320,10240]{1,0:T(8,128)} convert(bf16[320,10240]{1,0:T(8,128)(2,1)} %get-tuple-element.63) | non-fusion elementwise | flops 3276800 | bytes 19660800 | tf_op jit(solution)/shard_map/convert_element_type | solution.py:1091
  494.9 3.3 convert_element_type.17
  498.2 2.6 convert_element_type.14
  500.8 1.3 convert_element_type.15
  502.1 0.8 slice_reduce_fusion
  503.0 0.7 dynamic_slice.25
  503.6 0.8 copy.27
  504.5 1.1 copy.28
  (22 shorter events, 0.7 us)
Async XLA Ops:
  5.1 93.3 %copy-start.5 = (f32[1280]{0:T(1024)S(1)}, f32[1280]{0:T(1024)}, u32[]{:S(2)}) copy-start(f32[1280]{0:T(1024)} %param.20) | copy-start | bytes 15364
  201.7 105.1 %copy-start.6 = (f32[1,1280]{1,0:T(1,128)S(1)}, f32[1,1280]{1,0:T(1,128)}, u32[]{:S(2)}) copy-start(f32[1,1280]{1,0:T(1,128)} %get-tuple-element.52) | copy-start | bytes 15364
  201.7 105.1 %copy-start.7 = (f32[1,1280]{1,0:T(1,128)S(1)}, f32[1,1280]{1,0:T(1,128)}, u32[]{:S(2)}) copy-start(f32[1,1280]{1,0:T(1,128)} %get-tuple-element.55) | copy-start | bytes 15364
  201.7 105.1 %copy-start.8 = (f32[1,1280]{1,0:T(1,128)S(1)}, f32[1,1280]{1,0:T(1,128)}, u32[]{:S(2)}) copy-start(f32[1,1280]{1,0:T(1,128)} %get-tuple-element.56) | copy-start | bytes 15364
  485.4 9.6 %copy-start = (bf16[1280,1280]{1,0:T(8,128)(2,1)S(1)}, bf16[1280,1280]{1,0:T(8,128)(2,1)}, u32[]{:S(2)}) copy-start(bf16[1280,1280]{1,0:T(8,128)(2,1)} %get-tuple-element.64) | copy-start | bytes 9830404
  494.9 3.3 copy-start.1
  498.2 2.6 copy-start.3
  500.8 2.8 copy-start.4
  500.8 3.7 copy-start.2

commit v5 on v4

--- a/solution.py
+++ b/solution.py
@@ -59,10 +59,12 @@
     return (ki <= qi) & ((seg_row == 0) | (seg_row == seg_col))
 
 
-def add_into(dst, src, chunk):
+def add_into(dst, src, chunk, out=None):
+    out = dst if out is None else out
+
     def one(i, carry):
         at = ds(i * chunk, chunk, 16)
-        dst[at] = (dst[at].astype(F32) + src[at].astype(F32)).astype(dst.dtype)
+        out[at] = (dst[at].astype(F32) + src[at].astype(F32)).astype(dst.dtype)
         return carry
 
     lax.fori_loop(0, src.shape[0] // chunk, one, 0)
@@ -185,7 +187,7 @@
             for j in range(hp):
                 for c in range(2):
                     v = acc[:, c * hw + j * HEAD : c * hw + (j + 1) * HEAD]
-                    raw[c, j, at, :] = v
+                    raw[j, at, c * HEAD : (c + 1) * HEAD] = v
                     u = v * inv_rms(v) * gain[j : j + 1]
                     qkv[c, j, at, :HEAD] = u.astype(BF)
                 qkv[2, j, at, :HEAD] = acc[:, 2 * hw + j * HEAD : 2 * hw + (j + 1) * HEAD].astype(BF)
@@ -296,7 +298,7 @@
     sds = jax.ShapeDtypeStruct
     outs = [
         sds((S, tok, D), BF), sds((D, 3 * hw), BF), sds((D, D), BF), sds((2, FS, rows, fl), BF),
-        sds((2, hp, total, HEAD), F32), sds((3, hp, total, 2 * HEAD), BF), sds((hp, total, 2 * HEAD), F32),
+        sds((hp, total, 2 * HEAD), F32), sds((3, hp, total, 2 * HEAD), BF), sds((hp, total, 2 * HEAD), F32),
         sds((tok, D), BF), sds((tok, D), F32), sds((tok, D), F32),
     ]
     dma = lambda n: pltpu.SemaphoreType.DMA((n,))
@@ -308,7 +310,7 @@
         out_specs=[ANY] * 7 + [VM] * 3,
         scratch_shapes=[
             pltpu.VMEM((S, tok, D), BF), pltpu.VMEM((D, 3 * hw), BF), pltpu.VMEM((D, D), BF),
-            pltpu.VMEM((2, hp, total, HEAD), F32), pltpu.VMEM((3, hp, total, 2 * HEAD), BF),
+            pltpu.VMEM((hp, total, 2 * HEAD), F32), pltpu.VMEM((3, hp, total, 2 * HEAD), BF),
             pltpu.VMEM((hp, total, 2 * HEAD), F32), pltpu.VMEM((S, tok, total // 2), BF),
             pltpu.VMEM((hp, tok, HEAD), BF), pltpu.VMEM((S, tok, hw), BF), pltpu.VMEM((tok, D), BF),
             pltpu.VMEM((S, tok, hw), BF),
@@ -602,10 +604,107 @@
     )(mid, cot, wd, su, sg, alpha.reshape(1, D), wu, wup)
 
 
-def third_kernel(S, FS, hp, gmid, x_ref, attn, alpha, mine, segc, segr, gain, wo, wq_i, qkv_i, raw_i, res_i, hall_i,
-                 gx_o, dout_o, dqkv_o, dal_o, dsq_o,
-                 wq, qkv, raw, res, hall, gh1, ga, gsend, gxr, bias, hx, gqh, dkv, gq, ps, pr, dout, dqk, lo, lq,
-                 ld_sem, h_sem, s_gx, r_gx, s_p, r_p, s_x, r_x, out_sem):
+def make_chain(S, pieces, outs, sems):
+    s_in, r_raw, r_oth, s_ret, o_sem, s_o, r_o = sems
+    g, z, f = lax.axis_index("grp"), lax.axis_index("seq"), lax.axis_index("fsdp")
+    partner = (1 - g, z, f)
+    lower = z < S // 2
+    inner = jnp.where(lower, z + 1, z - 1)
+    mid = (z == S // 2 - 1) | (z == S // 2)
+    has_outer = (z > 0) & (z < S - 1)
+    outer = jnp.where(has_outer, jnp.where(lower, z - 1, z + 1), inner)
+    rest = jnp.logical_not(mid)
+
+    def toward(i, to_mid):
+        own, raw, oth, _ = pieces[i]
+        if to_mid:
+            return rcopy(own, oth, s_in.at[i], r_oth.at[i], (g, inner, f))
+        return rcopy(own, raw, s_in.at[i], r_raw.at[i], (g, inner, f))
+
+    def returned(i, from_mid):
+        own, raw, oth, _ = pieces[i]
+        return rcopy(raw if from_mid else oth, oth, s_ret.at[i], r_oth.at[i], (g, outer, f))
+
+    def local_out(i, src):
+        return pltpu.make_async_copy(src, pieces[i][3](outs), o_sem.at[i])
+
+    def remote_out(i, src):
+        return rcopy(src, pieces[i][3](outs), s_o.at[i], r_o.at[i], partner)
+
+    def send(i):
+        @pl.when(mid)
+        def _():
+            toward(i, True).start()
+
+        @pl.when(rest)
+        def _():
+            toward(i, False).start()
+
+    def launch(i):
+        @pl.when(jnp.logical_not(has_outer))
+        def _():
+            send(i)
+
+    def go_in(i):
+        own, raw, oth, _ = pieces[i]
+
+        @pl.when(has_outer)
+        def _():
+            rcopy(own, raw, s_in.at[i], r_raw.at[i], (g, outer, f)).wait_recv()
+            add_into(own, raw, 80)
+            send(i)
+
+    def finish(i, src, from_mid):
+        @pl.when(has_outer)
+        def _():
+            returned(i, from_mid).start()
+
+        local_out(i, src).start()
+        remote_out(i, src).start()
+
+    def arrived(i):
+        own, raw, oth, _ = pieces[i]
+        rcopy(own, oth, s_in.at[i], r_oth.at[i], (g, inner, f)).wait_recv()
+
+    def step(i, lag=5):
+        if i < len(pieces):
+            go_in(i)
+        if 1 <= i <= len(pieces):
+            @pl.when(mid)
+            def _():
+                own, raw, oth, _ = pieces[i - 1]
+                arrived(i - 1)
+                add_into(own, oth, 80, raw)
+                finish(i - 1, raw, True)
+        if lag <= i < len(pieces) + lag:
+            @pl.when(rest)
+            def _():
+                arrived(i - lag)
+                finish(i - lag, pieces[i - lag][2], False)
+
+    def drain():
+        for i in range(len(pieces)):
+            toward(i, True).wait_send()
+
+            @pl.when(has_outer)
+            def _():
+                returned(i, True).wait_send()
+
+            local_out(i, pieces[i][1]).wait()
+            remote_out(i, pieces[i][1]).wait()
+
+    return launch, step, drain
+
+
+def cuts(size, parts, unit):
+    step = size // unit
+    return [(a * step, (b - a) * step) for a, b in zip(parts[:-1], parts[1:])]
+
+
+def third_kernel(S, FS, hp, gmid, x_ref, attn, alpha, mine, segc, segr, gain, wo, wq_i, qkv_i, raw_i, res_i, hall_i, dd_i,
+                 gh1, ps_o, dout_o, dqkv_o, dn_o, dal_o, dsq_o,
+                 wq, qkv, raw, res, hall, ga, gsend, gxr, bias, hx, gqh, dkv, gq, ps, dout, dqk, lo, lq, own_d, raw_d, oth_d,
+                 ld_sem, h_sem, s_gx, r_gx, s_p, s_x, r_x, out_sem, *chain_sems):
     g, z, f = lax.axis_index("grp"), lax.axis_index("seq"), lax.axis_index("fsdp")
     tok = x_ref.shape[0]
     hw = hp * HEAD
@@ -621,11 +720,23 @@
     for c in loads:
         c.start()
 
+    hl = own_d.shape[0]
+    dd_c = pltpu.make_async_copy(dd_i.at[pl.ds(0, hl)], own_d, h_sem.at[2])
+    dd_c.start()
+    pieces = []
+    for lo_r, n_r in cuts(hl, (0, 1, 2, 4) if hl % 64 == 0 else (0, 2, 4), 4):
+        pieces.append((own_d.at[pl.ds(lo_r, n_r)], raw_d.at[pl.ds(lo_r, n_r)], oth_d.at[pl.ds(lo_r, n_r)],
+                       lambda o, lo_r=lo_r, n_r=n_r: o.at[g, pl.ds(lo_r, n_r)]))
+    launch, step, drain = make_chain(S, pieces, dn_o, chain_sems)
+    n_p = len(pieces)
+
     def h_tile(t):
         return pltpu.make_async_copy(hall_i.at[:, :, pl.ds(t * 256, 256)], hall.at[t % 2], h_sem.at[t % 2])
 
     h_tile(0).start()
     h_tile(1).start()
+    dd_c.wait()
+    launch(0)
     dal_o[...] = jnp.zeros_like(dal_o)
     dsq_o[...] = jnp.zeros_like(dsq_o)
     cr = tok // 4
@@ -666,6 +777,7 @@
         def _():
             gxr[k] = gsend[k]
 
+
     def dwo(t, carry):
         cols = ds(t * 256, 256, 128)
         v = mm_tn(mine[:, cols], ga[...]).astype(BF)
@@ -679,9 +791,10 @@
     attn_bias(S, tok, half, bias, segc, segr)
     for c in loads:
         c.wait()
+    done = 0
 
     def part(k):
-        return rcopy(ps.at[k], pr.at[z], s_p.at[k], r_p.at[z], (g, k, f))
+        return pltpu.make_async_copy(ps.at[k], ps_o.at[k], s_p.at[k])
 
     for qb in reversed(range(S)):
         q0 = qb * tok
@@ -691,6 +804,10 @@
         @pl.when(z != qb)
         def _():
             rcopy(gsend.at[0], gxr.at[qb], s_gx.at[0], r_gx.at[qb], (g, qb, f)).wait_recv()
+
+        if qb == S - 1:
+            for i in range(1, n_p):
+                launch(i)
 
         for j in range(hp):
             hx[j] = gxr[qb, :, j * HEAD : (j + 1) * HEAD]
@@ -717,7 +834,7 @@
                 dkv[j, :q0, HEAD:] = dv[:q0]
             gj = gain[pl.ds(j, 1), :]
             for c, d in ((0, dq), (1, dk[q0:])):
-                v = raw[c, j, q0:n]
+                v = raw[j, q0:n, c * HEAD : (c + 1) * HEAD]
                 inv = inv_rms(v)
                 u = v * inv
                 dsq_o[pl.ds(j, 1), :] += jnp.sum(d * u, axis=0, keepdims=True)
@@ -729,9 +846,10 @@
         gq[qb] = jnp.concatenate([gqh[c, j] for c in range(3) for j in range(hp)], axis=1)
         ps[qb] = mm_nt(gq[qb], wq[...]).astype(BF)
 
-        @pl.when(z != qb)
-        def _():
-            part(qb).start()
+        part(qb).start()
+        if done < n_p + 5:
+            step(done)
+            done += 1
 
     for t in range(D // 256):
         h_tile(t).wait()
@@ -746,196 +864,110 @@
     add_into(dout.at[g], lo, 128)
     o_o = pltpu.make_async_copy(dout.at[g], dout_o, out_sem.at[0])
     o_o.start()
+    while done < n_p + 5:
+        step(done)
+        done += 1
     x_q.wait_recv()
     add_into(dqk.at[g], lq, 128)
     o_q = pltpu.make_async_copy(dqk.at[g], dqkv_o, out_sem.at[1])
     o_q.start()
 
-    add_into(gh1, ps.at[z], 64)
     for k in range(S):
         @pl.when(z != k)
         def _():
-            rcopy(ps.at[0], pr.at[k], s_p.at[0], r_p.at[k], (g, k, f)).wait_recv()
-            add_into(gh1, pr.at[k], 64)
-
-    def post(i, carry):
-        at = ds(i * cr, cr, 16)
-        x = x_ref[at].astype(F32)
-        inv = inv_rms(x)
-        gx_o[at] = back(x * inv, inv, gh1[at])
-        return carry
-
-    lax.fori_loop(0, 4, post, 0)
-    for k in range(S):
-        @pl.when(z != k)
-        def _():
             gx(k).wait_send()
-            part(k).wait_send()
+
+        part(k).wait()
     x_o.wait_send()
     x_q.wait_send()
     o_o.wait()
     o_q.wait()
-
-
-def third(S, FS, hp, gmid, x, attn, alpha, mine, seg, gain, wo, wq, qkv, raw, res, hall):
+    drain()
+
+
+def third(S, FS, hp, gmid, x, attn, alpha, mine, seg, gain, wo, wq, qkv, raw, res, hall, dd):
     tok, total = x.shape[0], seg.shape[0]
     hw = hp * HEAD
     sds = jax.ShapeDtypeStruct
-    outs = [sds((tok, D), F32), sds((D, D // 2), BF), sds((D, 3 * hw // 2), BF), sds((1, D), F32), sds((hp, HEAD), F32)]
+    outs = [sds((tok, D), F32), sds((S, tok, D), BF), sds((D, D // 2), BF), sds((D, 3 * hw // 2), BF), sds((2, dd.shape[0] // 2, D), BF),
+            sds((1, D), F32), sds((hp, HEAD), F32)]
     dma = lambda n: pltpu.SemaphoreType.DMA((n,))
+    hd = pltpu.VMEM((dd.shape[0] // 2, D), BF)
     return pl.pallas_call(
         lambda *refs: third_kernel(S, FS, hp, *refs),
         out_shape=outs,
-        in_specs=[VM] * 9 + [ANY] * 5,
-        out_specs=[VM, ANY, ANY, VM, VM],
+        in_specs=[VM] * 9 + [ANY] * 6,
+        out_specs=[VM, ANY, ANY, ANY, ANY, VM, VM],
         scratch_shapes=[
-            pltpu.VMEM((D, 3 * hw), BF), pltpu.VMEM((3, hp, total, 2 * HEAD), BF), pltpu.VMEM((2, hp, total, HEAD), F32),
-            pltpu.VMEM((hp, total, 2 * HEAD), F32), pltpu.VMEM((2, S, tok, 256), BF), pltpu.VMEM((tok, D), F32),
+            pltpu.VMEM((D, 3 * hw), BF), pltpu.VMEM((3, hp, total, 2 * HEAD), BF), pltpu.VMEM((hp, total, 2 * HEAD), F32),
+            pltpu.VMEM((hp, total, 2 * HEAD), F32), pltpu.VMEM((2, S, tok, 256), BF),
             pltpu.VMEM((tok, D), BF), pltpu.VMEM((S, tok, hw), BF), pltpu.VMEM((S, tok, hw), BF),
             pltpu.VMEM((S, tok, total // 2), BF), pltpu.VMEM((hp, tok, HEAD), BF), pltpu.VMEM((3, hp, tok, HEAD), BF),
             pltpu.VMEM((hp, total, 2 * HEAD), F32), pltpu.VMEM((S, tok, 3 * hw), BF), pltpu.VMEM((S, tok, D), BF),
-            pltpu.VMEM((S, tok, D), BF), pltpu.VMEM((2, D, D // 2), BF), pltpu.VMEM((2, D, 3 * hw // 2), BF),
+            pltpu.VMEM((2, D, D // 2), BF), pltpu.VMEM((2, D, 3 * hw // 2), BF),
             pltpu.VMEM((D, D // 2), BF), pltpu.VMEM((D, 3 * hw // 2), BF),
-            dma(4), dma(2), dma(S), dma(S), dma(S), dma(S), dma(2), dma(2), dma(2),
-        ],
+            hd, hd, hd,
+            dma(4), dma(3), dma(S), dma(S), dma(S), dma(2), dma(2), dma(2),
+        ] + [dma(5)] * 7,
         compiler_params=pltpu.CompilerParams(collective_id=3, has_side_effects=True, vmem_limit_bytes=63 * 2**20),
         name="third",
-    )(gmid, x, attn, alpha.reshape(1, D), mine, seg.reshape(total, 1), seg.reshape(1, total), gain, wo, wq, qkv, raw, res, hall)
-
-
-def fourth_kernel(S, FS, hp, vec, du, dd, dout, dqkv,
-                  up_o, dn_o, out_o, qkv_o, vec_o, sqk_o,
-                  own_u, raw_u, oth_u, own_d, raw_d, oth_d, own_o, raw_o, oth_o, so, xo, sq, xq, agq, va, vb, vf, vz,
-                  ld_sem, s_u, r_u, s_xo, r_xo, s_xq, r_xq, s_in, r_raw, r_oth, s_ret,
-                  s_aq, r_aq, s_fq, r_fq, s_v, r_v, o_sem, s_o, r_o):
+    )(gmid, x, attn, alpha.reshape(1, D), mine, seg.reshape(total, 1), seg.reshape(1, total), gain, wo, wq, qkv, raw, res, hall, dd)
+
+
+def fourth_kernel(S, FS, hp, vec, x_ref, gh1, ps_i, du, dd, dout, dqkv,
+                  up_o, dn_o, out_o, gx_o, qkv_o, vec_o, sqk_o,
+                  own_u, raw_u, oth_u, own_d, raw_d, oth_d, own_o, raw_o, oth_o, so, xo, sq, xq, agq, ps, pr, va, vb, vf, vz,
+                  ld_sem, s_u, r_u, s_xo, r_xo, s_xq, r_xq, s_au, r_au, s_ad, r_ad, s_fq, r_fq, s_v, r_v,
+                  s_p, r_p, *chain_sems):
     g, z, f = lax.axis_index("grp"), lax.axis_index("seq"), lax.axis_index("fsdp")
+    tok = x_ref.shape[0]
     rows = own_u.shape[1]
     fl = own_u.shape[2]
-    hl = own_d.shape[0]
     ff = fl * FS
     hw = hp * HEAD
-    w2 = 3 * hw // 2
     dh = D // 2
     peers = [lax.rem(f + i, FS) for i in range(1, FS)]
     bpeers = [lax.rem(f + FS - i, FS) for i in range(1, FS)]
     zpeers = [lax.rem(z + i, S) for i in range(1, S)]
-    zb = [lax.rem(z + S - i, S) for i in range(1, S)]
+    above, below = (g, lax.rem(z + 1, S), f), (g, lax.rem(z + S - 1, S), f)
     partner = (1 - g, z, f)
+    first_z, last_z = z == 0, z == S - 1
     R = range(FS - 1)
     greet([(g, z, p) for p in peers] + [(g, p, f) for p in zpeers] + [partner])
 
     def blk(p):
         return ds(p * rows, rows, 16)
 
-    l_d = pltpu.make_async_copy(dd, own_d, ld_sem.at[0])
-    l_o = pltpu.make_async_copy(dout.at[blk(f)], so, ld_sem.at[1])
-    l_q = pltpu.make_async_copy(dqkv.at[blk(f)], sq, ld_sem.at[2])
-    l_u = pltpu.make_async_copy(du.at[blk(f)], own_u.at[f], ld_sem.at[3])
-    for c in (l_d, l_o, l_q, l_u):
+    l_u = pltpu.make_async_copy(du.at[blk(f)], own_u.at[f], ld_sem.at[0])
+    l_p = pltpu.make_async_copy(ps_i, ps, ld_sem.at[3])
+    l_q = pltpu.make_async_copy(dqkv.at[blk(f)], sq, ld_sem.at[1])
+    l_o = pltpu.make_async_copy(dout.at[blk(f)], so, ld_sem.at[2])
+    hl = own_d.shape[0]
+    l_d = pltpu.make_async_copy(dd.at[pl.ds(hl, hl)], own_d, ld_sem.at[4])
+    for c in (l_d, l_p, l_u, l_q, l_o):
         c.start()
-    c_o = [rcopy(dout.at[blk(p)], xo.at[i], s_xo.at[i], r_xo.at[i], (g, z, p)) for i, p in enumerate(peers)]
     c_q = [rcopy(dqkv.at[blk(p)], xq.at[i], s_xq.at[i], r_xq.at[i], (g, z, p)) for i, p in enumerate(peers)]
     c_u = [rcopy(du.at[blk(p)], own_u.at[f], s_u.at[i], r_u.at[i], (g, z, p)) for i, p in enumerate(peers)]
+    c_o = [rcopy(dout.at[blk(p)], xo.at[i], s_xo.at[i], r_xo.at[i], (g, z, p)) for i, p in enumerate(peers)]
+    for c in c_q + c_u + c_o:
+        c.start()
     va[...] = vec[...]
     v_c = rcopy(va, vb, s_v.at[0], r_v.at[0], partner)
     v_c.start()
-    for c in c_q + c_o + c_u:
-        c.start()
-
-    lower = z < S // 2
-    inner = jnp.where(lower, z + 1, z - 1)
-    outer = jnp.where(lower, z - 1, z + 1)
-    mid = (z == S // 2 - 1) | (z == S // 2)
-    has_outer = (z > 0) & (z < S - 1)
-    outer = jnp.where(has_outer, outer, inner)
 
     pieces = []
-    nd = 4
-    for i in range(nd):
-        a = pl.ds(i * (hl // nd), hl // nd)
-        pieces.append((own_d.at[a], raw_d.at[a], oth_d.at[a],
-                       lambda o, i=i: o[1].at[ds(g * hl + i * (hl // nd), hl // nd, 16)]))
-    order = [(f, -1)] + [(p, i) for i, p in enumerate(bpeers)]
-    for p, i in order:
-        if i == 0:
-            pieces.append((own_o, raw_o, oth_o, lambda o: o[2].at[:, ds(g * dh, dh, 128)]))
-        for k in range(2):
-            a = pl.ds(k * (rows // 2), rows // 2)
+    for lo_r, n_r in cuts(hl, (0, 1, 2), 2):
+        a = pl.ds(lo_r, n_r)
+        pieces.append((own_d.at[a], raw_d.at[a], oth_d.at[a], lambda o, a=a: o[2].at[g, a]))
+    for p in [f] + bpeers:
+        for lo_r, n_r in cuts(rows, (0, 1, 2), 2):
+            a = pl.ds(lo_r, n_r)
             pieces.append((own_u.at[p, a], raw_u.at[p, a], oth_u.at[p, a],
                            lambda o, p=p, a=a: o[0].at[a, ds(g * ff + p * fl, fl, 128)]))
-
-    def toward(i, to_mid):
-        own, raw, oth, _ = pieces[i]
-        if to_mid:
-            return rcopy(own, oth, s_in.at[i], r_oth.at[i], (g, inner, f))
-        return rcopy(own, raw, s_in.at[i], r_raw.at[i], (g, inner, f))
-
-    def returned(i, from_mid):
-        own, raw, oth, _ = pieces[i]
-        return rcopy(raw if from_mid else oth, oth, s_ret.at[i], r_oth.at[i], (g, outer, f))
-
-    def go_in(i):
-        own, raw, oth, _ = pieces[i]
-
-        @pl.when(has_outer)
-        def _():
-            rcopy(own, raw, s_in.at[i], r_raw.at[i], (g, outer, f)).wait_recv()
-            own[...] = (own[...].astype(F32) + raw[...].astype(F32)).astype(BF)
-
-        @pl.when(mid)
-        def _():
-            toward(i, True).start()
-
-        @pl.when(jnp.logical_not(mid))
-        def _():
-            toward(i, False).start()
-
-    outs = (up_o, dn_o, out_o)
-
-    def local_out(i, src):
-        return pltpu.make_async_copy(src, pieces[i][3](outs), o_sem.at[i])
-
-    def remote_out(i, src):
-        dst = pieces[i][3](outs)
-        return rcopy(src, dst, s_o.at[i], r_o.at[i], partner)
-
-    def mid_out(i):
-        own, raw, oth, _ = pieces[i]
-        rcopy(own, oth, s_in.at[i], r_oth.at[i], (g, inner, f)).wait_recv()
-        raw[...] = (own[...].astype(F32) + oth[...].astype(F32)).astype(BF)
-
-        @pl.when(has_outer)
-        def _():
-            returned(i, True).start()
-
-        local_out(i, raw).start()
-        remote_out(i, raw).start()
-
-    def other_out(i):
-        own, raw, oth, _ = pieces[i]
-        rcopy(own, oth, s_in.at[i], r_oth.at[i], (g, inner, f)).wait_recv()
-
-        @pl.when(has_outer)
-        def _():
-            returned(i, False).start()
-
-        local_out(i, oth).start()
-        remote_out(i, oth).start()
-
-    total = len(pieces)
-    lag = 5
-
-    def step(i):
-        if i < total:
-            go_in(i)
-        if 1 <= i <= total:
-            @pl.when(mid)
-            def _():
-                mid_out(i - 1)
-        if i >= lag:
-            @pl.when(jnp.logical_not(mid))
-            def _():
-                other_out(i - lag)
+    for lo_r, n_r in cuts(rows, (0, 1, 2), 2):
+        a = pl.ds(lo_r, n_r)
+        pieces.append((own_o.at[a], raw_o.at[a], oth_o.at[a], lambda o, a=a: o[1].at[a, ds(g * dh, dh, 128)]))
+    launch, step, drain = make_chain(S, pieces, (up_o, out_o, dn_o), chain_sems)
 
     def add_all(own, recv):
         acc = own[...].astype(F32)
@@ -943,58 +975,156 @@
             acc = acc + recv[i].astype(F32)
         return acc.astype(BF)
 
-    def aq(i):
-        return rcopy(agq.at[z, g], agq.at[z, g], s_aq.at[i], r_aq.at[i], (g, zpeers[i], f))
-
-    def fq(i):
-        src = z if i < 0 else zb[i]
-        return rcopy(agq.at[src, g], agq.at[src, g], s_fq.at[i + 1], r_fq.at[i + 1], partner)
+    def go_up(b):
+        return rcopy(ps.at[b], pr.at[b], s_p.at[b], r_p.at[b], above)
+
+    def go_down(b):
+        slot = jnp.where(z == b + 1, S, b)
+        return rcopy(ps.at[b], pr.at[slot], s_p.at[b], r_p.at[slot], below)
+
+    def gh_end(c):
+        @pl.when(first_z)
+        def _():
+            go_up(S - 1 - c).start()
+
+        @pl.when(last_z)
+        def _():
+            go_down(c).start()
+
+    def gh_mid(c):
+        bu, bd = S - 1 - c + z, c - (S - 1 - z)
+
+        def up():
+            @pl.when((z > 0) & (bu > z) & (bu < S))
+            def _():
+                go_up(bu).wait_recv()
+                add_into(ps.at[bu], pr.at[bu], 64)
+                go_up(bu).start()
+
+        def down():
+            @pl.when((z < S - 1) & (bd >= 0) & (bd < z))
+            def _():
+                rcopy(ps.at[bd], pr.at[bd], s_p.at[bd], r_p.at[bd], above).wait_recv()
+                add_into(ps.at[bd], pr.at[bd], 64)
+                go_down(bd).start()
+
+        @pl.when(z < S // 2)
+        def _():
+            up()
+
+        down()
+
+        @pl.when(z >= S // 2)
+        def _():
+            up()
+
+    def piece(b):
+        return agq.at[b, g]
+
+    def a_up(t, b):
+        return rcopy(piece(b), piece(b), s_au.at[t], r_au.at[t], above)
+
+    def a_down(t, b):
+        return rcopy(piece(b), piece(b), s_ad.at[t], r_ad.at[t], below)
+
+    def fq(b):
+        return rcopy(piece(b), piece(b), s_fq.at[b], r_fq.at[b], partner)
+
+    def a_start():
+        @pl.when(z < S - 1)
+        def _():
+            a_up(0, z).start()
+
+        @pl.when(z > 0)
+        def _():
+            a_down(0, z).start()
+
+        fq(z).start()
+
+    def a_relay(t):
+        bu, bd = z - 1 - t, z + 1 + t
+
+        @pl.when(bu >= 0)
+        def _():
+            a_up(t, bu).wait_recv()
+
+            @pl.when(z < S - 1)
+            def _():
+                a_up(t + 1, bu).start()
+
+            fq(bu).start()
+
+        @pl.when(bd < S)
+        def _():
+            a_down(t, bd).wait_recv()
+
+            @pl.when(z > 0)
+            def _():
+                a_down(t + 1, bd).start()
+
+            fq(bd).start()
 
     l_d.wait()
-    for i in range(nd):
-        step(i)
+    launch(0)
+    launch(1)
+    l_p.wait()
+    gh_end(0)
+    step(0)
     v_c.wait()
     vf[f] = va[...] + vb[...]
     v_f = [rcopy(vf.at[f], vf.at[f], s_v.at[1 + i], r_v.at[1 + i], (g, z, p)) for i, p in enumerate(peers)]
     for c in v_f:
         c.start()
+    step(1)
+    l_q.wait()
+    for c in c_q:
+        c.wait()
+    agq[z, g] = add_all(sq, xq)
+    a_start()
+    gh_mid(1)
     l_u.wait()
-    step(nd)
-    step(nd + 1)
+    launch(2)
+    launch(3)
+    gh_end(1)
+    step(2)
+    step(3)
+    gh_mid(2)
+    n = 4
+    for i in R:
+        c_u[i].wait()
+        launch(n)
+        launch(n + 1)
+        if 2 + i < S - 1:
+            gh_end(2 + i)
+        step(n)
+        step(n + 1)
+        n += 2
+        if 3 + i < S - 1:
+            gh_mid(3 + i)
+        if i < S - 1:
+            a_relay(i)
+        if i == 0:
+            for c in v_f:
+                c.wait()
+            acc = vf[0]
+            for k in range(1, FS):
+                acc = acc + vf[k]
+            sub = lax.broadcasted_iota(jnp.int32, acc.shape, 0)
+            vz[z] = jnp.where(sub < 3, acc, vf[f])
+            v_z = [rcopy(vz.at[z], vz.at[z], s_v.at[FS + k], r_v.at[FS + k], (g, p, f)) for k, p in enumerate(zpeers)]
+            for c in v_z:
+                c.start()
     l_o.wait()
     for c in c_o:
         c.wait()
     own_o[...] = add_all(so, xo)
-    step(nd + 2)
-    for c in v_f:
-        c.wait()
-    acc = vf[0]
-    for i in range(1, FS):
-        acc = acc + vf[i]
-    sub = lax.broadcasted_iota(jnp.int32, acc.shape, 0)
-    vz[z] = jnp.where(sub < 3, acc, vf[f])
-    v_z = [rcopy(vz.at[z], vz.at[z], s_v.at[FS + i], r_v.at[FS + i], (g, p, f)) for i, p in enumerate(zpeers)]
-    for c in v_z:
-        c.start()
-    l_q.wait()
-    for c in c_q:
-        c.wait()
-    agq[z, g] = add_all(sq, xq)
-    n = nd + 3
-    for i in R:
-        c_u[i].wait()
-        for k in range(2):
-            step(n)
-            n += 1
-        if i == R[-1]:
-            for j in range(S - 1):
-                aq(j).start()
-            fq(-1).start()
-    for k in range(lag):
-        step(n + k)
-    for j in range(S - 1):
-        aq(j).wait_recv()
-        fq(j).start()
+    launch(n)
+    launch(n + 1)
+    step(n)
+    step(n + 1)
+    n += 2
+    for i in range(FS - 1, S - 1):
+        a_relay(i)
     for c in v_z:
         c.wait()
     acc = vz[0]
@@ -1003,60 +1133,92 @@
     vec_o[...] = acc
     for i in range(S):
         sqk_o[i] = vz[i]
-    for j in range(-1, S - 1):
-        fq(j).wait_recv()
+    step(n)
+    step(n + 1)
+
+    cr = tok // 4
+    gx_o[...] = gh1[...]
+    add_into(gx_o, ps.at[z], 64)
+
+    @pl.when(z > 0)
+    def _():
+        go_up(z).wait_recv()
+        add_into(gx_o, pr.at[z], 64)
+
+    @pl.when(z < S - 1)
+    def _():
+        rcopy(ps.at[0], pr.at[S], s_p.at[0], r_p.at[S], above).wait_recv()
+        add_into(gx_o, pr.at[S], 64)
+
+    def post(i, carry):
+        at = ds(i * cr, cr, 16)
+        x = x_ref[at].astype(F32)
+        inv = inv_rms(x)
+        gx_o[at] = back(x * inv, inv, gx_o[at])
+        return carry
+
+    lax.fori_loop(0, 4, post, 0)
+    for k in range(S):
+        fq(k).wait_recv()
     full = [jnp.concatenate([agq[k, 0], agq[k, 1]], axis=1) for k in range(S)]
     cols = []
     for c in range(3):
         row = jnp.concatenate([full[k][:, c * hw : (c + 1) * hw] for k in range(S)], axis=1)
         cols.append(row[:, :D])
     qkv_o[...] = jnp.concatenate(cols, axis=1)
-    for j in range(-1, S - 1):
-        fq(j).wait_send()
-    for j in range(S - 1):
-        aq(j).wait_send()
-    for i in range(n):
-        own, raw, oth, _ = pieces[i]
-        toward(i, True).wait_send()
-
-        @pl.when(has_outer)
-        def _():
-            returned(i, True).wait_send()
-
-        local_out(i, raw).wait()
-        remote_out(i, raw).wait()
-
-
-def fourth(S, FS, hp, vec, du, dd, dout, dqkv):
+    for k in range(2, 5):
+        step(n + k)
+    for k in range(S):
+        fq(k).wait_send()
+
+        @pl.when(z != k)
+        def _():
+            go_up(k).wait_send()
+
+    for t in range(S - 1):
+        @pl.when((z < S - 1) & (z - t >= 0))
+        def _():
+            a_up(t, z).wait_send()
+
+        @pl.when((z > 0) & (z + t < S))
+        def _():
+            a_down(t, z).wait_send()
+
+    drain()
+
+
+def fourth(S, FS, hp, vec, x, gh1, ps, du, dd, dout, dqkv):
+    tok = x.shape[0]
     fl = du.shape[1]
     rows = D // FS
-    hl = dd.shape[0]
     hw = hp * HEAD
     w2 = 3 * hw // 2
     dh = D // 2
-    n = 5 + 2 * FS
+    n = 4 + 2 * FS
     sds = jax.ShapeDtypeStruct
-    outs = [sds((rows, 2 * FS * fl), BF), sds((2 * hl, D), BF), sds((rows, D), BF), sds((rows, 3 * D), BF),
+    outs = [sds((rows, 2 * FS * fl), BF), sds((2, dd.shape[0] // 2, D), BF), sds((rows, D), BF), sds((tok, D), F32), sds((rows, 3 * D), BF),
             sds(vec.shape, F32), sds((S,) + vec.shape, F32)]
     dma = lambda k: pltpu.SemaphoreType.DMA((k,))
     F1 = FS - 1
-    u, d, o = pltpu.VMEM((FS, rows, fl), BF), pltpu.VMEM((hl, D), BF), pltpu.VMEM((rows, dh), BF)
+    u, o = pltpu.VMEM((FS, rows, fl), BF), pltpu.VMEM((rows, dh), BF)
+    hd = pltpu.VMEM((dd.shape[0] // 2, D), BF)
     v = pltpu.VMEM(vec.shape, F32)
     return pl.pallas_call(
         lambda *refs: fourth_kernel(S, FS, hp, *refs),
         out_shape=outs,
-        in_specs=[VM] + [ANY] * 4,
-        out_specs=[ANY, ANY, ANY, VM, VM, VM],
+        in_specs=[VM] * 3 + [ANY] * 5,
+        out_specs=[ANY, ANY, ANY, VM, VM, VM, VM],
         scratch_shapes=[
-            u, u, u, d, d, d, o, o, o, o, pltpu.VMEM((F1, rows, dh), BF),
+            u, u, u, hd, hd, hd, o, o, o, o, pltpu.VMEM((F1, rows, dh), BF),
             pltpu.VMEM((rows, w2), BF), pltpu.VMEM((F1, rows, w2), BF), pltpu.VMEM((S, 2, rows, w2), BF),
+            pltpu.VMEM((S, tok, D), BF), pltpu.VMEM((S + 1, tok, D), BF),
             v, v, pltpu.VMEM((FS,) + vec.shape, F32), pltpu.VMEM((S,) + vec.shape, F32),
-            dma(4), dma(F1), dma(F1), dma(F1), dma(F1), dma(F1), dma(F1), dma(n), dma(n), dma(n), dma(n),
-            dma(S), dma(S), dma(S), dma(S), dma(FS + S), dma(FS + S), dma(n), dma(n), dma(n),
-        ],
+            dma(5), dma(F1), dma(F1), dma(F1), dma(F1), dma(F1), dma(F1),
+            dma(S), dma(S), dma(S), dma(S), dma(S), dma(S), dma(FS + S), dma(FS + S), dma(S), dma(S + 1),
+        ] + [dma(n)] * 7,
         compiler_params=pltpu.CompilerParams(collective_id=4, has_side_effects=True, vmem_limit_bytes=60 * 2**20),
         name="fourth",
-    )(vec, du, dd, dout, dqkv)
+    )(vec, x, gh1, ps, du, dd, dout, dqkv)
 
 
 def body(S, FS, inputs, segments, w_qkv, w_out, w_upgate, w_down, s_qk, alpha_attn, alpha_mlp, s_up, s_gate, cotangent):
@@ -1075,13 +1237,16 @@
     su = lax.dynamic_slice_in_dim(s_up, f * fl, fl).reshape(1, fl)
     sg = lax.dynamic_slice_in_dim(s_gate, f * fl, fl).reshape(1, fl)
     out, g_mid, du, dd, d_mlp, d_su, d_sg = second(S, FS, mid, cotangent[0], w_down, su, sg, alpha_mlp, wu, w_upgate)
-    g_x, dout, dqkv, d_attn, d_sqk = third(S, FS, hp, g_mid, x, attn, alpha_attn, mine, seg, gain, wo, wq, qkv, raw, res, hall)
+    gh1, ps, dout, dqkv, dn_a, d_attn, d_sqk = third(
+        S, FS, hp, g_mid, x, attn, alpha_attn, mine, seg, gain, wo, wq, qkv, raw, res, hall, dd
+    )
 
     def row(v):
         return jnp.pad(v.reshape(1, -1), ((0, 0), (0, D - v.size)))
 
     vec = jnp.concatenate([row(d_mlp), row(d_attn), row(d_sqk), row(d_su), row(d_sg), jnp.zeros((3, D), F32)])
-    d_up, d_down, d_o, d_q, tot, parts = fourth(S, FS, hp, vec, du, dd, dout, dqkv)
+    d_up, dn_b, d_o, g_x, d_q, tot, parts = fourth(S, FS, hp, vec, x, gh1, ps, du, dd, dout, dqkv)
+    d_down = jnp.concatenate([dn_a[0], dn_b[0], dn_a[1], dn_b[1]])
     sqk = parts[:, 2, :hw].reshape(-1)
 
     def own(v):

time: 507 us -> 486 us (0.959)
  Pallas kernels: 472 us -> 454 us
    pallas_call x1, Pallas kernels: 104 us -> 75.2 us  [third(): pl.pallas_call(lambda *refs: third_kernel(S, FS, hp, *refs), out_shape=ou...]
    pallas_call x1, Pallas kernels: 175 us -> 186 us  [fourth(): pl.pallas_call(lambda *refs: fourth_kernel(S, FS, hp, *refs), out_shape=o...]
where the time goes in v5:
time: 486 us
  Pallas kernels  454 us (93%)
  local copies, waits for them, and re-layouts  17.4 us (4%)
  other arithmetic  13.4 us (3%)
    pallas_call x1, Pallas kernels, fourth(): pl.pallas_call(lambda *refs: fourth_kernel(S, FS, hp, *refs), out_shape=o...  186 us
    pallas_call x1, Pallas kernels, second(): pl.pallas_call(lambda *refs: second_kernel(S, FS, NC, *refs), out_shape=o...  103 us
    pallas_call x1, Pallas kernels, first(): pl.pallas_call(lambda *refs: first_kernel(S, FS, hp, *refs), out_shape=ou...  90.6 us
    pallas_call x1, Pallas kernels, third(): pl.pallas_call(lambda *refs: third_kernel(S, FS, hp, *refs), out_shape=ou...  75.2 us

profile of v5, /device:TPU:0, one launch (start us, length us, event | category | flops | bytes accessed | tf_op | source)
XLA Modules:
  0.0 485.8 jit_solution(13751859436840350174)
XLA Ops:
  0.6 0.8 dynamic_slice.22
  1.4 0.7 reshape.43.refs_5_.refs_7_
  2.1 1.7 copy.23.refs_1_.refs_5_
  3.8 1.3 reshape.44.refs_6_.refs_3_
  5.1 90.6 %first.1 = (bf16[4,256,1280]{2,1,0:T(8,128)(2,1)}, bf16[1280,960]{1,0:T(8,128)(2,1)}, bf16[1280,1280]{1,0:T(8,128)(2,1)}, bf16[2,4,320,1280]{3,2,1,0:T(8,128)(2,...) custom-call(bf16[256,1280]{1,0:T(8,128)(2,1)} %bitcast.15, ...), custom_call_target="tpu_custom_call" | custom-call | tf_op jit(solution)/shard_map/first/pallas_call | solution.py:306
  95.7 0.8 dynamic_slice.23
  96.5 0.6 reshape.45.refs_3_
  97.1 0.8 dynamic_slice.24
  99.1 102.6 %second.1 = (bf16[256,1280]{1,0:T(8,128)(2,1)}, f32[256,1280]{1,0:T(8,128)}, bf16[1280,1280]{1,0:T(8,128)(2,1)}, bf16[640,1280]{1,0:T(8,128)(2,1)}, f32[1,1280]{...) custom-call(f32[256,1280]{1,0:T(8,128)} %get-tuple-element.42.refs_0_, bf16[256,1280]{1,0:T(8,128)(2,1)} %bitcast.19, ...), custom_call_target="tpu_custom_call" | custom-call | tf_op jit(solution)/shard_map/second/pallas_call | solution.py:590
  201.7 75.2 %third.1 = (f32[256,1280]{1,0:T(8,128)}, bf16[4,256,1280]{2,1,0:T(8,128)(2,1)}, bf16[1280,640]{1,0:T(8,128)(2,1)}, bf16[1280,480]{1,0:T(8,128)(2,1)}, bf16[2,320...) custom-call(f32[256,1280]{1,0:T(8,128)} %get-tuple-element.46.refs_0_, bf16[256,1280]{1,0:T(8,128)(2,1)} %bitcast.16, ...), custom_call_target="tpu_custom_call" | custom-call | tf_op jit(solution)/shard_map/third/pallas_call | solution.py:896
  276.9 0.8 reshape.48
  277.7 1.4 concatenate.6.refs_0_
  279.0 185.9 %fourth.1 = (bf16[320,10240]{1,0:T(8,128)(2,1)}, bf16[2,320,1280]{2,1,0:T(8,128)(2,1)}, bf16[320,1280]{1,0:T(8,128)(2,1)}, f32[256,1280]{1,0:T(8,128)}, bf16[320...) custom-call(f32[8,1280]{1,0:T(8,128)} %concatenate.6.refs_0_, bf16[256,1280]{1,0:T(8,128)(2,1)} %bitcast.17, ...), custom_call_target="tpu_custom_call" | custom-call | tf_op jit(solution)/shard_map/fourth/pallas_call | solution.py:1206
  464.9 1.6 slice_reduce_fusion.1
  466.5 0.7 dynamic-slice_reduce_fusion
  467.2 1.8 slice_bitcast_fusion.2
  468.9 3.0 maximum_convert_fusion
  472.0 6.5 %convert_element_type.16 = f32[320,10240]{1,0:T(8,128)} convert(bf16[320,10240]{1,0:T(8,128)(2,1)S(1)} %bitcast.14) | non-fusion elementwise | flops 3276800 | bytes 19660800 | tf_op jit(solution)/shard_map/convert_element_type | solution.py:1256
  478.5 2.6 convert_element_type.14
  481.1 1.3 convert_element_type.15
  482.4 0.8 slice_reduce_fusion
  483.3 0.7 dynamic_slice.25
  483.9 0.8 copy.27
  484.8 1.1 copy.28
  (28 shorter events, 1.3 us)
Async XLA Ops:
  5.1 93.4 %copy-start.5 = (f32[1280]{0:T(1024)S(1)}, f32[1280]{0:T(1024)}, u32[]{:S(2)}) copy-start(f32[1280]{0:T(1024)} %param.20) | copy-start | bytes 15364
  201.7 76.0 %copy-start.6 = (f32[1,1280]{1,0:T(1,128)S(1)}, f32[1,1280]{1,0:T(1,128)}, u32[]{:S(2)}) copy-start(f32[1,1280]{1,0:T(1,128)} %get-tuple-element.45) | copy-start | bytes 15364
  201.7 76.0 %copy-start.7 = (f32[1,1280]{1,0:T(1,128)S(1)}, f32[1,1280]{1,0:T(1,128)}, u32[]{:S(2)}) copy-start(f32[1,1280]{1,0:T(1,128)} %get-tuple-element.58) | copy-start | bytes 15364
  201.7 76.0 %copy-start.8 = (f32[1,1280]{1,0:T(1,128)S(1)}, f32[1,1280]{1,0:T(1,128)}, u32[]{:S(2)}) copy-start(f32[1,1280]{1,0:T(1,128)} %get-tuple-element.59) | copy-start | bytes 15364
  279.0 188.1 %copy-start.1 = (bf16[2,320,1280]{2,1,0:T(8,128)(2,1)S(1)}, bf16[2,320,1280]{2,1,0:T(8,128)(2,1)}, u32[]{:S(2)}) copy-start(bf16[2,320,1280]{2,1,0:T(8,128)(2,1)} %get-tuple-element.69) | copy-start | bytes 4915204
  467.1 4.8 slice-start
  468.9 3.0 slice-start.1
  471.9 6.6 %copy-start = (bf16[320,3840]{1,0:T(8,128)(2,1)S(1)}, bf16[320,3840]{1,0:T(8,128)(2,1)}, u32[]{:S(2)}) copy-start(bf16[320,3840]{1,0:T(8,128)(2,1)} %get-tuple-element.66) | copy-start | bytes 7372804
  478.5 2.6 copy-start.3
  478.5 5.4 %copy-start.4 = (bf16[256,1280]{1,0:T(8,128)(2,1)S(1)}, bf16[256,1280]{1,0:T(8,128)(2,1)}, u32[]{:S(2)}) copy-start(bf16[256,1280]{1,0:T(8,128)(2,1)} %get-tuple-element.44) | copy-start | bytes 1966084
  481.1 3.7 copy-start.2

commit v6 on v5

--- a/solution.py
+++ b/solution.py
@@ -70,16 +70,17 @@
     lax.fori_loop(0, src.shape[0] // chunk, one, 0)
 
 
-def attn_bias(S, tok, half, bias, segc, segr):
+def attn_bias(S, tok, half, bias, segr):
     for qb in range(S):
         q0 = qb * tok
+        column = jnp.transpose(jnp.broadcast_to(segr[:, q0 : q0 + tok], (128, tok)))[:, :1]
         k0 = q0 if q0 < half else half
         nk = q0 + tok - k0
-        ok = visible(segc[q0 : q0 + tok], segr[:, k0 : k0 + nk], q0, k0, tok, nk)
+        ok = visible(column, segr[:, k0 : k0 + nk], q0, k0, tok, nk)
         bias[qb, :, :nk] = jnp.where(ok, 0.0, neg_big).astype(BF)
 
 
-def first_kernel(S, FS, hp, x_ref, segc, segr, wqkv, wout, gain, alpha, wup,
+def first_kernel(S, FS, hp, x_ref, segr, wqkv, wout, par, wup,
                  hall_o, wq_o, wo_o, wu_o, raw_o, qkv_o, res_o, mine_o, attn_o, mid_o,
                  hall, wq, wo, raw, qkv, res, bias, oh, mixs, mine, recv,
                  s_up, r_up, s_dn, r_dn, s_wq, r_wq, s_wo, r_wo, s_wu, r_wu, f_wq, f_wo, f_wu,
@@ -136,7 +137,7 @@
     c_wq = [rcopy(wq_half(f, g), wq_half(f, g), s_wq.at[i], r_wq.at[i], (g, z, p)) for i, p in enumerate(fpeers)]
     for c in c_wq:
         c.start()
-    attn_bias(S, tok, half, bias, segc, segr)
+    attn_bias(S, tok, half, bias, segr)
     wo[ds(f * rows, rows, 16)] = wout[...]
     qkv[2, :, :, HEAD:] = jnp.where(lax.broadcasted_iota(jnp.int32, (hp, total, HEAD), 2) == 0, 1.0, 0.0).astype(BF)
 
@@ -188,7 +189,7 @@
                 for c in range(2):
                     v = acc[:, c * hw + j * HEAD : c * hw + (j + 1) * HEAD]
                     raw[j, at, c * HEAD : (c + 1) * HEAD] = v
-                    u = v * inv_rms(v) * gain[j : j + 1]
+                    u = v * inv_rms(v) * par[2:3, j * HEAD : (j + 1) * HEAD]
                     qkv[c, j, at, :HEAD] = u.astype(BF)
                 qkv[2, j, at, :HEAD] = acc[:, 2 * hw + j * HEAD : 2 * hw + (j + 1) * HEAD].astype(BF)
 
@@ -263,7 +264,7 @@
     mine_o[...] = mine[...]
     x = x_ref[...].astype(F32)
     h = x * inv_rms(x)
-    n_ = h + alpha[...] * (attn * inv_rms(attn) - h)
+    n_ = h + par[0:1] * (attn * inv_rms(attn) - h)
     mid_o[...] = n_ * inv_rms(n_)
 
     for t in range(S - 1):
@@ -290,7 +291,7 @@
         c.wait()
 
 
-def first(S, FS, hp, x, seg, wqkv, wout, gain, alpha, wup):
+def first(S, FS, hp, x, seg, wqkv, wout, par, wup):
     tok, total = x.shape[0], seg.shape[0]
     rows = wqkv.shape[0]
     hw = hp * HEAD
@@ -306,7 +307,7 @@
     return pl.pallas_call(
         lambda *refs: first_kernel(S, FS, hp, *refs),
         out_shape=outs,
-        in_specs=[VM] * 7 + [ANY],
+        in_specs=[VM] * 5 + [ANY],
         out_specs=[ANY] * 7 + [VM] * 3,
         scratch_shapes=[
             pltpu.VMEM((S, tok, D), BF), pltpu.VMEM((D, 3 * hw), BF), pltpu.VMEM((D, D), BF),
@@ -319,11 +320,11 @@
         ],
         compiler_params=pltpu.CompilerParams(collective_id=1, has_side_effects=True, vmem_limit_bytes=60 * 2**20),
         name="first",
-    )(x, seg.reshape(total, 1), seg.reshape(1, total), wqkv, wout, gain, alpha.reshape(1, D), wup)
-
-
-def second_kernel(S, FS, NC, mid, cot, wd, su, sg, alpha, wu_i, wup,
-                  out_o, gmid_o, du_o, dd_o, dal_o, dsu_o, dsg_o,
+    )(x, seg.reshape(1, total), wqkv, wout, par, wup)
+
+
+def second_kernel(S, FS, NC, mid, cot, wd, par, wu_i, wup,
+                  out_o, gmid_o, du_o, dd_o, vec_o,
                   wu, mida, up, gate, hid, ps, pr, rl, gma, gu, dup, ddn, lu, ld,
                   s_a, r_a, s_b, r_b, s_c, r_c, s_d, r_d, w_sem, s_x, r_x, out_sem):
     g, z, f = lax.axis_index("grp"), lax.axis_index("seq"), lax.axis_index("fsdp")
@@ -444,9 +445,7 @@
                     loads.append(pltpu.make_async_copy(wu_i.at[k, peers[i]], wu.at[k, ds(peers[i] * rows, rows, 16)], w_sem.at[k, i + 1]))
             for ld_c in loads:
                 ld_c.start()
-            dsu_o[...] = jnp.zeros_like(dsu_o)
-            dsg_o[...] = jnp.zeros_like(dsg_o)
-            dal_o[...] = jnp.zeros_like(dal_o)
+            vec_o[...] = jnp.zeros_like(vec_o)
         g_relay(mida, s_a, r_a, c)
     for ld_c in loads:
         ld_c.wait()
@@ -461,8 +460,8 @@
             gt = mm(a_in, wu[1, :, cols])
             up[c, :, cols] = u
             gate[c, :, cols] = gt
-            a = gt * sg[:, cols]
-            hid[c, :, cols] = (u * su[:, cols] * (a * jax.nn.sigmoid(a))).astype(BF)
+            a = gt * par[4:5, cols]
+            hid[c, :, cols] = (u * par[3:4, cols] * (a * jax.nn.sigmoid(a))).astype(BF)
             return carry
 
         lax.fori_loop(0, fl // nt, fwd, 0)
@@ -481,7 +480,7 @@
     for c in range(NC):
         at = slice(c * ct, (c + 1) * ct)
         mlp = s_total(s_b, r_b, c)
-        al = alpha[...]
+        al = par[1:2]
         md = mid[at]
         inv_m = inv_rms(mlp)
         um = mlp * inv_m
@@ -491,7 +490,7 @@
         o = m * inv_o
         out_o[at] = o.astype(BF)
         g_m = back(o, inv_o, cot[at].astype(F32))
-        dal_o[...] += jnp.sum(g_m * dif, axis=0, keepdims=True)
+        vec_o[0:1] += jnp.sum(g_m * dif, axis=0, keepdims=True)
         gmid_o[at] = (1 - al) * g_m
         gma[c, f] = back(um, inv_m, al * g_m).astype(BF)
         g_issue(gma, s_c, r_c, c)
@@ -505,16 +504,16 @@
             gh = mm_nt(gma[c].reshape(M, D), wd[cols, :])
             u = up[c, :, cols]
             gt = gate[c, :, cols]
-            sgc = sg[:, cols]
-            suc = su[:, cols]
+            sgc = par[4:5, cols]
+            suc = par[3:4, cols]
             a = gt * sgc
             sig = jax.nn.sigmoid(a)
             gs = gh * (a * sig)
             gu[0, c, :, cols] = (gs * suc).astype(BF)
-            dsu_o[:, cols] += jnp.sum(u * gs, axis=0, keepdims=True)
+            vec_o[3:4, cols] += jnp.sum(u * gs, axis=0, keepdims=True)
             g_a = gh * u * suc * (sig * (1 + a * (1 - sig)))
             gu[1, c, :, cols] = (g_a * sgc).astype(BF)
-            dsg_o[:, cols] += jnp.sum(gt * g_a, axis=0, keepdims=True)
+            vec_o[4:5, cols] += jnp.sum(gt * g_a, axis=0, keepdims=True)
             return carry
 
         lax.fori_loop(0, fl // nt, bwd, 0)
@@ -576,7 +575,7 @@
     o_u.wait()
 
 
-def second(S, FS, mid, cot, wd, su, sg, alpha, wu, wup):
+def second(S, FS, mid, cot, wd, par, wu, wup):
     NC = 2
     tok = mid.shape[0]
     ct = tok // NC
@@ -584,14 +583,14 @@
     M = FS * ct
     sds = jax.ShapeDtypeStruct
     outs = [sds((tok, D), BF), sds((tok, D), F32), sds((D, fl), BF), sds((fl // 2, D), BF),
-            sds((1, D), F32), sds((1, fl), F32), sds((1, fl), F32)]
+            sds((8, D), F32)]
     dma = pltpu.SemaphoreType.DMA
     F1 = FS - 1
     return pl.pallas_call(
         lambda *refs: second_kernel(S, FS, NC, *refs),
         out_shape=outs,
-        in_specs=[VM] * 6 + [ANY] * 2,
-        out_specs=[VM, VM, ANY, ANY, VM, VM, VM],
+        in_specs=[VM] * 4 + [ANY] * 2,
+        out_specs=[VM, VM, ANY, ANY, VM],
         scratch_shapes=[
             pltpu.VMEM((2, D, fl), BF), pltpu.VMEM((NC, FS, ct, D), BF), pltpu.VMEM((NC, M, fl), F32),
             pltpu.VMEM((NC, M, fl), F32), pltpu.VMEM((NC, M, fl), BF), pltpu.VMEM((NC, FS, ct, D), BF),
@@ -601,7 +600,7 @@
         ] + [dma((NC, max(F1, 6)))] * 8 + [dma((2, FS)), dma((2,)), dma((2,)), dma((2,))],
         compiler_params=pltpu.CompilerParams(collective_id=2, has_side_effects=True, vmem_limit_bytes=63 * 2**20),
         name="second",
-    )(mid, cot, wd, su, sg, alpha.reshape(1, D), wu, wup)
+    )(mid, cot, wd, par, wu, wup)
 
 
 def make_chain(S, pieces, outs, sems):
@@ -701,9 +700,9 @@
     return [(a * step, (b - a) * step) for a, b in zip(parts[:-1], parts[1:])]
 
 
-def third_kernel(S, FS, hp, gmid, x_ref, attn, alpha, mine, segc, segr, gain, wo, wq_i, qkv_i, raw_i, res_i, hall_i, dd_i,
-                 gh1, ps_o, dout_o, dqkv_o, dn_o, dal_o, dsq_o,
-                 wq, qkv, raw, res, hall, ga, gsend, gxr, bias, hx, gqh, dkv, gq, ps, dout, dqk, lo, lq, own_d, raw_d, oth_d,
+def third_kernel(S, FS, hp, gmid, x_ref, attn, mine, segr, par, wo, wq_i, qkv_i, raw_i, res_i, hall_i, dd_i,
+                 gh1, ps_o, dout_o, dqkv_o, dn_o, vec_o,
+                 dsq_o, gain, wq, qkv, raw, res, hall, ga, gsend, gxr, bias, hx, gqh, dkv, gq, ps, dout, dqk, lo, lq, own_d, raw_d, oth_d,
                  ld_sem, h_sem, s_gx, r_gx, s_p, s_x, r_x, out_sem, *chain_sems):
     g, z, f = lax.axis_index("grp"), lax.axis_index("seq"), lax.axis_index("fsdp")
     tok = x_ref.shape[0]
@@ -737,7 +736,9 @@
     h_tile(1).start()
     dd_c.wait()
     launch(0)
-    dal_o[...] = jnp.zeros_like(dal_o)
+    vec_o[...] = jnp.zeros_like(vec_o)
+    for j in range(hp):
+        gain[j : j + 1] = par[2:3, j * HEAD : (j + 1) * HEAD]
     dsq_o[...] = jnp.zeros_like(dsq_o)
     cr = tok // 4
 
@@ -748,12 +749,12 @@
         av = attn[at]
         inv_a = inv_rms(av)
         ua = av * inv_a
-        al = alpha[...]
+        al = par[0:1]
         dif = ua - h
         n_ = h + al * dif
         inv_n = inv_rms(n_)
         g_n = back(n_ * inv_n, inv_n, gmid[at])
-        dal_o[...] += jnp.sum(g_n * dif, axis=0, keepdims=True)
+        vec_o[1:2] += jnp.sum(g_n * dif, axis=0, keepdims=True)
         gh1[at] = (1 - al) * g_n
         ga[at] = back(ua, inv_a, al * g_n).astype(BF)
         return carry
@@ -788,7 +789,7 @@
     lax.fori_loop(0, D // 256, dwo, 0)
     x_o = rcopy(dout.at[1 - g], lo, s_x.at[0], r_x.at[0], partner)
     x_o.start()
-    attn_bias(S, tok, half, bias, segc, segr)
+    attn_bias(S, tok, half, bias, segr)
     for c in loads:
         c.wait()
     done = 0
@@ -864,6 +865,8 @@
     add_into(dout.at[g], lo, 128)
     o_o = pltpu.make_async_copy(dout.at[g], dout_o, out_sem.at[0])
     o_o.start()
+    for j in range(hp):
+        vec_o[2:3, j * HEAD : (j + 1) * HEAD] = dsq_o[j : j + 1]
     while done < n_p + 5:
         step(done)
         done += 1
@@ -885,20 +888,21 @@
     drain()
 
 
-def third(S, FS, hp, gmid, x, attn, alpha, mine, seg, gain, wo, wq, qkv, raw, res, hall, dd):
+def third(S, FS, hp, gmid, x, attn, mine, seg, par, wo, wq, qkv, raw, res, hall, dd):
     tok, total = x.shape[0], seg.shape[0]
     hw = hp * HEAD
     sds = jax.ShapeDtypeStruct
     outs = [sds((tok, D), F32), sds((S, tok, D), BF), sds((D, D // 2), BF), sds((D, 3 * hw // 2), BF), sds((2, dd.shape[0] // 2, D), BF),
-            sds((1, D), F32), sds((hp, HEAD), F32)]
+            sds((8, D), F32)]
     dma = lambda n: pltpu.SemaphoreType.DMA((n,))
     hd = pltpu.VMEM((dd.shape[0] // 2, D), BF)
     return pl.pallas_call(
         lambda *refs: third_kernel(S, FS, hp, *refs),
         out_shape=outs,
-        in_specs=[VM] * 9 + [ANY] * 6,
-        out_specs=[VM, ANY, ANY, ANY, ANY, VM, VM],
+        in_specs=[VM] * 7 + [ANY] * 6,
+        out_specs=[VM, ANY, ANY, ANY, ANY, VM],
         scratch_shapes=[
+            pltpu.VMEM((hp, HEAD), F32), pltpu.VMEM((hp, HEAD), F32),
             pltpu.VMEM((D, 3 * hw), BF), pltpu.VMEM((3, hp, total, 2 * HEAD), BF), pltpu.VMEM((hp, total, 2 * HEAD), F32),
             pltpu.VMEM((hp, total, 2 * HEAD), F32), pltpu.VMEM((2, S, tok, 256), BF),
             pltpu.VMEM((tok, D), BF), pltpu.VMEM((S, tok, hw), BF), pltpu.VMEM((S, tok, hw), BF),
@@ -911,10 +915,10 @@
         ] + [dma(5)] * 7,
         compiler_params=pltpu.CompilerParams(collective_id=3, has_side_effects=True, vmem_limit_bytes=63 * 2**20),
         name="third",
-    )(gmid, x, attn, alpha.reshape(1, D), mine, seg.reshape(total, 1), seg.reshape(1, total), gain, wo, wq, qkv, raw, res, hall, dd)
-
-
-def fourth_kernel(S, FS, hp, vec, x_ref, gh1, ps_i, du, dd, dout, dqkv,
+    )(gmid, x, attn, mine, seg.reshape(1, total), par, wo, wq, qkv, raw, res, hall, dd)
+
+
+def fourth_kernel(S, FS, hp, vec, vec2, x_ref, gh1, ps_i, du, dd, dout, dqkv,
                   up_o, dn_o, out_o, gx_o, qkv_o, vec_o, sqk_o,
                   own_u, raw_u, oth_u, own_d, raw_d, oth_d, own_o, raw_o, oth_o, so, xo, sq, xq, agq, ps, pr, va, vb, vf, vz,
                   ld_sem, s_u, r_u, s_xo, r_xo, s_xq, r_xq, s_au, r_au, s_ad, r_ad, s_fq, r_fq, s_v, r_v,
@@ -951,7 +955,7 @@
     c_o = [rcopy(dout.at[blk(p)], xo.at[i], s_xo.at[i], r_xo.at[i], (g, z, p)) for i, p in enumerate(peers)]
     for c in c_q + c_u + c_o:
         c.start()
-    va[...] = vec[...]
+    va[...] = vec[...] + vec2[...]
     v_c = rcopy(va, vb, s_v.at[0], r_v.at[0], partner)
     v_c.start()
 
@@ -1069,57 +1073,71 @@
     launch(1)
     l_p.wait()
     gh_end(0)
-    step(0)
     v_c.wait()
     vf[f] = va[...] + vb[...]
     v_f = [rcopy(vf.at[f], vf.at[f], s_v.at[1 + i], r_v.at[1 + i], (g, z, p)) for i, p in enumerate(peers)]
     for c in v_f:
         c.start()
-    step(1)
     l_q.wait()
     for c in c_q:
         c.wait()
     agq[z, g] = add_all(sq, xq)
     a_start()
-    gh_mid(1)
     l_u.wait()
+    l_o.wait()
     launch(2)
     launch(3)
-    gh_end(1)
+    ends = first_z | last_z
+    inner = jnp.logical_not(ends)
+
+    def last_piece():
+        for c in c_o:
+            c.wait()
+        own_o[...] = add_all(so, xo)
+
+    @pl.when(ends)
+    def _():
+        for i in R:
+            c_u[i].wait()
+            launch(4 + 2 * i)
+            launch(5 + 2 * i)
+            if 1 + i < S - 2:
+                gh_end(1 + i)
+        last_piece()
+        launch(4 + 2 * len(R))
+        launch(5 + 2 * len(R))
+        gh_end(S - 2)
+
+    step(0)
+    step(1)
+    gh_mid(1)
     step(2)
     step(3)
-    gh_mid(2)
     n = 4
     for i in R:
-        c_u[i].wait()
-        launch(n)
-        launch(n + 1)
-        if 2 + i < S - 1:
-            gh_end(2 + i)
+        if i < S - 1:
+            a_relay(i)
+
+        @pl.when(inner)
+        def _():
+            c_u[i].wait()
+
         step(n)
         step(n + 1)
         n += 2
-        if 3 + i < S - 1:
-            gh_mid(3 + i)
-        if i < S - 1:
-            a_relay(i)
-        if i == 0:
-            for c in v_f:
-                c.wait()
-            acc = vf[0]
-            for k in range(1, FS):
-                acc = acc + vf[k]
-            sub = lax.broadcasted_iota(jnp.int32, acc.shape, 0)
-            vz[z] = jnp.where(sub < 3, acc, vf[f])
-            v_z = [rcopy(vz.at[z], vz.at[z], s_v.at[FS + k], r_v.at[FS + k], (g, p, f)) for k, p in enumerate(zpeers)]
-            for c in v_z:
-                c.start()
-    l_o.wait()
-    for c in c_o:
+        if 2 + i < S - 1:
+            gh_mid(2 + i)
+    for c in v_f:
         c.wait()
-    own_o[...] = add_all(so, xo)
-    launch(n)
-    launch(n + 1)
+    acc = vf[0]
+    for k in range(1, FS):
+        acc = acc + vf[k]
+    sub = lax.broadcasted_iota(jnp.int32, acc.shape, 0)
+    vz[z] = jnp.where(sub < 3, acc, vf[f])
+    v_z = [rcopy(vz.at[z], vz.at[z], s_v.at[FS + k], r_v.at[FS + k], (g, p, f)) for k, p in enumerate(zpeers)]
+    for c in v_z:
+        c.start()
+    pl.when(inner)(last_piece)
     step(n)
     step(n + 1)
     n += 2
@@ -1187,7 +1205,7 @@
     drain()
 
 
-def fourth(S, FS, hp, vec, x, gh1, ps, du, dd, dout, dqkv):
+def fourth(S, FS, hp, vec, vec2, x, gh1, ps, du, dd, dout, dqkv):
     tok = x.shape[0]
     fl = du.shape[1]
     rows = D // FS
@@ -1206,7 +1224,7 @@
     return pl.pallas_call(
         lambda *refs: fourth_kernel(S, FS, hp, *refs),
         out_shape=outs,
-        in_specs=[VM] * 3 + [ANY] * 5,
+        in_specs=[VM] * 4 + [ANY] * 5,
         out_specs=[ANY, ANY, ANY, VM, VM, VM, VM],
         scratch_shapes=[
             u, u, u, hd, hd, hd, o, o, o, o, pltpu.VMEM((F1, rows, dh), BF),
@@ -1218,7 +1236,7 @@
         ] + [dma(n)] * 7,
         compiler_params=pltpu.CompilerParams(collective_id=4, has_side_effects=True, vmem_limit_bytes=60 * 2**20),
         name="fourth",
-    )(vec, x, gh1, ps, du, dd, dout, dqkv)
+    )(vec, vec2, x, gh1, ps, du, dd, dout, dqkv)
 
 
 def body(S, FS, inputs, segments, w_qkv, w_out, w_upgate, w_down, s_qk, alpha_attn, alpha_mlp, s_up, s_gate, cotangent):
@@ -1232,20 +1250,21 @@
     x = inputs[0]
     seg = segments[0]
     gains = jnp.pad(s_qk, (0, S * hw - D))
-    gain = lax.dynamic_slice_in_dim(gains, z * hw, hw).reshape(hp, HEAD)
-    hall, wq, wo, wu, raw, qkv, res, mine, attn, mid = first(S, FS, hp, x, seg, w_qkv, w_out, gain, alpha_attn, w_upgate)
-    su = lax.dynamic_slice_in_dim(s_up, f * fl, fl).reshape(1, fl)
-    sg = lax.dynamic_slice_in_dim(s_gate, f * fl, fl).reshape(1, fl)
-    out, g_mid, du, dd, d_mlp, d_su, d_sg = second(S, FS, mid, cotangent[0], w_down, su, sg, alpha_mlp, wu, w_upgate)
-    gh1, ps, dout, dqkv, dn_a, d_attn, d_sqk = third(
-        S, FS, hp, g_mid, x, attn, alpha_attn, mine, seg, gain, wo, wq, qkv, raw, res, hall, dd
+
+    def row(v):
+        return jnp.pad(v, (0, D - v.size))
+
+    par = jnp.stack([
+        alpha_attn, alpha_mlp, row(lax.dynamic_slice_in_dim(gains, z * hw, hw)),
+        row(lax.dynamic_slice_in_dim(s_up, f * fl, fl)), row(lax.dynamic_slice_in_dim(s_gate, f * fl, fl)),
+    ])
+    par = jnp.pad(par, ((0, 3), (0, 0)))
+    hall, wq, wo, wu, raw, qkv, res, mine, attn, mid = first(S, FS, hp, x, seg, w_qkv, w_out, par, w_upgate)
+    out, g_mid, du, dd, vec = second(S, FS, mid, cotangent[0], w_down, par, wu, w_upgate)
+    gh1, ps, dout, dqkv, dn_a, vec2 = third(
+        S, FS, hp, g_mid, x, attn, mine, seg, par, wo, wq, qkv, raw, res, hall, dd
     )
-
-    def row(v):
-        return jnp.pad(v.reshape(1, -1), ((0, 0), (0, D - v.size)))
-
-    vec = jnp.concatenate([row(d_mlp), row(d_attn), row(d_sqk), row(d_su), row(d_sg), jnp.zeros((3, D), F32)])
-    d_up, dn_b, d_o, g_x, d_q, tot, parts = fourth(S, FS, hp, vec, x, gh1, ps, du, dd, dout, dqkv)
+    d_up, dn_b, d_o, g_x, d_q, tot, parts = fourth(S, FS, hp, vec, vec2, x, gh1, ps, du, dd, dout, dqkv)
     d_down = jnp.concatenate([dn_a[0], dn_b[0], dn_a[1], dn_b[1]])
     sqk = parts[:, 2, :hw].reshape(-1)
 

time: 486 us -> 479 us (0.986)
  local copies, waits for them, and re-layouts: 17.4 us -> 12.1 us
where the time goes in v6:
time: 479 us
  Pallas kernels  451 us (94%)
  other arithmetic  15.1 us (3%)
  local copies, waits for them, and re-layouts  12.1 us (3%)
    pallas_call x1, Pallas kernels, fourth(): pl.pallas_call(lambda *refs: fourth_kernel(S, FS, hp, *refs), out_shape=o...  182 us
    pallas_call x1, Pallas kernels, second(): pl.pallas_call(lambda *refs: second_kernel(S, FS, NC, *refs), out_shape=o...  103 us
    pallas_call x1, Pallas kernels, first(): pl.pallas_call(lambda *refs: first_kernel(S, FS, hp, *refs), out_shape=ou...  90.8 us
    pallas_call x1, Pallas kernels, third(): pl.pallas_call(lambda *refs: third_kernel(S, FS, hp, *refs), out_shape=ou...  75.2 us

profile of v6, /device:TPU:0, one launch (start us, length us, event | category | flops | bytes accessed | tf_op | source)
XLA Modules:
  0.0 478.7 jit_solution(7117201077056075001)
XLA Ops:
  0.6 0.8 dynamic_slice.22
  1.4 0.7 stack.18
  2.1 0.7 stack.19
  2.8 0.8 dynamic_slice.23
  3.6 0.8 dynamic_slice.24
  4.5 0.6 pad.9.refs_4_.refs_3_.refs_5_
  5.1 90.8 %first.1 = (bf16[4,256,1280]{2,1,0:T(8,128)(2,1)}, bf16[1280,960]{1,0:T(8,128)(2,1)}, bf16[1280,1280]{1,0:T(8,128)(2,1)}, bf16[2,4,320,1280]{3,2,1,0:T(8,128)(2,...) custom-call(bf16[256,1280]{1,0:T(8,128)(2,1)} %bitcast.14, ...), custom_call_target="tpu_custom_call" | custom-call | tf_op jit(solution)/shard_map/first/pallas_call | solution.py:307
  95.9 102.6 %second.1 = (bf16[256,1280]{1,0:T(8,128)(2,1)}, f32[256,1280]{1,0:T(8,128)}, bf16[1280,1280]{1,0:T(8,128)(2,1)}, bf16[640,1280]{1,0:T(8,128)(2,1)}, f32[8,1280]{1,0:T(8,128)}) custom-call(f32[256,1280]{1,0:T(8,128)} %get-tuple-element.39.refs_0_, bf16[256,1280]{1,0:T(8,128)(2,1)} %bitcast.18, bf16[1280,1280]{1,0:T(8,128)(2,1)} %refs_2_.3, ...), custom_call_target="tpu_custom_call" | custom-call | tf_op jit(solution)/shard_map/second/pallas_call | solution.py:589
  198.5 75.2 %third.1 = (f32[256,1280]{1,0:T(8,128)}, bf16[4,256,1280]{2,1,0:T(8,128)(2,1)}, bf16[1280,640]{1,0:T(8,128)(2,1)}, bf16[1280,480]{1,0:T(8,128)(2,1)}, bf16[2,320,1280]{2,1,0:T(8,128)(2,1)}, /*index=5*/f32[8,1280]{1,0:T(8,128)}) custom-call(f32[256,1280]{1,0:T(8,128)} %get-tuple-element.43.refs_0_, bf16[256,1280]{1,0:T(8,128)(2,1)} %bitcast.15, ...), custom_call_target="tpu_custom_call" | custom-call | tf_op jit(solution)/shard_map/third/pallas_call | solution.py:899
  273.7 182.3 %fourth.1 = (bf16[320,10240]{1,0:T(8,128)(2,1)}, bf16[2,320,1280]{2,1,0:T(8,128)(2,1)}, bf16[320,1280]{1,0:T(8,128)(2,1)}, f32[256,1280]{1,0:T(8,128)}, bf16[320...) custom-call(f32[8,1280]{1,0:T(8,128)} %get-tuple-element.42.refs_0_, ...), custom_call_target="tpu_custom_call" | custom-call | tf_op jit(solution)/shard_map/fourth/pallas_call | solution.py:1224
  456.0 0.9 slice_reduce_fusion
  456.9 0.1 reshape_squeeze.3
  457.0 0.7 dynamic_slice.25
  457.7 1.6 slice_reduce_fusion.1
  459.2 0.7 dynamic-slice_reduce_fusion
  459.9 2.4 convert_element_type.17
  462.3 1.8 slice_bitcast_fusion.2
  464.1 0.0 slice-start.1
  464.1 3.6 maximum_convert_fusion
  467.7 2.6 convert_element_type.16
  470.3 0.0 slice-done.1
  470.3 6.5 %convert_element_type.18 = f32[320,10240]{1,0:T(8,128)} convert(bf16[320,10240]{1,0:T(8,128)(2,1)S(1)} %bitcast.13) | non-fusion elementwise | flops 3276800 | bytes 19660800 | tf_op jit(solution)/shard_map/convert_element_type | solution.py:1275
  476.8 0.8 copy.25
  477.7 1.1 copy.26
  (16 shorter events, 0.1 us)
Async XLA Ops:
  456.0 6.4 %copy-start.1 = (bf16[2,320,1280]{2,1,0:T(8,128)(2,1)S(1)}, bf16[2,320,1280]{2,1,0:T(8,128)(2,1)}, u32[]{:S(2)}) copy-start(bf16[2,320,1280]{2,1,0:T(8,128)(2,1)} %get-tuple-element.63) | copy-start | bytes 4915204
  462.3 7.9 %slice-start = ((s8[6553600]{0:T(1024)(128)(4,1)}), s8[4194304]{0:T(1024)(128)(4,1)S(1)}, s32[]{:S(2)}) async-start(s8[6553600]{0:T(1024)(128)(4,1)} %bitcast.12), calls=%async_computation | async-start | bytes 8388608
  464.1 3.6 copy-start
  464.1 6.2 %slice-start.1 = ((s8[6553600]{0:T(1024)(128)(4,1)}), s8[2359296]{0:T(1024)(128)(4,1)S(1)}, s32[]{:S(2)}) async-start(s8[6553600]{0:T(1024)(128)(4,1)} %bitcast.12), calls=%async_computation.1 | async-start | bytes 4718592
  470.3 6.6 %copy-start.3 = (bf16[256,1280]{1,0:T(8,128)(2,1)S(1)}, bf16[256,1280]{1,0:T(8,128)(2,1)}, u32[]{:S(2)}) copy-start(bf16[256,1280]{1,0:T(8,128)(2,1)} %get-tuple-element.41) | copy-start | bytes 1966084
  470.3 7.4 %copy-start.2 = (f32[256,1280]{1,0:T(8,128)S(1)}, f32[256,1280]{1,0:T(8,128)}, u32[]{:S(2)}) copy-start(f32[256,1280]{1,0:T(8,128)} %get-tuple-element.59) | copy-start | bytes 3932164

commit v7 on v6

--- a/solution.py
+++ b/solution.py
@@ -189,7 +189,7 @@
                 for c in range(2):
                     v = acc[:, c * hw + j * HEAD : c * hw + (j + 1) * HEAD]
                     raw[j, at, c * HEAD : (c + 1) * HEAD] = v
-                    u = v * inv_rms(v) * par[2:3, j * HEAD : (j + 1) * HEAD]
+                    u = v * inv_rms(v) * par[:, 2 * D + j * HEAD : 2 * D + (j + 1) * HEAD]
                     qkv[c, j, at, :HEAD] = u.astype(BF)
                 qkv[2, j, at, :HEAD] = acc[:, 2 * hw + j * HEAD : 2 * hw + (j + 1) * HEAD].astype(BF)
 
@@ -264,7 +264,7 @@
     mine_o[...] = mine[...]
     x = x_ref[...].astype(F32)
     h = x * inv_rms(x)
-    n_ = h + par[0:1] * (attn * inv_rms(attn) - h)
+    n_ = h + par[:, :D] * (attn * inv_rms(attn) - h)
     mid_o[...] = n_ * inv_rms(n_)
 
     for t in range(S - 1):
@@ -460,8 +460,8 @@
             gt = mm(a_in, wu[1, :, cols])
             up[c, :, cols] = u
             gate[c, :, cols] = gt
-            a = gt * par[4:5, cols]
-            hid[c, :, cols] = (u * par[3:4, cols] * (a * jax.nn.sigmoid(a))).astype(BF)
+            a = gt * par[:, ds(3 * D + ff + f * fl + t * nt, nt, 128)]
+            hid[c, :, cols] = (u * par[:, ds(3 * D + f * fl + t * nt, nt, 128)] * (a * jax.nn.sigmoid(a))).astype(BF)
             return carry
 
         lax.fori_loop(0, fl // nt, fwd, 0)
@@ -480,7 +480,7 @@
     for c in range(NC):
         at = slice(c * ct, (c + 1) * ct)
         mlp = s_total(s_b, r_b, c)
-        al = par[1:2]
+        al = par[:, D : 2 * D]
         md = mid[at]
         inv_m = inv_rms(mlp)
         um = mlp * inv_m
@@ -504,8 +504,8 @@
             gh = mm_nt(gma[c].reshape(M, D), wd[cols, :])
             u = up[c, :, cols]
             gt = gate[c, :, cols]
-            sgc = par[4:5, cols]
-            suc = par[3:4, cols]
+            sgc = par[:, ds(3 * D + ff + f * fl + t * nt, nt, 128)]
+            suc = par[:, ds(3 * D + f * fl + t * nt, nt, 128)]
             a = gt * sgc
             sig = jax.nn.sigmoid(a)
             gs = gh * (a * sig)
@@ -738,7 +738,7 @@
     launch(0)
     vec_o[...] = jnp.zeros_like(vec_o)
     for j in range(hp):
-        gain[j : j + 1] = par[2:3, j * HEAD : (j + 1) * HEAD]
+        gain[j : j + 1] = par[:, 2 * D + j * HEAD : 2 * D + (j + 1) * HEAD]
     dsq_o[...] = jnp.zeros_like(dsq_o)
     cr = tok // 4
 
@@ -749,7 +749,7 @@
         av = attn[at]
         inv_a = inv_rms(av)
         ua = av * inv_a
-        al = par[0:1]
+        al = par[:, :D]
         dif = ua - h
         n_ = h + al * dif
         inv_n = inv_rms(n_)
@@ -1254,11 +1254,9 @@
     def row(v):
         return jnp.pad(v, (0, D - v.size))
 
-    par = jnp.stack([
-        alpha_attn, alpha_mlp, row(lax.dynamic_slice_in_dim(gains, z * hw, hw)),
-        row(lax.dynamic_slice_in_dim(s_up, f * fl, fl)), row(lax.dynamic_slice_in_dim(s_gate, f * fl, fl)),
-    ])
-    par = jnp.pad(par, ((0, 3), (0, 0)))
+    par = jnp.concatenate([
+        alpha_attn, alpha_mlp, row(lax.dynamic_slice_in_dim(gains, z * hw, hw)), s_up, s_gate
+    ]).reshape(1, -1)
     hall, wq, wo, wu, raw, qkv, res, mine, attn, mid = first(S, FS, hp, x, seg, w_qkv, w_out, par, w_upgate)
     out, g_mid, du, dd, vec = second(S, FS, mid, cotangent[0], w_down, par, wu, w_upgate)
     gh1, ps, dout, dqkv, dn_a, vec2 = third(

time: 479 us -> 479 us (level)
  no operation moved by 1% of the time
where the time goes in v7:
time: 479 us
  Pallas kernels  451 us (94%)
  other arithmetic  15.1 us (3%)
  local copies, waits for them, and re-layouts  11.9 us (2%)
    pallas_call x1, Pallas kernels, fourth(): pl.pallas_call(lambda *refs: fourth_kernel(S, FS, hp, *refs), out_shape=o...  182 us
    pallas_call x1, Pallas kernels, second(): pl.pallas_call(lambda *refs: second_kernel(S, FS, NC, *refs), out_shape=o...  103 us
    pallas_call x1, Pallas kernels, first(): pl.pallas_call(lambda *refs: first_kernel(S, FS, hp, *refs), out_shape=ou...  90.8 us
    pallas_call x1, Pallas kernels, third(): pl.pallas_call(lambda *refs: third_kernel(S, FS, hp, *refs), out_shape=ou...  75.4 us

profile of v7, /device:TPU:0, one launch (start us, length us, event | category | flops | bytes accessed | tf_op | source)
XLA Modules:
  0.0 478.9 jit_solution(9468585773629509445)
XLA Ops:
  0.6 0.8 dynamic_slice.16
  1.4 0.7 constant_dynamic-update-slice_fusion.3
  2.1 0.7 constant_dynamic-update-slice_fusion.2
  2.8 0.7 constant_dynamic-update-slice_fusion.1
  3.6 0.7 constant_dynamic-update-slice_fusion
  4.3 0.7 reshape.27.refs_4_.refs_3_.refs_5_
  5.0 90.8 %first.1 = (bf16[4,256,1280]{2,1,0:T(8,128)(2,1)}, bf16[1280,960]{1,0:T(8,128)(2,1)}, bf16[1280,1280]{1,0:T(8,128)(2,1)}, bf16[2,4,320,1280]{3,2,1,0:T(8,128)(2,...) custom-call(bf16[256,1280]{1,0:T(8,128)(2,1)} %bitcast.14, ...), custom_call_target="tpu_custom_call" | custom-call | tf_op jit(solution)/shard_map/first/pallas_call | solution.py:307
  95.8 102.6 %second.1 = (bf16[256,1280]{1,0:T(8,128)(2,1)}, f32[256,1280]{1,0:T(8,128)}, bf16[1280,1280]{1,0:T(8,128)(2,1)}, bf16[640,1280]{1,0:T(8,128)(2,1)}, f32[8,1280]{1,0:T(8,128)}) custom-call(f32[256,1280]{1,0:T(8,128)} %get-tuple-element.39.refs_0_, bf16[256,1280]{1,0:T(8,128)(2,1)} %bitcast.18, bf16[1280,1280]{1,0:T(8,128)(2,1)} %refs_2_.3, ...), custom_call_target="tpu_custom_call" | custom-call | tf_op jit(solution)/shard_map/second/pallas_call | solution.py:589
  198.4 75.4 %third.1 = (f32[256,1280]{1,0:T(8,128)}, bf16[4,256,1280]{2,1,0:T(8,128)(2,1)}, bf16[1280,640]{1,0:T(8,128)(2,1)}, bf16[1280,480]{1,0:T(8,128)(2,1)}, bf16[2,320,1280]{2,1,0:T(8,128)(2,1)}, /*index=5*/f32[8,1280]{1,0:T(8,128)}) custom-call(f32[256,1280]{1,0:T(8,128)} %get-tuple-element.43.refs_0_, bf16[256,1280]{1,0:T(8,128)(2,1)} %bitcast.15, ...), custom_call_target="tpu_custom_call" | custom-call | tf_op jit(solution)/shard_map/third/pallas_call | solution.py:899
  273.8 182.3 %fourth.1 = (bf16[320,10240]{1,0:T(8,128)(2,1)}, bf16[2,320,1280]{2,1,0:T(8,128)(2,1)}, bf16[320,1280]{1,0:T(8,128)(2,1)}, f32[256,1280]{1,0:T(8,128)}, bf16[320...) custom-call(f32[8,1280]{1,0:T(8,128)} %get-tuple-element.42.refs_0_, ...), custom_call_target="tpu_custom_call" | custom-call | tf_op jit(solution)/shard_map/fourth/pallas_call | solution.py:1224
  456.1 0.9 slice_reduce_fusion
  457.1 0.1 reshape_squeeze.3
  457.1 0.7 dynamic_slice.17
  457.8 1.6 slice_reduce_fusion.1
  459.4 0.7 dynamic-slice_reduce_fusion
  460.0 2.4 convert_element_type.15
  462.5 1.8 slice_bitcast_fusion.2
  464.2 0.0 slice-start.1
  464.2 3.6 maximum_convert_fusion
  467.8 2.6 convert_element_type.14
  470.4 0.0 slice-done.1
  470.4 6.5 %convert_element_type.16 = f32[320,10240]{1,0:T(8,128)} convert(bf16[320,10240]{1,0:T(8,128)(2,1)S(1)} %bitcast.13) | non-fusion elementwise | flops 3276800 | bytes 19660800 | tf_op jit(solution)/shard_map/convert_element_type | solution.py:1273
  477.0 0.8 copy.30
  477.8 1.1 copy.31
  (13 shorter events, 0.0 us)
Async XLA Ops:
  456.1 6.4 %copy-start.1 = (bf16[2,320,1280]{2,1,0:T(8,128)(2,1)S(1)}, bf16[2,320,1280]{2,1,0:T(8,128)(2,1)}, u32[]{:S(2)}) copy-start(bf16[2,320,1280]{2,1,0:T(8,128)(2,1)} %get-tuple-element.63) | copy-start | bytes 4915204
  462.5 7.9 %slice-start = ((s8[6553600]{0:T(1024)(128)(4,1)}), s8[4194304]{0:T(1024)(128)(4,1)S(1)}, s32[]{:S(2)}) async-start(s8[6553600]{0:T(1024)(128)(4,1)} %bitcast.12), calls=%async_computation | async-start | bytes 8388608
  464.2 3.6 copy-start
  464.2 6.2 %slice-start.1 = ((s8[6553600]{0:T(1024)(128)(4,1)}), s8[2359296]{0:T(1024)(128)(4,1)S(1)}, s32[]{:S(2)}) async-start(s8[6553600]{0:T(1024)(128)(4,1)} %bitcast.12), calls=%async_computation.1 | async-start | bytes 4718592
  470.4 6.6 %copy-start.3 = (bf16[256,1280]{1,0:T(8,128)(2,1)S(1)}, bf16[256,1280]{1,0:T(8,128)(2,1)}, u32[]{:S(2)}) copy-start(bf16[256,1280]{1,0:T(8,128)(2,1)} %get-tuple-element.41) | copy-start | bytes 1966084
  470.4 7.4 %copy-start.2 = (f32[256,1280]{1,0:T(8,128)S(1)}, f32[256,1280]{1,0:T(8,128)}, u32[]{:S(2)}) copy-start(f32[256,1280]{1,0:T(8,128)} %get-tuple-element.59) | copy-start | bytes 3932164
